TPU v7x, 128 devices: a whole 4x4x4 slice. The times are simulated.
128 devices in a mesh: data: 1, seq: 128 (over z, y, x, core).
Axes of the slice: x: 4, y: 4, z: 4, core: 2. Of those that a mesh axis runs over, the one named last changes fastest.
Arguments:
- dec_in: bfloat16 [4096, 384], P(('data', 'seq'))
- memory: bfloat16 [131072, 384], P(('data', 'seq'))
- mem_len: int32 [1], P('data')
- grad_out: float32 [4096, 384], P(('data', 'seq'))
- norm_attn: bfloat16 [384], replicated
- wq_cross: bfloat16 [384, 6, 64], replicated
- wk_cross: bfloat16 [384, 6, 64], replicated
- wv_cross: bfloat16 [384, 6, 64], replicated
- wo_cross: bfloat16 [6, 64, 384], replicated
- norm_mlp: bfloat16 [384], replicated
- w_gate: bfloat16 [384, 1536], replicated
- w_up: bfloat16 [384, 1536], replicated
- w_down: bfloat16 [1536, 384], replicated
Outputs:
- output 1: float32 [4096, 384], P(('data', 'seq'))
- output 2: float32 [131072, 384], P(('data', 'seq'))
- output 3: float32 [384], P('data')
- output 4: float32 [384, 6, 64], P('data')
- output 5: float32 [384, 6, 64], P('data')
- output 6: float32 [384, 6, 64], P('data')
- output 7: float32 [6, 64, 384], P('data')
- output 8: float32 [384], P('data')
- output 9: float32 [384, 1536], P('data')
- output 10: float32 [384, 1536], P('data')
- output 11: float32 [1536, 384], P('data')
All inputs are finite; a program needn't handle non-finite values.
Results may differ from a plain program's by a relative error of at most 0.0157402.
Values are sent between devices in bfloat16 or wider.
A program may use at most 1 GiB of HBM per device.

v0:
```python
import jax
import jax.numpy as jnp
from jax import lax
from jax.sharding import PartitionSpec as P


def rms_norm(tensor, gain):
    mean_sq = jnp.mean(tensor * tensor, axis=-1, keepdims=True)
    return tensor * lax.rsqrt(mean_sq + 1e-6) * gain


def gated_unit(gate_pre, up_pre):
    return jax.nn.silu(gate_pre) * up_pre


def solution(mesh):
    group_size = mesh.shape['seq']
    row_spec = P(('data', 'seq'), None)
    weight_spec = P()
    part_vec = P('data')
    part_mat = P('data', None)
    part_cube = P('data', None, None)

    def device_step(dec_in, memory, mem_len, grad_out, norm_attn, wq_cross, wk_cross, wv_cross, wo_cross, norm_mlp, w_gate, w_up, w_down):
        q_rows, model_dim = dec_in.shape
        m_rows = memory.shape[0]
        heads, head_dim = wq_cross.shape[1], wq_cross.shape[2]
        kv_heads = wk_cross.shape[1]
        head_group = heads // kv_heads
        score_scale = head_dim ** -0.5
        wo_grouped = wo_cross.reshape(kv_heads, head_group, head_dim, model_dim)
        mem_pos = lax.axis_index('seq') * m_rows + jnp.arange(m_rows)
        valid_mask = mem_pos < mem_len[0]

        x_in = dec_in.astype(jnp.float32)
        normed_f, norm_pull = jax.vjp(rms_norm, x_in, norm_attn.astype(jnp.float32))
        normed = normed_f.astype(jnp.bfloat16)
        local_query = jnp.einsum('td,dhe->the', normed, wq_cross, preferred_element_type=jnp.float32).astype(jnp.bfloat16)
        dec_query = lax.all_gather(local_query, 'seq', axis=0, tiled=True).reshape(q_rows * group_size, kv_heads, head_group, head_dim)
        mem_keys = jnp.einsum('td,dke->tke', memory, wk_cross, preferred_element_type=jnp.float32).astype(jnp.bfloat16)
        mem_vals = jnp.einsum('td,dke->tke', memory, wv_cross, preferred_element_type=jnp.float32).astype(jnp.bfloat16)

        def masked_scores():
            raw_scores = jnp.einsum('qkge,tke->kqgt', dec_query, mem_keys, preferred_element_type=jnp.float32)
            return jnp.where(valid_mask, raw_scores * score_scale, -1e30)

        scores = masked_scores()
        local_max = jnp.max(scores, axis=-1)
        exp_scores = jnp.exp(scores - local_max[..., None])
        local_sum = jnp.sum(exp_scores, axis=-1)
        local_out = jnp.einsum('kqgt,tke->kqge', exp_scores.astype(jnp.bfloat16), mem_vals, preferred_element_type=jnp.float32)
        global_max = lax.pmax(local_max, 'seq')
        rescale = jnp.exp(local_max - global_max)
        out_sum = lax.psum_scatter(local_out * rescale[..., None], 'seq', scatter_dimension=1, tiled=True)
        den_sum = lax.psum_scatter(local_sum * rescale, 'seq', scatter_dimension=1, tiled=True)
        attended_f = out_sum / den_sum[..., None]
        attended = attended_f.astype(jnp.bfloat16)
        hidden_f = x_in + jnp.einsum('kqge,kged->qd', attended, wo_grouped, preferred_element_type=jnp.float32)
        hidden = hidden_f.astype(jnp.bfloat16)
        normed_mlp_f, mlp_norm_pull = jax.vjp(rms_norm, hidden.astype(jnp.float32), norm_mlp.astype(jnp.float32))
        normed_mlp = normed_mlp_f.astype(jnp.bfloat16)
        gate_pre = jnp.dot(normed_mlp, w_gate, preferred_element_type=jnp.float32)
        up_pre = jnp.dot(normed_mlp, w_up, preferred_element_type=jnp.float32)
        mlp_f, gated_pull = jax.vjp(gated_unit, gate_pre, up_pre)
        mlp_act = mlp_f.astype(jnp.bfloat16)

        grad_top = grad_out.astype(jnp.bfloat16)
        g_down = jnp.einsum('qf,qd->fd', mlp_act, grad_top, preferred_element_type=jnp.float32)
        grad_act = jnp.einsum('qd,fd->qf', grad_top, w_down, preferred_element_type=jnp.float32)
        grad_gate, grad_up = gated_pull(grad_act)
        grad_gate_b = grad_gate.astype(jnp.bfloat16)
        grad_up_b = grad_up.astype(jnp.bfloat16)
        g_gate = jnp.einsum('qd,qf->df', normed_mlp, grad_gate_b, preferred_element_type=jnp.float32)
        g_up = jnp.einsum('qd,qf->df', normed_mlp, grad_up_b, preferred_element_type=jnp.float32)
        grad_normed_mlp = (jnp.einsum('qf,df->qd', grad_gate_b, w_gate, preferred_element_type=jnp.float32)
                           + jnp.einsum('qf,df->qd', grad_up_b, w_up, preferred_element_type=jnp.float32))
        grad_hidden_norm, g_norm_mlp = mlp_norm_pull(grad_normed_mlp)
        grad_hidden = grad_out + grad_hidden_norm
        grad_hidden_b = grad_hidden.astype(jnp.bfloat16)
        g_wo = jnp.einsum('kqge,qd->kged', attended, grad_hidden_b, preferred_element_type=jnp.float32).reshape(heads, head_dim, model_dim)
        grad_attended = jnp.einsum('qd,kged->kqge', grad_hidden_b, wo_grouped, preferred_element_type=jnp.float32)
        row_delta = jnp.sum(grad_attended * attended_f, axis=-1)
        grad_att_all = lax.all_gather(grad_attended.astype(jnp.bfloat16), 'seq', axis=1, tiled=True)
        stats = lax.all_gather(jnp.stack([den_sum, row_delta]), 'seq', axis=2, tiled=True)
        attn_prob = jnp.exp(masked_scores() - global_max[..., None]) / stats[0][..., None]
        grad_prob = jnp.einsum('kqge,tke->kqgt', grad_att_all, mem_vals, preferred_element_type=jnp.float32)
        grad_scores = (attn_prob * (grad_prob - stats[1][..., None]) * score_scale).astype(jnp.bfloat16)
        grad_vals = jnp.einsum('kqgt,kqge->tke', attn_prob.astype(jnp.bfloat16), grad_att_all, preferred_element_type=jnp.float32)
        grad_keys = jnp.einsum('kqgt,qkge->tke', grad_scores, dec_query, preferred_element_type=jnp.float32)
        grad_query_part = jnp.einsum('kqgt,tke->kqge', grad_scores, mem_keys, preferred_element_type=jnp.float32)
        grad_query = lax.psum_scatter(grad_query_part, 'seq', scatter_dimension=1, tiled=True)
        grad_query_b = jnp.transpose(grad_query, (1, 0, 2, 3)).reshape(q_rows, heads, head_dim).astype(jnp.bfloat16)
        g_wq = jnp.einsum('td,the->dhe', normed, grad_query_b, preferred_element_type=jnp.float32)
        grad_normed = jnp.einsum('the,dhe->td', grad_query_b, wq_cross, preferred_element_type=jnp.float32)
        grad_x_norm, g_norm_attn = norm_pull(grad_normed)
        g_dec = grad_hidden + grad_x_norm
        grad_keys_b = grad_keys.astype(jnp.bfloat16)
        grad_vals_b = grad_vals.astype(jnp.bfloat16)
        g_wk = jnp.einsum('td,tke->dke', memory, grad_keys_b, preferred_element_type=jnp.float32)
        g_wv = jnp.einsum('td,tke->dke', memory, grad_vals_b, preferred_element_type=jnp.float32)
        g_mem = (jnp.einsum('tke,dke->td', grad_keys_b, wk_cross, preferred_element_type=jnp.float32)
                 + jnp.einsum('tke,dke->td', grad_vals_b, wv_cross, preferred_element_type=jnp.float32))
        weight_grads = lax.psum((g_norm_attn, g_wq, g_wk, g_wv, g_wo, g_norm_mlp, g_gate, g_up, g_down), 'seq')
        return (g_dec, g_mem) + tuple(weight_grads)

    return jax.shard_map(device_step, mesh=mesh,
                         in_specs=(row_spec, row_spec, part_vec, row_spec) + (weight_spec,) * 9,
                         out_specs=(row_spec, row_spec, part_vec, part_cube, part_cube, part_cube, part_cube, part_vec, part_mat, part_mat, part_mat),
                         check_vma=False)
```

profile of v0, /device:TPU:1, one launch (start us, length us, event | category | flops | bytes accessed | tf_op | source)
XLA Modules:
  0.0 2014.3 jit_solution(2442564336966375728)
XLA Ops:
  7.2 0.9 fusion.45
  8.2 0.5 copy-done.42
  8.7 0.7 convert_element_type.86
  9.4 0.6 copy-done.36
  9.9 1.9 convolution_convert_fusion.1
  12.6 2.9 fusion.77
  15.5 1.8 fusion.76
  17.3 68.4 %all-gather.3.cloned.1.call-done = bf16[4096,6,64]{2,0,1:T(8,128)(2,1)} async-done(((bf16[32,6,64]{2,0,1:T(8,128)(2,1)}), bf16[4096,6,64]{2,0,1:T(8,128)(2,1)}) %all-gather.3.cloned.1.call-update) | async-done | bytes 3145744 | tf_op jit(solution)/shard_map/all_gather | solution.py:39
  85.7 36.2 %fusion.2 = (f32[6,4096]{1,0:T(8,128)}, f32[6,4096,1024]{1,2,0:T(8,128)}) fusion(pred[1024]{0:T(1024)(128)(4,1)S(1)} %add_compare_fusion, bf16[4096,6,64]{2,0,1:T(8,128)(2,1)} %all-gather.3.cloned.1.call-done, f32[1024,6,64]{0,2,1:T(8,128)S(1)} %bitcast.136), kind=kOutput, calls=%fused_computation.6 | convolution fusion | flops 3297091584 | bytes 105481216 | tf_op jit(solution)/shard_map/qkge,tke->kqgt/dot_general | solution.py:44
  122.0 31.4 %fusion = f32[6,4096]{1,0:T(8,128)S(1)} fusion(f32[6,4096,1024]{1,2,0:T(8,128)} %get-tuple-element.33, f32[6,4096]{1,0:T(8,128)} %get-tuple-element.32, pred[1024]{0:T(1024)(128)(4,1)S(1)} %add_compare_fusion), kind=kLoop, calls=%fused_computation.4 | loop fusion | flops 100638720 | bytes 100860928 | tf_op jit(solution)/shard_map/reduce_sum | solution.py:50
  153.4 113.0 %all-reduce.9.cloned.1.call-done = f32[6,4096,1]{1,0,2:T(8,128)} async-done(((f32[6,4096,1]{1,0,2:T(8,128)}), f32[6,4096,1]{1,0,2:T(8,128)}) %all-reduce.9.cloned.1.call-update) | async-done | bytes 98320 | tf_op jit(solution)/shard_map/pmax | solution.py:52
  266.5 0.9 fusion.40
  267.4 3.7 copy.68
  271.1 0.0 all-reduce.11.cloned.1.call-start
  271.1 38.6 %multiply_bitcast_fusion = f32[6,4096,1,64]{1,3,0,2:T(8,128)} fusion(f32[6,4096]{1,0:T(8,128)S(1)} %get-tuple-element.28, f32[6,4096,1024]{1,2,0:T(8,128)} %get-tuple-element.33, f32[6,4096]{1,0:T(8,128)S(1)} %copy-done.12, pred[1024]{0:T(1024)(128)(4,1)S(1)} %add_compare_fusion, f32[1024,6,64]{0,2,1:T(8,128)S(1)} %bitcast.142), kind=kOutput, calls=%fused_computation.13 | convolution fusion | flops 3323854848 | bytes 108725248 | tf_op jit(solution)/shard_map/kqgt,tke->kqge/dot_general | solution.py:51
  309.7 27.2 %copy.50 = f32[6,4096,1,64]{3,2,0,1:T(1,128)} copy(f32[6,4096,1,64]{1,3,0,2:T(8,128)} %multiply_bitcast_fusion) | data formatting | bytes 12582912 | tf_op jit(solution)/shard_map/mul | solution.py:54
  337.0 0.6 copy-done.41
  337.6 572.2 %reduce-scatter.4.cloned.1.call-done = f32[32,6]{1,0:T(8,128)} async-done(((f32[4096,6]{1,0:T(8,128)}), f32[32,6]{1,0:T(8,128)}) %reduce-scatter.4.cloned.1.call-update) | async-done | bytes 784
  909.8 0.8 copy.69
  910.6 172.2 %all-reduce.11.cloned.1.call-done = f32[6,4096,1,64]{3,2,0,1:T(1,128)} async-done(((f32[6,4096,1,64]{3,2,0,1:T(1,128)}), f32[6,4096,1,64]{3,2,0,1:T(1,128)}) %all-reduce.11.cloned.1.call-update) | async-done | bytes 6291472
  1082.7 1.0 constant_dynamic-slice_fusion.1
  1083.7 1.4 multiply_reduce_fusion.3
  1085.1 0.1 multiply_convert_fusion.4
  1085.2 0.3 fusion.79
  1085.5 0.3 copy-done.20
  1085.8 0.3 fusion.78
  1086.2 1.3 multiply_convert_fusion.2
  1087.5 0.5 fusion.80
  1088.0 1.1 multiply_reduce_fusion.1
  1089.1 0.1 fusion.43
  1089.2 0.9 convert_bitcast_fusion
  1090.2 0.1 copy.52
  1090.3 38.5 %all_gather.10 = f32[2,6,4096,1]{1,0,3,2:T(2,128)S(1)} all-gather(f32[2,6,32,1]{1,0,3,2:T(2,128)S(1)} %copy.52), channel_id=1, replica_groups=mesh['data'=1,'seq'=128] {'seq'}, dimensions={2}, use_global_device_ids=true | all-gather | bytes 198144 | tf_op jit(solution)/shard_map/all_gather | solution.py:84
  1128.9 4.1 fusion.73
  1133.0 2.3 copy.53
  1135.3 0.6 copy.56
  1135.9 1.2 fusion.48
  1137.1 1.9 fusion.83
  1139.0 1.9 fusion.82
  1140.9 1.9 fusion.37
  1142.8 16.7 all-gather.5.cloned.1.call-done
  1159.6 62.1 %multiply_convert_fusion = bf16[6,4096,1024]{1,2,0:T(8,128)(2,1)} fusion(f32[6,4096]{1,0:T(8,128)S(1)} %copy.56, bf16[6,4096,1,64]{3,1,2,0:T(8,128)(2,1)} %all-gather.5.cloned.1.call-done, f32[1024,6,64]{0,2,1:T(8,128)S(1)} %bitcast.143, f32[6,4096]{1,0:T(8,128)S(1)} %copy.53, f32[6,4096]{1,0:T(8,128)S(1)} %bitcast.146, ...), kind=kOutput, calls=%fused_computation | convolution fusion | flops 3422945280 | bytes 156009472 | tf_op jit(solution)/shard_map/kqge,tke->kqgt/dot_general | solution.py:86
  1221.7 22.0 %convolution_bitcast_fusion = f32[6,4096,1,64]{1,3,0,2:T(8,128)} fusion(bf16[6,4096,1024]{1,2,0:T(8,128)(2,1)} %multiply_convert_fusion, f32[1024,6,64]{0,2,1:T(8,128)} %bitcast.137), kind=kOutput, calls=%fused_computation.14 | convolution fusion | flops 3221618688 | bytes 58195968 | tf_op jit(solution)/shard_map/kqgt,tke->kqge/dot_general | solution.py:90
  1243.7 22.4 %fusion.17 = bf16[1024,6,64]{0,2,1:T(8,128)(2,1)S(1)} fusion(bf16[4096,6,64]{2,0,1:T(8,128)(2,1)} %all-gather.3.cloned.1.call-done, bf16[6,4096,1024]{1,2,0:T(8,128)(2,1)} %multiply_convert_fusion), kind=kOutput, calls=%fused_computation.18 | convolution fusion | flops 3221618688 | bytes 54263808 | tf_op jit(solution)/shard_map/kqgt,qkge->tke/dot_general | solution.py:89
  1266.1 1.4 convolution_bitcast_fusion.2
  1267.5 50.1 %fusion.18 = bf16[1024,6,64]{0,2,1:T(8,128)(2,1)S(1)} fusion(bf16[6,4096,1,64]{3,1,2,0:T(8,128)(2,1)} %all-gather.5.cloned.1.call-done, f32[6,4096,1024]{1,2,0:T(8,128)} %get-tuple-element.33, f32[6,4096]{1,0:T(8,128)S(1)} %copy.53, f32[6,4096]{1,0:T(8,128)S(1)} %bitcast.147, pred[1024]{0:T(1024)(128)(4,1)S(1)} %add_compare_fusion), kind=kOutput, calls=%fused_computation.19 | convolution fusion | flops 3347447808 | bytes 104793088 | tf_op jit(solution)/shard_map/kqgt,kqge->tke/dot_general | solution.py:88
  1317.6 1.4 convolution_bitcast_fusion.1
  1319.0 27.2 %copy.59 = f32[6,4096,1,64]{3,2,0,1:T(1,128)} copy(f32[6,4096,1,64]{1,3,0,2:T(8,128)} %convolution_bitcast_fusion) | data formatting | bytes 12582912 | tf_op jit(solution)/shard_map/kqgt,tke->kqge/dot_general | solution.py:90
  1346.2 481.9 %all-reduce.14 = bf16[6,4096,1,64]{3,2,0,1:T(2,128)(2,1)} all-reduce(f32[6,4096,1,64]{3,2,0,1:T(1,128)} %copy.59), channel_id=4, replica_groups=mesh['data'=1,'seq'=128] {'seq'}, use_global_device_ids=true, to_apply=%region_9.10.clone | all-reduce | flops 1572864 | bytes 9437184
  1828.2 1.1 constant_dynamic-slice_fusion
  1829.3 1.1 fusion.56
  1830.5 0.3 fusion.42
  1830.8 65.6 %all-reduce.2 = (f32[384]{0:T(512)}, f32[384]{0:T(512)}) all-reduce(f32[384]{0:T(512)S(1)} %get-tuple-element.13, f32[384]{0:T(512)S(1)} %copy-done.40), channel_id=1, replica_groups=mesh['data'=1,'seq'=128] {'seq'}, use_global_device_ids=true, to_apply=%region_12.13 | all-reduce | flops 768 | bytes 6144 | tf_op jit(solution)/shard_map/psum | solution.py:103
  1896.5 0.7 fusion.44
  1897.2 0.7 fusion.81
  1897.9 1.8 bitcast_add_fusion
  1899.7 95.2 %all-reduce.13.cloned.1.call-done = (f32[384,6,64]{0,2,1:T(8,128)}, f32[384,6,64]{0,2,1:T(8,128)}, f32[384,6,64]{0,2,1:T(8,128)}, f32[6,64,384]{2,1,0:T(8,128)},...) async-done(((f32[384,6,64]{0,2,1:T(8,128)}, f32[384,6,64]{0,2,1:T(8,128)}, f32[384,6,64]{0,2,1:T(8,128)}, f32[6,64,384]{2,1,0:T(8,128)}, ...) | async-done | bytes 9437200 | tf_op jit(solution)/shard_map/psum | solution.py:103
  1995.0 2.1 copy.102
  1997.0 2.1 copy.103
  1999.1 1.9 copy.104
  2001.0 2.0 copy.105
  2003.0 1.4 copy.106
  2004.4 1.4 copy.107
  2005.8 1.4 copy.108
  (104 shorter events, 0.6 us)
Async XLA Ops:
  7.2 1079.0 %copy-start = (bf16[1536,384]{1,0:T(8,128)(2,1)S(1)}, bf16[1536,384]{1,0:T(8,128)(2,1)}, u32[]{:S(2)}) copy-start(bf16[1536,384]{1,0:T(8,128)(2,1)} %param.25) | copy-start | bytes 3538948
  7.2 78.5 %all-gather.3.cloned.1.call-start = ((), (), s32[]{:S(2)}) async-start(), calls=%async_computation.1 | async-start | bytes 6340608 | tf_op jit(solution)/shard_map/all_gather | solution.py:39
  8.2 0.5 copy-start.42
  8.7 0.7 copy-start.38
  9.4 0.6 copy-start.36
  11.9 254.6 %all-reduce.9.cloned.1.call-start = ((), (), s32[]{:S(2)}) async-start(), calls=%async_computation.2 | async-start | bytes 262144 | tf_op jit(solution)/shard_map/pmax | solution.py:52
  17.3 104.6 %copy-start.2 = (f32[1024,384]{0,1}, f32[1024,384]{0,1:S(1)}, u32[]{:S(2)}) copy-start(f32[1024,384]{0,1:S(1)} %fusion.76) | copy-start | bytes 4718596
  122.0 787.8 %reduce-scatter.4.cloned.1.call-start = ((), (), s32[]{:S(2)}) async-start(), calls=%async_computation.4 | async-start | bytes 2113536
  122.0 144.4 %copy-start.12 = (f32[6,4096]{1,0:T(8,128)S(1)}, f32[6,4096]{1,0:T(8,128)}, u32[]{:S(2)}) copy-start(f32[6,4096]{1,0:T(8,128)} %get-tuple-element.32) | copy-start | bytes 294916
  122.0 149.1 %copy-start.13 = (f32[1024,384]{0,1:S(1)}, f32[1024,384]{0,1}, u32[]{:S(2)}) copy-start(f32[1024,384]{0,1} %fusion.77) | copy-start | bytes 4718596
  271.1 811.6 %all-reduce.11.cloned.1.call-start = ((), (), s32[]{:S(2)}) async-start(), calls=%async_computation.5 | async-start | bytes 25165824
  336.9 0.7 copy-start.41
  336.9 748.3 %copy-start.8 = (bf16[384,1536]{1,0:T(8,128)(2,1)S(1)}, bf16[384,1536]{1,0:T(8,128)(2,1)}, u32[]{:S(2)}) copy-start(bf16[384,1536]{1,0:T(8,128)(2,1)} %param.23) | copy-start | bytes 3538948
  336.9 748.9 %copy-start.7 = (bf16[384,1536]{1,0:T(8,128)(2,1)S(1)}, bf16[384,1536]{1,0:T(8,128)(2,1)}, u32[]{:S(2)}) copy-start(bf16[384,1536]{1,0:T(8,128)(2,1)} %param.24) | copy-start | bytes 3538948
  337.0 822.6 %all-gather.5.cloned.1.call-start = ((), (), s32[]{:S(2)}) async-start(), calls=%async_computation.3 | async-start | bytes 6340608 | tf_op jit(solution)/shard_map/all_gather | solution.py:83
  1082.7 6.4 copy-start.33
  1082.7 6.5 copy-start.44
  1083.7 6.5 copy-start.29
  1085.2 0.6 copy-start.20
  1085.8 3.3 copy-start.16
  1086.1 3.0 copy-start.18
  1087.5 1.7 copy-start.25
  1087.5 2.7 copy-start.27
  1089.2 46.7 %copy-start.23 = (f32[32,384]{1,0:T(8,128)}, f32[32,384]{1,0:T(8,128)S(1)}, u32[]{:S(2)}) copy-start(f32[32,384]{1,0:T(8,128)S(1)} %fusion.43) | copy-start | bytes 147460
  1090.2 904.8 %all-reduce.13.cloned.1.call-start = ((), (), s32[]{:S(2)}) async-start(), calls=%async_computation.6 | async-start | bytes 18874368 | tf_op jit(solution)/shard_map/psum | solution.py:103
  1128.8 7.1 copy-start.30
  1128.9 8.2 copy-start.21
  1128.9 8.2 copy-start.26
  1128.9 10.1 copy-start.28
  1133.0 7.9 copy-start.17
  1133.0 7.9 copy-start.19
  1133.0 7.9 copy-start.34
  1133.0 26.6 %copy-start.35 = (f32[6,4096,1]{1,0,2:T(8,128)S(1)}, f32[6,4096,1]{1,0,2:T(8,128)}, u32[]{:S(2)}) copy-start(f32[6,4096,1]{1,0,2:T(8,128)} %all-reduce.9.cloned.1.call-done) | copy-start | bytes 294916
  1135.9 23.7 %copy-start.14 = (f32[1024,384]{0,1:S(1)}, f32[1024,384]{0,1}, u32[]{:S(2)}) copy-start(f32[1024,384]{0,1} %fusion.77) | copy-start | bytes 4718596
  1243.7 22.4 %copy-start.5 = (bf16[1024,384]{1,0:T(8,128)(2,1)S(1)}, bf16[1024,384]{1,0:T(8,128)(2,1)}, u32[]{:S(2)}) copy-start(bf16[1024,384]{1,0:T(8,128)(2,1)} %param.14) | copy-start | bytes 2359300
  1266.1 51.5 %copy-start.3 = (bf16[1024,6,64]{0,2,1:T(8,128)(2,1)}, bf16[1024,6,64]{0,2,1:T(8,128)(2,1)S(1)}, u32[]{:S(2)}) copy-start(bf16[1024,6,64]{0,2,1:T(8,128)(2,1)S(1)} %fusion.17) | copy-start | bytes 2359300
  1267.5 50.1 %copy-start.6 = (bf16[1024,384]{1,0:T(8,128)(2,1)S(1)}, bf16[1024,384]{1,0:T(8,128)(2,1)}, u32[]{:S(2)}) copy-start(bf16[1024,384]{1,0:T(8,128)(2,1)} %param.14) | copy-start | bytes 2359300
  1346.2 483.0 %copy-start.22 = (bf16[32,384]{1,0:T(8,128)(2,1)S(1)}, bf16[32,384]{1,0:T(8,128)(2,1)}, u32[]{:S(2)}) copy-start(bf16[32,384]{1,0:T(8,128)(2,1)} %param.13) | copy-start | bytes 73732
  1346.2 483.0 %copy-start.37 = (f32[384]{0:T(512)S(1)}, f32[384]{0:T(512)}, u32[]{:S(2)}) copy-start(f32[384]{0:T(512)} %copy-done.36) | copy-start | bytes 4612
  1346.2 483.0 %copy-start.39 = (f32[32]{0:T(128)S(1)}, f32[32]{0:T(128)}, u32[]{:S(2)}) copy-start(f32[32]{0:T(128)} %copy-done.38) | copy-start | bytes 388
  1828.1 2.3 copy-start.15
  1828.1 2.7 copy-start.40
  1828.1 68.3 %copy-start.43 = (f32[32]{0:T(128)S(1)}, f32[32]{0:T(128)}, u32[]{:S(2)}) copy-start(f32[32]{0:T(128)} %copy-done.42) | copy-start | bytes 388
  1828.1 68.3 %copy-start.24 = (f32[32,384]{1,0:T(8,128)S(1)}, f32[32,384]{1,0:T(8,128)}, u32[]{:S(2)}) copy-start(f32[32,384]{1,0:T(8,128)} %copy-done.23) | copy-start | bytes 147460
  1828.1 69.0 %copy-start.4 = (bf16[1024,6,64]{0,2,1:T(8,128)(2,1)S(1)}, bf16[1024,6,64]{0,2,1:T(8,128)(2,1)}, u32[]{:S(2)}) copy-start(bf16[1024,6,64]{0,2,1:T(8,128)(2,1)} %copy-done.3) | copy-start | bytes 2359300
  1828.2 69.0 %copy-start.31 = (bf16[384,6,64]{0,2,1:T(8,128)(2,1)S(1)}, bf16[384,6,64]{0,2,1:T(8,128)(2,1)}, u32[]{:S(2)}) copy-start(bf16[384,6,64]{0,2,1:T(8,128)(2,1)} %param.19) | copy-start | bytes 884740
  1830.4 67.4 %copy-start.32 = (bf16[384,6,64]{0,2,1:T(8,128)(2,1)S(1)}, bf16[384,6,64]{0,2,1:T(8,128)(2,1)}, u32[]{:S(2)}) copy-start(bf16[384,6,64]{0,2,1:T(8,128)(2,1)} %param.20) | copy-start | bytes 884740
  1995.0 8.1 copy-start.11
  1995.0 9.5 copy-start.10
  1997.0 8.8 copy-start.9
  2001.0 6.2 copy-start.1
Sparse Core Ops, SparseCore 0:
  12.0 73.6 all-gather.2
  122.1 144.3 all-reduce.8
  271.2 638.5 reduce-scatter.3
  914.5 168.1 all-reduce.10
  1090.3 69.2 all-gather.4
  1830.6 164.3 all-reduce.12
where the time goes:
time: 2020 us; the launch traced here: 2010 us
  waiting for transfers between devices  1040 us (51%)
  blocking collectives  586 us (29%)
  matrix products  258 us (13%)
  local copies, waits for them, and re-layouts  82.5 us (4%)
  other arithmetic  34.8 us (2%)
    unnamed x8, waiting for transfers between devices  744 us
    unnamed x1, blocking collectives  482 us
    pmax x1, waiting for transfers between devices, device_step(): global_max = lax.pmax(local_max, 'seq')  113 us
    psum x1, waiting for transfers between devices, device_step(): lax.psum((g_norm_attn, g_wq, g_wk, g_wv, g_wo, g_norm_mlp, g_gate, g_up,...  95.2 us
    all_gather x1, waiting for transfers between devices, device_step(): lax.all_gather(local_query, 'seq', axis=0, tiled=True)  68.4 us
    psum x1, blocking collectives, device_step(): lax.psum((g_norm_attn, g_wq, g_wk, g_wv, g_wo, g_norm_mlp, g_gate, g_up,...  65.6 us
    dot_general x1, matrix products, device_step(): jnp.einsum('kqge,tke->kqgt', grad_att_all, mem_vals, preferred_element_ty...  62.1 us
    dot_general x1, matrix products, device_step(): jnp.einsum('kqgt,kqge->tke', attn_prob.astype(jnp.bfloat16), grad_att_all...  50.1 us
  transfers between devices with their start and end apart: 6, of which 6 were waited for; matrix products, arithmetic and copies ran while one was open for 6% of the time, Pallas kernels for 0%

commit v1 on v0

v1 whole, which is shorter than its diff:
```python
import functools

import jax
import jax.numpy as jnp
from jax import lax
from jax.experimental import pallas as pl
from jax.experimental.pallas import tpu as pltpu
from jax.sharding import PartitionSpec as P

F32 = jnp.float32
BF16 = jnp.bfloat16
MESH = pl.DeviceIdType.MESH
VMEM_LIMIT = 62 * 1024 * 1024
NEG = -1e30
ORDERS = ((0, 1, 2), (2, 0, 1), (1, 2, 0))
PARTS = 3
TILE = 128


def rms_norm(tensor, gain):
    mean_sq = jnp.mean(tensor * tensor, axis=-1, keepdims=True)
    return tensor * lax.rsqrt(mean_sq + 1e-6) * gain


def gated_unit(gate_pre, up_pre):
    return jax.nn.silu(gate_pre) * up_pre


class Place:
    def __init__(self, n):
        self.n = n
        me = lax.axis_index("seq")
        self.me = me
        self.core = lax.rem(me, 2)
        x = lax.rem(me // 2, n)
        y = lax.rem(me // (2 * n), n)
        z = me // (2 * n * n)
        self.coord = (z, y, x)
        self.stride = (2 * n * n, 2 * n, 2)

    def along(self, axis, k):
        here = self.coord[axis]
        return self.me + (lax.rem(here + k, self.n) - here) * self.stride[axis]

    def other_core(self):
        return self.me + 1 - 2 * self.core

    def to(self, k):
        return {"seq": k}

    def barrier(self):
        sem = pltpu.get_barrier_semaphore()
        for axis in range(3):
            for k in range(1, self.n):
                pl.semaphore_signal(sem, inc=1, device_id=self.to(self.along(axis, k)), device_id_type=MESH)
        pl.semaphore_signal(sem, inc=1, device_id=self.to(self.other_core()), device_id_type=MESH)
        pl.semaphore_wait(sem, 3 * (self.n - 1) + 1)


def rcopy(src, dst, send, recv, device):
    return pltpu.make_async_remote_copy(src_ref=src, dst_ref=dst, send_sem=send, recv_sem=recv,
                                        device_id={"seq": device}, device_id_type=MESH)


def lanes(start, size):
    return pl.ds(pl.multiple_of(start, TILE), size)


def gather_kernel(n, has_stats, *refs):
    if has_stats:
        x_ref, s_ref, out_ref, sout_ref, rows, srows, send, recv, ssend, srecv, csend, crecv = refs
    else:
        x_ref, out_ref, rows, send, recv, csend, crecv = refs
    at = Place(n)
    r = TILE // n
    at.barrier()
    pairs = [(0, x_ref, rows, out_ref)]
    if has_stats:
        pairs.append((1, s_ref, srows, sout_ref))

    def sems(kind):
        return (send, recv) if kind == 0 else (ssend, srecv)

    copies = {}
    for p in range(PARTS):
        a3 = ORDERS[p][2]
        mine = pl.ds(pl.multiple_of(at.coord[a3] * r, r), r)
        for kind, src, dst, _ in pairs:
            snd, rcv = sems(kind)
            for k in range(1, n):
                c = rcopy(src.at[p], dst.at[p, mine, :], snd.at[0, p, k - 1], rcv.at[0, p, k - 1], at.along(a3, k))
                c.start()
                copies[0, p, kind, k] = c
            dst[p, mine, :] = src[p]
    for p in range(PARTS):
        a1, a2, _ = ORDERS[p]
        base = ((at.core * n + at.coord[a1]) * n + at.coord[a2]) * TILE
        for kind, _, dst, full in pairs:
            for k in range(1, n):
                copies[0, p, kind, k].wait()
            block = dst[p].astype(F32).T
            full[p, :, lanes(base, TILE)] = block[:full.shape[1]].astype(full.dtype)
    for stage in (1, 2):
        for p in range(PARTS):
            a1, a2, _ = ORDERS[p]
            if stage == 1:
                axis, width = a2, TILE
                base = ((at.core * n + at.coord[a1]) * n + at.coord[a2]) * TILE
            else:
                axis, width = a1, TILE * n
                base = (at.core * n + at.coord[a1]) * n * TILE
                for kind, *_ in pairs:
                    for k in range(1, n):
                        copies[1, p, kind, k].wait()
            for kind, _, _, full in pairs:
                snd, rcv = sems(kind)
                view = full.at[p, :, lanes(base, width)]
                for k in range(1, n):
                    c = rcopy(view, view, snd.at[stage, p, k - 1], rcv.at[stage, p, k - 1], at.along(axis, k))
                    c.start()
                    copies[stage, p, kind, k] = c
    final = []
    for p in range(PARTS):
        for kind, _, _, full in pairs:
            for k in range(1, n):
                copies[2, p, kind, k].wait()
            width = n * n * TILE
            view = full.at[p, :, lanes(at.core * width, width)]
            c = rcopy(view, view, csend.at[kind, p], crecv.at[kind, p], at.other_core())
            c.start()
            final.append(c)
    for c in final:
        c.wait()


def all_gather_t(n, cid, rows, stats=None):
    total = 2 * n * n * TILE
    r = TILE // n
    has = stats is not None
    vm = pl.BlockSpec(memory_space=pltpu.VMEM)
    outs = [jax.ShapeDtypeStruct((PARTS, TILE, total), BF16)]
    scratch = [pltpu.VMEM((PARTS, TILE, TILE), BF16)]
    args = [rows]
    sem = pltpu.SemaphoreType.DMA
    if has:
        outs.append(jax.ShapeDtypeStruct((PARTS, 8, total), F32))
        scratch.append(pltpu.VMEM((PARTS, TILE, TILE), F32))
        args.append(stats)
    scratch += [sem((3, PARTS, n - 1)), sem((3, PARTS, n - 1))]
    if has:
        scratch += [sem((3, PARTS, n - 1)), sem((3, PARTS, n - 1))]
    scratch += [sem((2, PARTS)), sem((2, PARTS))]
    res = pl.pallas_call(
        functools.partial(gather_kernel, n, has),
        out_shape=tuple(outs), in_specs=[vm] * len(args), out_specs=(vm,) * len(outs),
        scratch_shapes=scratch, name="gather_stats" if has else "gather_q",
        compiler_params=pltpu.CompilerParams(collective_id=cid, has_side_effects=True, vmem_limit_bytes=VMEM_LIMIT),
    )(*args)
    return res if has else res[0]


def merge(blocks, rows_axis):
    take = (lambda b, i, j: b[i:j]) if rows_axis == 0 else (lambda b, i, j: b[:, i:j])
    half = TILE // 2
    outs, maxes, sums = [], [], []
    for h in range(2):
        ms = [take(b, TILE + h, TILE + h + 1) for b in blocks]
        m = functools.reduce(jnp.maximum, ms)
        ws = [jnp.exp(v - m) for v in ms]
        o = sum(take(b, half * h, half * h + half) * w for b, w in zip(blocks, ws))
        l = sum(take(b, TILE + 2 + h, TILE + 3 + h) * w for b, w in zip(blocks, ws))
        outs.append(o)
        maxes.append(m)
        sums.append(l)
    return outs, maxes + sums


def scatter_kernel(n, with_stats, x_ref, *refs):
    if with_stats:
        o_ref, st_ref, buf0, acc0, buf1, acc1, buf2, acc2, buf3, csend, crecv, send, recv = refs
    else:
        o_ref, buf0, acc0, buf1, acc1, buf2, acc2, buf3, csend, crecv, send, recv = refs
    at = Place(n)
    r = TILE // n
    at.barrier()
    half = n * n * TILE

    def combine(dst, p, col, blocks):
        vals = blocks
        if with_stats:
            outs, stats = merge(vals, 0)
            dst[p, 0:TILE // 2, col] = outs[0]
            dst[p, TILE // 2:TILE, col] = outs[1]
            dst[p, TILE:TILE + 8, col] = jnp.concatenate(stats + [jnp.zeros_like(stats[0])] * 4, axis=0)
        else:
            dst[p, :, col] = functools.reduce(jnp.add, vals)

    first = []
    for p in range(PARTS):
        c = rcopy(x_ref.at[p, :, lanes((1 - at.core) * half, half)], buf0.at[p], csend.at[p], crecv.at[p], at.other_core())
        c.start()
        first.append(c)
    copies = {}
    for p in range(PARTS):
        a1 = ORDERS[p][0]
        first[p].wait()
        step = n * TILE
        for j in range(n):
            combine(acc0, p, pl.ds(j * step, step),
                    [x_ref[p, :, lanes(at.core * half + j * step, step)], buf0[p, :, j * step:(j + 1) * step]])
        for k in range(1, n):
            there = lax.rem(at.coord[a1] + k, n)
            c = rcopy(acc0.at[p, :, lanes(there * step, step)], buf1.at[p, k - 1],
                      send.at[0, p, k - 1], recv.at[0, p, k - 1], at.along(a1, k))
            c.start()
            copies[0, p, k] = c
    for p in range(PARTS):
        a1, a2, _ = ORDERS[p]
        for k in range(1, n):
            copies[0, p, k].wait()
        mine = at.coord[a1] * n * TILE
        for j in range(n):
            col = slice(j * TILE, (j + 1) * TILE)
            combine(acc1, p, pl.ds(j * TILE, TILE),
                    [acc0[p, :, lanes(mine + j * TILE, TILE)]] + [buf1[p, k, :, col] for k in range(n - 1)])
        for k in range(1, n):
            there = lax.rem(at.coord[a2] + k, n)
            c = rcopy(acc1.at[p, :, lanes(there * TILE, TILE)], buf2.at[p, k - 1],
                      send.at[1, p, k - 1], recv.at[1, p, k - 1], at.along(a2, k))
            c.start()
            copies[1, p, k] = c
    for p in range(PARTS):
        _, a2, a3 = ORDERS[p]
        for k in range(1, n):
            copies[1, p, k].wait()
        blocks = [acc1[p, :, lanes(at.coord[a2] * TILE, TILE)]] + [buf2[p, k] for k in range(n - 1)]
        if with_stats:
            outs, stats = merge(blocks, 0)
            acc2[p, :, 0:TILE] = jnp.concatenate(outs, axis=0).T
            tail = jnp.concatenate(stats + [jnp.zeros((TILE - 4, TILE), F32)], axis=0)
            acc2[p, :, TILE:2 * TILE] = tail.T
        else:
            acc2[p] = functools.reduce(jnp.add, blocks).T
        for k in range(1, n):
            there = lax.rem(at.coord[a3] + k, n)
            c = rcopy(acc2.at[p, pl.ds(pl.multiple_of(there * r, r), r), :], buf3.at[p, k - 1],
                      send.at[2, p, k - 1], recv.at[2, p, k - 1], at.along(a3, k))
            c.start()
            copies[2, p, k] = c
    for p in range(PARTS):
        a3 = ORDERS[p][2]
        for k in range(1, n):
            copies[2, p, k].wait()
        blocks = [acc2[p, pl.ds(pl.multiple_of(at.coord[a3] * r, r), r), :]] + [buf3[p, k] for k in range(n - 1)]
        if with_stats:
            outs, (m0, m1, l0, l1) = merge(blocks, 1)
            o_ref[p] = jnp.concatenate([outs[0] / l0, outs[1] / l1], axis=1)
            col = lax.broadcasted_iota(jnp.int32, (r, TILE), 1)
            st_ref[p] = jnp.where(col == 0, m0 + jnp.log(l0), jnp.where(col == 1, m1 + jnp.log(l1), 0.0))
        else:
            o_ref[p] = functools.reduce(jnp.add, blocks)


def reduce_scatter_t(n, cid, x, with_stats):
    rows = x.shape[1]
    r = TILE // n
    wide = 2 * TILE if with_stats else TILE
    vm = pl.BlockSpec(memory_space=pltpu.VMEM)
    sem = pltpu.SemaphoreType.DMA
    half = n * n * TILE
    outs = [jax.ShapeDtypeStruct((PARTS, r, TILE), F32)] * (2 if with_stats else 1)
    scratch = [
        pltpu.VMEM((PARTS, rows, half), F32), pltpu.VMEM((PARTS, rows, half), F32),
        pltpu.VMEM((PARTS, n - 1, rows, n * TILE), F32), pltpu.VMEM((PARTS, rows, n * TILE), F32),
        pltpu.VMEM((PARTS, n - 1, rows, TILE), F32), pltpu.VMEM((PARTS, TILE, wide), F32),
        pltpu.VMEM((PARTS, n - 1, r, wide), F32),
        sem((PARTS,)), sem((PARTS,)), sem((3, PARTS, n - 1)), sem((3, PARTS, n - 1)),
    ]
    res = pl.pallas_call(
        functools.partial(scatter_kernel, n, with_stats),
        out_shape=tuple(outs), in_specs=[vm], out_specs=(vm,) * len(outs), scratch_shapes=scratch,
        name="scatter_out" if with_stats else "scatter_dq",
        compiler_params=pltpu.CompilerParams(collective_id=cid, has_side_effects=True, vmem_limit_bytes=VMEM_LIMIT),
    )(x)
    return res if with_stats else res[0]


QB = 256


def aux_rows(rows, width):
    pad = jnp.zeros((64 - len(rows), width), F32)
    return jnp.concatenate(list(rows) + [pad], axis=0).astype(BF16)


def split3(v):
    hi = v.astype(BF16).astype(F32)
    mid = (v - hi).astype(BF16).astype(F32)
    lo = (v - hi - mid).astype(BF16).astype(F32)
    return [hi, mid, lo]


def fwd_kernel(q_ref, k_ref, vt_ref, o_ref):
    total = q_ref.shape[2]
    half = TILE // 2
    one = jnp.ones((1, QB), F32)
    aux = aux_rows([one], QB)

    def body(b, _):
        col = pl.ds(pl.multiple_of(b * QB, QB), QB)
        for p in range(PARTS):
            maxes, sums = [], []
            for j in range(2):
                qa = jnp.concatenate([q_ref[p, half * j:half * (j + 1), col], aux], axis=0)
                s = jnp.dot(k_ref[2 * p + j], qa, preferred_element_type=F32)
                m = jnp.max(s, axis=0, keepdims=True)
                e = jnp.exp(s - m)
                l = jnp.sum(e, axis=0, keepdims=True)
                o_ref[p, half * j:half * (j + 1), col] = jnp.dot(
                    vt_ref[p, half * j:half * (j + 1), :], e.astype(BF16), preferred_element_type=F32)
                maxes.append(m)
                sums.append(l)
            o_ref[p, TILE:TILE + 8, col] = jnp.concatenate(maxes + sums + [jnp.zeros((4, QB), F32)], axis=0)
        return 0

    lax.fori_loop(0, total // QB, body, 0)


def attention_fwd(q_t, k_aug, v_t):
    total, keys = q_t.shape[2], k_aug.shape[1]
    vm = pl.BlockSpec(memory_space=pltpu.VMEM)
    return pl.pallas_call(
        fwd_kernel, out_shape=jax.ShapeDtypeStruct((PARTS, TILE + 8, total), F32),
        in_specs=[vm] * 3, out_specs=vm, name="attention_fwd",
        cost_estimate=pl.CostEstimate(flops=4 * 384 * total * keys, bytes_accessed=12_000_000, transcendentals=6 * total * keys),
        compiler_params=pltpu.CompilerParams(vmem_limit_bytes=VMEM_LIMIT),
    )(q_t, k_aug, v_t)


def bwd_kernel(q_ref, do_ref, st_ref, k_ref, v_ref, kt_ref, dq_ref, dk_ref, dv_ref):
    total = q_ref.shape[2]
    half = TILE // 2
    one = jnp.ones((1, QB), F32)
    zero = jnp.zeros((1, QB), F32)
    blank = jnp.zeros((half, QB), BF16)
    nt = (((1,), (1,)), ((), ()))
    dk_ref[...] = jnp.zeros_like(dk_ref)
    dv_ref[...] = jnp.zeros_like(dv_ref)

    def body(b, _):
        col = pl.ds(pl.multiple_of(b * QB, QB), QB)
        for p in range(PARTS):
            probs, dscores, dos, qs = [], [], [], []
            for j in range(2):
                qh = q_ref[p, half * j:half * (j + 1), col]
                doh = do_ref[p, half * j:half * (j + 1), col]
                lse = st_ref[p, j:j + 1, col]
                delta = st_ref[p, 2 + j:3 + j, col]
                qa = jnp.concatenate([qh, aux_rows([one] + split3(-lse), QB)], axis=0)
                da = jnp.concatenate([doh, aux_rows([zero] + split3(-delta), QB)], axis=0)
                e = jnp.exp(jnp.dot(k_ref[2 * p + j], qa, preferred_element_type=F32))
                dp = jnp.dot(v_ref[2 * p + j], da, preferred_element_type=F32)
                ds = (e * dp).astype(BF16)
                probs.append(e.astype(BF16))
                dscores.append(ds)
                order = (lambda a: [a, blank]) if j == 0 else (lambda a: [blank, a])
                dos.append(jnp.concatenate(order(doh), axis=0))
                qs.append(jnp.concatenate(order(qh), axis=0))
                dq_ref[p, half * j:half * (j + 1), col] = 0.125 * jnp.dot(
                    kt_ref[p, half * j:half * (j + 1), :], ds, preferred_element_type=F32)
            dv_ref[p] += (lax.dot_general(probs[0], dos[0], nt, preferred_element_type=F32)
                          + lax.dot_general(probs[1], dos[1], nt, preferred_element_type=F32))
            dk_ref[p] += (lax.dot_general(dscores[0], qs[0], nt, preferred_element_type=F32)
                          + lax.dot_general(dscores[1], qs[1], nt, preferred_element_type=F32))
        return 0

    lax.fori_loop(0, total // QB, body, 0)


def attention_bwd(q_t, do_t, stats, k_aug, v_aug, k_t):
    total, keys = q_t.shape[2], k_aug.shape[1]
    vm = pl.BlockSpec(memory_space=pltpu.VMEM)
    acc = jax.ShapeDtypeStruct((PARTS, keys, TILE), F32)
    return pl.pallas_call(
        bwd_kernel, out_shape=(jax.ShapeDtypeStruct((PARTS, TILE, total), F32), acc, acc),
        in_specs=[vm] * 6, out_specs=(vm,) * 3, name="attention_bwd",
        cost_estimate=pl.CostEstimate(flops=10 * 384 * total * keys, bytes_accessed=20_000_000, transcendentals=6 * total * keys),
        compiler_params=pltpu.CompilerParams(vmem_limit_bytes=VMEM_LIMIT),
    )(q_t, do_t, stats, k_aug, v_aug, k_t)


def solution(mesh):
    group = mesh.shape['seq']
    n = round((group // 2) ** (1 / 3))
    row_spec = P(('data', 'seq'), None)
    weight_spec = P()
    part_vec = P('data')
    part_mat = P('data', None)
    part_cube = P('data', None, None)

    def by_part(a):
        return jnp.transpose(a.reshape(a.shape[0], PARTS, TILE), (1, 0, 2))

    def by_row(a):
        return jnp.transpose(a, (1, 0, 2)).reshape(a.shape[1], PARTS * TILE)

    def device_step(dec_in, memory, mem_len, grad_out, norm_attn, wq_cross, wk_cross, wv_cross, wo_cross, norm_mlp, w_gate, w_up, w_down):
        q_rows, model_dim = dec_in.shape
        m_rows = memory.shape[0]
        heads, head_dim = wq_cross.shape[1], wq_cross.shape[2]
        wide = heads * head_dim
        wq, wk, wv = (w.reshape(model_dim, wide) for w in (wq_cross, wk_cross, wv_cross))
        wo = wo_cross.reshape(wide, model_dim)
        mem_pos = lax.axis_index('seq') * m_rows + jnp.arange(m_rows)
        bias = jnp.where(mem_pos < mem_len[0], 0.0, NEG).astype(BF16)

        x_in = dec_in.astype(F32)
        normed_f, norm_pull = jax.vjp(rms_norm, x_in, norm_attn.astype(F32))
        normed = normed_f.astype(BF16)
        local_query = jnp.dot(normed, wq, preferred_element_type=F32).astype(BF16) * jnp.asarray(head_dim ** -0.5, BF16)
        q_t = all_gather_t(n, 0, by_part(local_query))

        mem_keys = jnp.dot(memory, wk, preferred_element_type=F32).astype(BF16)
        mem_vals = jnp.dot(memory, wv, preferred_element_type=F32).astype(BF16)
        k_t = mem_keys.T.reshape(PARTS, TILE, m_rows)
        v_t = mem_vals.T.reshape(PARTS, TILE, m_rows)
        ones = jnp.ones((m_rows, 3), BF16)
        aux_k = jnp.concatenate([bias[:, None], ones, jnp.zeros((m_rows, 60), BF16)], axis=1)
        aux_v = jnp.concatenate([jnp.zeros((m_rows, 1), BF16), ones, jnp.zeros((m_rows, 60), BF16)], axis=1)

        def augment(a, aux):
            return jnp.stack([jnp.concatenate([a[:, head_dim * h:head_dim * (h + 1)], aux], axis=1) for h in range(heads)])

        k_aug = augment(mem_keys, aux_k)
        v_aug = augment(mem_vals, aux_v)

        partial = attention_fwd(q_t, k_aug, v_t)
        out_parts, lse = reduce_scatter_t(n, 1, partial, True)
        attended_f = by_row(out_parts)

        attended = attended_f.astype(BF16)
        hidden_f = x_in + jnp.dot(attended, wo, preferred_element_type=F32)
        hidden = hidden_f.astype(BF16)
        normed_mlp_f, mlp_norm_pull = jax.vjp(rms_norm, hidden.astype(F32), norm_mlp.astype(F32))
        normed_mlp = normed_mlp_f.astype(BF16)
        gate_pre = jnp.dot(normed_mlp, w_gate, preferred_element_type=F32)
        up_pre = jnp.dot(normed_mlp, w_up, preferred_element_type=F32)
        mlp_f, gated_pull = jax.vjp(gated_unit, gate_pre, up_pre)
        mlp_act = mlp_f.astype(BF16)

        grad_top = grad_out.astype(BF16)
        g_down = jnp.einsum('qf,qd->fd', mlp_act, grad_top, preferred_element_type=F32)
        grad_act = jnp.einsum('qd,fd->qf', grad_top, w_down, preferred_element_type=F32)
        grad_gate, grad_up = gated_pull(grad_act)
        grad_gate_b = grad_gate.astype(BF16)
        grad_up_b = grad_up.astype(BF16)
        g_gate = jnp.einsum('qd,qf->df', normed_mlp, grad_gate_b, preferred_element_type=F32)
        g_up = jnp.einsum('qd,qf->df', normed_mlp, grad_up_b, preferred_element_type=F32)
        grad_normed_mlp = (jnp.einsum('qf,df->qd', grad_gate_b, w_gate, preferred_element_type=F32)
                           + jnp.einsum('qf,df->qd', grad_up_b, w_up, preferred_element_type=F32))
        grad_hidden_norm, g_norm_mlp = mlp_norm_pull(grad_normed_mlp)
        grad_hidden = grad_out + grad_hidden_norm
        grad_hidden_b = grad_hidden.astype(BF16)
        g_wo = jnp.einsum('qe,qd->ed', attended, grad_hidden_b, preferred_element_type=F32).reshape(heads, head_dim, model_dim)
        grad_attended = jnp.einsum('qd,ed->qe', grad_hidden_b, wo, preferred_element_type=F32)
        delta = jnp.sum((grad_attended * attended_f).reshape(q_rows, PARTS, 2, head_dim), axis=-1)
        delta = jnp.transpose(delta, (1, 0, 2))
        stats_in = jnp.concatenate([lse[:, :, 0:2], delta, jnp.zeros((PARTS, q_rows, TILE - 4), F32)], axis=2)
        do_t, stats = all_gather_t(n, 2, by_part(grad_attended.astype(BF16)), stats_in)

        early = lax.psum((g_wo, g_norm_mlp, g_gate, g_up, g_down), 'seq')

        dq_part, dk, dv = attention_bwd(q_t, do_t, stats, k_aug, v_aug, k_t)
        grad_query_b = by_row(reduce_scatter_t(n, 3, dq_part, False)).astype(BF16)

        g_wq = jnp.einsum('td,te->de', normed, grad_query_b, preferred_element_type=F32)
        grad_normed = jnp.einsum('te,de->td', grad_query_b, wq, preferred_element_type=F32)
        grad_x_norm, g_norm_attn = norm_pull(grad_normed)
        g_dec = grad_hidden + grad_x_norm
        dk_b = by_row(dk.astype(BF16))
        dv_b = by_row(dv.astype(BF16))
        g_wk = jnp.einsum('td,te->de', memory, dk_b, preferred_element_type=F32)
        g_wv = jnp.einsum('td,te->de', memory, dv_b, preferred_element_type=F32)
        g_mem = (jnp.einsum('te,de->td', dk_b, wk, preferred_element_type=F32)
                 + jnp.einsum('te,de->td', dv_b, wv, preferred_element_type=F32))
        late = lax.psum((g_norm_attn, g_wq, g_wk, g_wv), 'seq')
        cube = (model_dim, heads, head_dim)
        g_wo, g_norm_mlp, g_gate, g_up, g_down = early
        g_norm_attn, g_wq, g_wk, g_wv = late
        return (g_dec, g_mem, g_norm_attn, g_wq.reshape(cube), g_wk.reshape(cube), g_wv.reshape(cube),
                g_wo, g_norm_mlp, g_gate, g_up, g_down)

    return jax.shard_map(device_step, mesh=mesh,
                         in_specs=(row_spec, row_spec, part_vec, row_spec) + (weight_spec,) * 9,
                         out_specs=(row_spec, row_spec, part_vec, part_cube, part_cube, part_cube, part_cube, part_vec, part_mat, part_mat, part_mat),
                         check_vma=False)
```

time: 2020 us -> 502 us (0.25)
  waiting for transfers between devices: 1040 us -> 96 us
  blocking collectives: 586 us -> 64.7 us
  Pallas kernels: 0 us -> 269 us
  matrix products: 258 us -> 23.1 us
  local copies, waits for them, and re-layouts: 82.5 us -> 23.9 us
  other arithmetic: 34.8 us -> 9.47 us
    unnamed x8 -> x1, waiting for transfers between devices: 744 us -> 0.02 us
    unnamed x1 -> x0, blocking collectives: 482 us -> none
    pallas_call x0 -> x6, Pallas kernels: none -> 269 us  [the longest x1 76.5 us: attention_bwd(): pl.pallas_call(bwd_kernel, out_shape=(jax.ShapeDtypeStruct((PARTS, TILE,...]
    dot_general x24 -> x20, matrix products: 253 us -> 23.1 us  [the longest x1 1.94 us: device_step(): jnp.einsum('qd,qf->df', normed_mlp, grad_gate_b, preferred_element_type=F32)]
    pmax x1 -> x0, waiting for transfers between devices: 113 us -> none  [device_step(): global_max = lax.pmax(local_max, 'seq')]
    all_gather x2 -> x0, waiting for transfers between devices: 85.1 us -> none  [the longest x1 68.4 us: device_step(): lax.all_gather(local_query, 'seq', axis=0, tiled=True)]
    all_gather x1 -> x0, blocking collectives: 38.5 us -> none  [device_step(): lax.all_gather(jnp.stack([den_sum, row_delta]), 'seq', axis=2, tiled=True)]
    reduce_sum x1, other arithmetic: 31.4 us -> 0.2 us  [device_step(): jnp.sum((grad_attended * attended_f).reshape(q_rows, PARTS, 2, head_dim),...]
  transfers between devices with their start and end apart: 6 -> 1, of which waited for: 6 -> 1; matrix products, arithmetic and copies ran while one was open for 6% -> 1% of each run, Pallas kernels for 0% -> 0%
where the time goes in v1:
time: 502 us; the launch traced here: 501 us
  Pallas kernels  269 us (54%)
  waiting for transfers between devices  96 us (19%)
  blocking collectives  64.7 us (13%)
  local copies, waits for them, and re-layouts  23.9 us (5%)
  matrix products  23.1 us (5%)
  between operations  15.2 us (3%)
  other arithmetic  9.47 us (2%)
    psum x1, waiting for transfers between devices, device_step(): late = lax.psum((g_norm_attn, g_wq, g_wk, g_wv), 'seq')  96 us
    pallas_call x1, Pallas kernels, attention_bwd(): pl.pallas_call(bwd_kernel, out_shape=(jax.ShapeDtypeStruct((PARTS, TILE,...  76.5 us
    pallas_call x1, Pallas kernels, attention_fwd(): pl.pallas_call(fwd_kernel, out_shape=jax.ShapeDtypeStruct((PARTS, TILE +...  70.8 us
    pallas_call x2, Pallas kernels, reduce_scatter_t(): pl.pallas_call(functools.partial(scatter_kernel, n, with_stats), out_shap...  67 us
    psum x1, blocking collectives, device_step(): late = lax.psum((g_norm_attn, g_wq, g_wk, g_wv), 'seq')  64.7 us
    pallas_call x2, Pallas kernels, all_gather_t(): pl.pallas_call(functools.partial(gather_kernel, n, has), out_shape=tuple(...  54.8 us
    unnamed x99, local copies, waits for them, and re-layouts  15.8 us
  transfers between devices with their start and end apart: 1, of which 1 were waited for; matrix products, arithmetic and copies ran while one was open for 1% of the time, Pallas kernels for 0%

profile of v1, /device:TPU:1, one launch (start us, length us, event | category | flops | bytes accessed | tf_op | source)
XLA Modules:
  0.0 501.5 jit_solution(3480156548151695149)
XLA Ops:
  7.2 1.9 convolution_convert_fusion.1
  9.2 0.9 copy-done.3
  10.1 1.4 fusion.61
  12.4 0.5 copy-done.44
  13.0 0.2 fusion.3
  13.2 0.6 copy.88
  13.9 27.9 %gather_q.1.q_ref = bf16[3,128,4096]{2,1,0:T(8,128)(2,1)} custom-call(bf16[3,32,128]{2,1,0:T(8,128)(2,1)} %bitcast.186), custom_call_target="tpu_custom_call" | custom-call | tf_op jit(solution)/shard_map/gather_q/pallas_call | solution.py:153
  41.8 1.6 convolution_convert_fusion
  43.4 1.4 fusion.60
  44.8 1.2 copy.44
  46.3 0.2 fusion.17
  46.5 0.2 fusion.18
  46.9 0.2 fusion.19
  47.2 0.2 fusion.20
  47.4 0.2 fusion.21.k_ref
  47.6 1.1 copy-done.41
  48.8 70.8 %attention_fwd.1.x_ref = f32[3,136,4096]{2,1,0:T(8,128)} custom-call(bf16[3,128,4096]{2,1,0:T(8,128)(2,1)} %gather_q.1.q_ref, bf16[6,1024,128]{2,1,0:T(8,128)(2,1)} %copy-done.41, bf16[3,128,1024]{2,1,0:T(8,128)(2,1)} %bitcast.184), custom_call_target="tpu_custom_call" | custom-call | flops 6442450944 | bytes 12000000 | tf_op jit(solution)/shard_map/attention_fwd/pallas_call | solution.py:332
  119.6 34.5 %scatter_out.1 = (f32[3,32,128]{2,1,0:T(8,128)}, f32[3,32,128]{2,1,0:T(8,128)}) custom-call(f32[3,136,4096]{2,1,0:T(8,128)} %attention_fwd.1.x_ref), custom_call_target="tpu_custom_call" | custom-call | tf_op jit(solution)/shard_map/scatter_out/pallas_call | solution.py:279
  154.1 1.3 multiply_reduce_fusion.2
  155.6 1.6 fusion.64
  157.2 0.3 fusion.65
  157.5 0.5 multiply_convert_fusion.1
  158.0 0.5 fusion.66
  158.4 1.9 fusion.70
  160.4 1.9 fusion.26
  162.3 0.6 fusion.39
  162.9 1.9 fusion.71
  164.8 0.6 multiply_reduce_fusion
  165.6 0.2 bitcast_multiply_fusion
  165.9 0.2 reduce_sum.65
  166.1 0.6 copy.87
  166.8 1.2 copy.49
  168.0 0.7 maximum_maximum_fusion.refs_1_
  168.7 26.9 %gather_stats.1 = (bf16[3,128,4096]{2,1,0:T(8,128)(2,1)}, f32[3,8,4096]{2,1,0:T(8,128)}) custom-call(bf16[3,32,128]{2,1,0:T(8,128)(2,1)} %bitcast.187, f32[3,32,128]{2,1,0:T(8,128)} %maximum_maximum_fusion.refs_1_), custom_call_target="tpu_custom_call" | custom-call | tf_op jit(solution)/shard_map/gather_stats/pallas_call | solution.py:153
  195.6 1.1 fusion.5
  196.8 1.2 fusion.7
  198.0 1.1 fusion.9
  199.1 0.2 fusion.11
  199.7 1.1 copy-done.40
  200.8 76.5 %attention_bwd.1 = (f32[3,128,4096]{2,1,0:T(8,128)}, f32[3,1024,128]{2,1,0:T(8,128)}, f32[3,1024,128]{2,1,0:T(8,128)}) custom-call(bf16[3,128,4096]{2,1,0:T(8,128)(2,1)} %gather_q.1.q_ref, bf16[3,128,4096]{2,1,0:T(8,128)(2,1)} %get-tuple-element.20.do_ref, f32[3,8,4096]{2,1,0:T(8,128)} %get-tuple-element.21.st_ref, bf16[6,1024,128]{2,1,0:T(8,128)(2,1)} %copy-done.41, ...), custom_call_target="tpu_custom_call" | custom-call | flops 16106127360 | bytes 20000000 | tf_op jit(solution)/shard_map/attention_bwd/pallas_call | solution.py:384
  277.3 2.1 convert_bitcast_fusion
  279.4 0.3 copy.51
  279.7 1.4 fusion.68
  281.1 0.3 copy.52
  281.4 1.4 fusion.69
  282.8 32.6 %scatter_dq.1 = f32[3,32,128]{2,1,0:T(8,128)} custom-call(f32[3,128,4096]{2,1,0:T(8,128)} %get-tuple-element.22.x_ref), custom_call_target="tpu_custom_call" | custom-call | tf_op jit(solution)/shard_map/scatter_dq/pallas_call | solution.py:279
  315.4 1.9 fusion.40
  317.4 1.1 fusion.35
  318.6 0.9 copy-done.16
  319.5 0.3 fusion.30
  319.7 64.7 %all-reduce = (f32[384]{0:T(512)}, f32[384]{0:T(512)}) all-reduce(f32[384]{0:T(512)S(1)} %get-tuple-element.27, f32[384]{0:T(512)S(1)} %get-tuple-element.25), channel_id=1, replica_groups=mesh['data'=1,'seq'=128] {'seq'}, use_global_device_ids=true, to_apply=%region_6.7 | all-reduce | flops 768 | bytes 6144 | tf_op jit(solution)/shard_map/psum | solution.py:486
  384.4 0.7 fusion.32
  385.1 0.7 fusion.67
  385.8 1.8 convolution_add_fusion
  387.7 96.0 %all-reduce.4.cloned.1.call-done = (f32[384,6,64]{0,2,1:T(8,128)}, f32[384,6,64]{0,2,1:T(8,128)}, f32[384,6,64]{0,2,1:T(8,128)}, f32[6,64,384]{2,1,0:T(8,128)}, ...) async-done(((f32[384,6,64]{0,2,1:T(8,128)}, f32[384,6,64]{0,2,1:T(8,128)}, f32[384,6,64]{0,2,1:T(8,128)}, f32[6,64,384]{2,1,0:T(8,128)}, ...) | async-done | bytes 9437200 | tf_op jit(solution)/shard_map/psum | solution.py:486
  483.7 2.0 copy.107
  485.7 0.8 copy.108
  486.5 0.8 copy.109
  487.4 0.8 copy.110
  488.2 1.4 copy.111
  489.6 1.1 copy-done.11
  490.7 1.4 copy.112
  492.1 1.1 copy-done.10
  493.2 1.4 copy.113
  (109 shorter events, 1.9 us)
Async XLA Ops:
  7.2 150.3 %copy-start = (bf16[1536,384]{1,0:T(8,128)(2,1)S(1)}, bf16[1536,384]{1,0:T(8,128)(2,1)}, u32[]{:S(2)}) copy-start(bf16[1536,384]{1,0:T(8,128)(2,1)} %param.25) | copy-start | bytes 3538948
  7.2 476.5 %all-reduce.4.cloned.1.call-start = ((), (), s32[]{:S(2)}) async-start(), calls=%async_computation | async-start | bytes 18874368 | tf_op jit(solution)/shard_map/psum | solution.py:486
  9.2 0.9 copy-start.3
  10.1 2.2 copy-start.27
  10.1 2.3 copy-start.42
  10.1 2.9 copy-start.15
  12.4 0.6 copy-start.44
  13.9 27.9 %copy-start.2 = (bf16[1024,384]{1,0:T(8,128)(2,1)S(1)}, bf16[1024,384]{1,0:T(8,128)(2,1)}, u32[]{:S(2)}) copy-start(bf16[1024,384]{1,0:T(8,128)(2,1)} %param.14) | copy-start | bytes 2359300
  44.8 1.3 copy-start.26
  44.8 1.5 copy-start.25
  44.8 1.7 copy-start.24
  46.0 0.9 copy-start.23
  46.1 1.1 copy-start.22
  46.3 1.1 copy-start.21
  47.6 1.1 copy-start.41
  119.6 34.5 %copy-start.28 = (bf16[32,384]{1,0:T(8,128)(2,1)S(1)}, bf16[32,384]{1,0:T(8,128)(2,1)}, u32[]{:S(2)}) copy-start(bf16[32,384]{1,0:T(8,128)(2,1)} %param.13) | copy-start | bytes 73732
  119.6 35.9 %copy-start.43 = (bf16[384]{0:T(512)(128)(2,1)S(1)}, bf16[384]{0:T(512)(128)(2,1)}, u32[]{:S(2)}) copy-start(bf16[384]{0:T(512)(128)(2,1)} %param.22) | copy-start | bytes 2308
  154.1 3.1 copy-start.9
  154.1 3.4 copy-start.37
  160.4 1.9 copy-start.36
  162.3 2.5 copy-start.8
  162.9 2.6 copy-start.14
  164.8 1.9 copy-start.4
  165.4 2.6 copy-start.39
  165.4 30.2 %copy-start.5 = (bf16[1024,64]{1,0:T(8,128)(2,1)S(1)}, bf16[1024,64]{1,0:T(8,128)(2,1)}, u32[]{:S(2)}) copy-start(bf16[1024,64]{1,0:T(8,128)(2,1)} %constant.31.clone.1) | copy-start | bytes 393220
  165.5 151.9 %copy-start.30 = (f32[32,384]{1,0:T(8,128)}, f32[32,384]{1,0:T(8,128)S(1)}, u32[]{:S(2)}) copy-start(f32[32,384]{1,0:T(8,128)S(1)} %fusion.31) | copy-start | bytes 147460
  167.9 31.2 %copy-start.20 = (bf16[1024,64]{1,0:T(8,128)(2,1)S(1)}, bf16[1024,64]{1,0:T(8,128)(2,1)}, u32[]{:S(2)}) copy-start(bf16[1024,64]{1,0:T(8,128)(2,1)} %get-tuple-element.40) | copy-start | bytes 393220
  195.6 3.7 copy-start.19
  196.8 2.7 copy-start.18
  199.7 1.1 copy-start.40
  279.7 1.7 copy-start.6
  282.8 32.6 %copy-start.29 = (bf16[32,384]{1,0:T(8,128)(2,1)S(1)}, bf16[32,384]{1,0:T(8,128)(2,1)}, u32[]{:S(2)}) copy-start(bf16[32,384]{1,0:T(8,128)(2,1)} %param.13) | copy-start | bytes 73732
  282.8 34.5 %copy-start.38 = (bf16[384,32]{0,1:T(8,128)(2,1)S(1)}, bf16[384,32]{0,1:T(8,128)(2,1)}, u32[]{:S(2)}) copy-start(bf16[384,32]{0,1:T(8,128)(2,1)} %fusion.39) | copy-start | bytes 73732
  318.5 1.0 copy-start.16
  318.5 1.0 copy-start.35
  318.5 65.9 %copy-start.45 = (f32[32]{0:T(128)S(1)}, f32[32]{0:T(128)}, u32[]{:S(2)}) copy-start(f32[32]{0:T(128)} %copy-done.44) | copy-start | bytes 388
  318.5 65.9 %copy-start.31 = (f32[32,384]{1,0:T(8,128)S(1)}, f32[32,384]{1,0:T(8,128)}, u32[]{:S(2)}) copy-start(f32[32,384]{1,0:T(8,128)} %copy-done.30) | copy-start | bytes 147460
  318.5 66.6 %copy-start.7 = (bf16[1024,3,128]{0,2,1:T(8,128)(2,1)S(1)}, bf16[1024,3,128]{0,2,1:T(8,128)(2,1)}, u32[]{:S(2)}) copy-start(bf16[1024,3,128]{0,2,1:T(8,128)(2,1)} %copy-done.6) | copy-start | bytes 2359300
  318.5 66.6 %copy-start.17 = (bf16[384,6,64]{0,2,1:T(8,128)(2,1)S(1)}, bf16[384,6,64]{0,2,1:T(8,128)(2,1)}, u32[]{:S(2)}) copy-start(bf16[384,6,64]{0,2,1:T(8,128)(2,1)} %param.19) | copy-start | bytes 884740
  319.5 66.4 %copy-start.13 = (bf16[384,6,64]{0,2,1:T(8,128)(2,1)S(1)}, bf16[384,6,64]{0,2,1:T(8,128)(2,1)}, u32[]{:S(2)}) copy-start(bf16[384,6,64]{0,2,1:T(8,128)(2,1)} %param.20) | copy-start | bytes 884740
  483.7 2.1 copy-start.34
  483.7 2.9 copy-start.33
  483.7 3.7 copy-start.32
  485.7 2.5 copy-start.12
  488.2 2.5 copy-start.11
  490.7 2.5 copy-start.10
  490.7 3.9 copy-start.1
Sparse Core Ops, SparseCore 0:
  318.7 164.9 all-reduce.3

commit v2 on v1

--- a/solution.py
+++ b/solution.py
@@ -175,19 +175,31 @@
     return outs, maxes + sums
 
 
-def scatter_kernel(n, with_stats, x_ref, *refs):
-    if with_stats:
-        o_ref, st_ref, buf0, acc0, buf1, acc1, buf2, acc2, buf3, csend, crecv, send, recv = refs
-    else:
-        o_ref, buf0, acc0, buf1, acc1, buf2, acc2, buf3, csend, crecv, send, recv = refs
-    at = Place(n)
-    r = TILE // n
-    at.barrier()
-    half = n * n * TILE
-
-    def combine(dst, p, col, blocks):
-        vals = blocks
-        if with_stats:
+class Scatter:
+    def __init__(self, n, at, with_stats, bufs):
+        self.n, self.at, self.with_stats = n, at, with_stats
+        (self.far, self.near, self.buf0, self.buf1, self.acc1, self.buf2, self.acc2, self.buf3,
+         self.csend, self.crecv, self.send, self.recv) = bufs
+        self.step = n * TILE
+
+    @staticmethod
+    def scratch(n, rows, wide):
+        sem = pltpu.SemaphoreType.DMA
+        half = n * n * TILE
+        r = TILE // n
+        return [
+            pltpu.VMEM((PARTS, rows, half), F32), pltpu.VMEM((PARTS, rows, half), F32), pltpu.VMEM((PARTS, rows, half), F32),
+            pltpu.VMEM((PARTS, n - 1, rows, n * TILE), F32), pltpu.VMEM((PARTS, rows, n * TILE), F32),
+            pltpu.VMEM((PARTS, n - 1, rows, TILE), F32), pltpu.VMEM((PARTS, TILE, wide), F32),
+            pltpu.VMEM((PARTS, n - 1, r, wide), F32),
+            sem((PARTS, n)), sem((PARTS, n)), sem((3, PARTS, n - 1)), sem((3, PARTS, n - 1)),
+        ]
+
+    def chunk(self, p, k):
+        return lax.rem(self.at.coord[ORDERS[p][0]] + k, self.n)
+
+    def combine(self, dst, p, col, vals):
+        if self.with_stats:
             outs, stats = merge(vals, 0)
             dst[p, 0:TILE // 2, col] = outs[0]
             dst[p, TILE // 2:TILE, col] = outs[1]
@@ -195,94 +207,217 @@
         else:
             dst[p, :, col] = functools.reduce(jnp.add, vals)
 
-    first = []
-    for p in range(PARTS):
-        c = rcopy(x_ref.at[p, :, lanes((1 - at.core) * half, half)], buf0.at[p], csend.at[p], crecv.at[p], at.other_core())
-        c.start()
-        first.append(c)
-    copies = {}
-    for p in range(PARTS):
-        a1 = ORDERS[p][0]
-        first[p].wait()
-        step = n * TILE
-        for j in range(n):
-            combine(acc0, p, pl.ds(j * step, step),
-                    [x_ref[p, :, lanes(at.core * half + j * step, step)], buf0[p, :, j * step:(j + 1) * step]])
+    def core_copy(self, p, k):
+        view = (p, slice(None), lanes(self.chunk(p, k) * self.step, self.step))
+        return rcopy(self.far.at[view], self.buf0.at[view], self.csend.at[p, k], self.crecv.at[p, k], self.at.other_core())
+
+    def first_copy(self, p, k):
+        return rcopy(self.near.at[p, :, lanes(self.chunk(p, k) * self.step, self.step)], self.buf1.at[p, k - 1],
+                     self.send.at[0, p, k - 1], self.recv.at[0, p, k - 1], self.at.along(ORDERS[p][0], k))
+
+    def far_done(self, k):
+        for p in range(PARTS):
+            self.core_copy(p, k).start()
+
+    def near_done(self, k):
+        for p in range(PARTS):
+            self.core_copy(p, k).wait()
+
+            def fold(j, _, p=p):
+                col = lanes(self.chunk(p, k) * self.step + j * TILE, TILE)
+                self.combine(self.near, p, col, [self.near[p, :, col], self.buf0[p, :, col]])
+                return 0
+
+            lax.fori_loop(0, self.n, fold, 0)
+
+            @pl.when(k > 0)
+            def _(p=p):
+                self.first_copy(p, k).start()
+
+    def finish(self, o_ref, st_ref=None):
+        n, at = self.n, self.at
+        r = TILE // n
+        copies = {}
+        for p in range(PARTS):
+            a1, a2, _ = ORDERS[p]
+            for k in range(1, n):
+                self.first_copy(p, k).wait()
+            mine = at.coord[a1] * n * TILE
+            for j in range(n):
+                col = slice(j * TILE, (j + 1) * TILE)
+                self.combine(self.acc1, p, pl.ds(j * TILE, TILE),
+                             [self.near[p, :, lanes(mine + j * TILE, TILE)]] + [self.buf1[p, k, :, col] for k in range(n - 1)])
+            for k in range(1, n):
+                there = lax.rem(at.coord[a2] + k, n)
+                c = rcopy(self.acc1.at[p, :, lanes(there * TILE, TILE)], self.buf2.at[p, k - 1],
+                          self.send.at[1, p, k - 1], self.recv.at[1, p, k - 1], at.along(a2, k))
+                c.start()
+                copies[1, p, k] = c
+        for p in range(PARTS):
+            _, a2, a3 = ORDERS[p]
+            for k in range(1, n):
+                copies[1, p, k].wait()
+            blocks = [self.acc1[p, :, lanes(at.coord[a2] * TILE, TILE)]] + [self.buf2[p, k] for k in range(n - 1)]
+            if self.with_stats:
+                outs, stats = merge(blocks, 0)
+                self.acc2[p, :, 0:TILE] = jnp.concatenate(outs, axis=0).T
+                tail = jnp.concatenate(stats + [jnp.zeros((TILE - 4, TILE), F32)], axis=0)
+                self.acc2[p, :, TILE:2 * TILE] = tail.T
+            else:
+                self.acc2[p] = functools.reduce(jnp.add, blocks).T
+            for k in range(1, n):
+                there = lax.rem(at.coord[a3] + k, n)
+                c = rcopy(self.acc2.at[p, pl.ds(pl.multiple_of(there * r, r), r), :], self.buf3.at[p, k - 1],
+                          self.send.at[2, p, k - 1], self.recv.at[2, p, k - 1], at.along(a3, k))
+                c.start()
+                copies[2, p, k] = c
+        for p in range(PARTS):
+            a3 = ORDERS[p][2]
+            for k in range(1, n):
+                copies[2, p, k].wait()
+            blocks = [self.acc2[p, pl.ds(pl.multiple_of(at.coord[a3] * r, r), r), :]] + [self.buf3[p, k] for k in range(n - 1)]
+            if self.with_stats:
+                outs, (m0, m1, l0, l1) = merge(blocks, 1)
+                o_ref[p] = jnp.concatenate([outs[0] / l0, outs[1] / l1], axis=1)
+                col = lax.broadcasted_iota(jnp.int32, (r, TILE), 1)
+                st_ref[p] = jnp.where(col == 0, m0 + jnp.log(l0), jnp.where(col == 1, m1 + jnp.log(l1), 0.0))
+            else:
+                o_ref[p] = functools.reduce(jnp.add, blocks)
+
+
+def rows_of(start, size):
+    return pl.ds(pl.multiple_of(start, 8), size)
+
+
+class Wide:
+    def __init__(self, shape, n):
+        self.part, self.cols = shape[0] // PARTS, shape[1]
+        self.r1, self.r2, self.c3 = self.part // 2, self.part // 2 // n, shape[1] // n
+        self.l1, self.l2, self.l3 = (self.r1, self.cols), (self.r2, self.cols), (self.r2, self.c3)
+
+    def full1(self, p, c):
+        return rows_of(self.part * p + self.r1 * c, self.r1), slice(None)
+
+    def full2(self, p, c, a):
+        return rows_of(self.part * p + self.r1 * c + self.r2 * a, self.r2), slice(None)
+
+    def full3(self, p, c, a, b):
+        return rows_of(self.part * p + self.r1 * c + self.r2 * a, self.r2), lanes(self.c3 * b, self.c3)
+
+    def in1(self, a):
+        return rows_of(self.r2 * a, self.r2), slice(None)
+
+    def in2(self, b):
+        return slice(None), lanes(self.c3 * b, self.c3)
+
+
+class Tall(Wide):
+    def __init__(self, shape, n):
+        super().__init__(shape, n)
+        self.r3 = self.r2 // n
+        self.l3 = (self.r3, self.cols)
+
+    def full3(self, p, c, a, b):
+        return rows_of(self.part * p + self.r1 * c + self.r2 * a + self.r3 * b, self.r3), slice(None)
+
+    def in2(self, b):
+        return rows_of(self.r3 * b, self.r3), slice(None)
+
+
+class Stack:
+    def __init__(self, shape, n):
+        w, rows, cols = shape
+        self.part, self.w3 = rows // PARTS, w // n
+        self.r1, self.r2 = self.part // 2, self.part // 2 // n
+        self.l1, self.l2, self.l3 = (w, self.r1, cols), (w, self.r2, cols), (self.w3, self.r2, cols)
+
+    def full1(self, p, c):
+        return slice(None), rows_of(self.part * p + self.r1 * c, self.r1), slice(None)
+
+    def full2(self, p, c, a):
+        return slice(None), rows_of(self.part * p + self.r1 * c + self.r2 * a, self.r2), slice(None)
+
+    def full3(self, p, c, a, b):
+        return pl.ds(self.w3 * b, self.w3), rows_of(self.part * p + self.r1 * c + self.r2 * a, self.r2), slice(None)
+
+    def in1(self, a):
+        return slice(None), rows_of(self.r2 * a, self.r2), slice(None)
+
+    def in2(self, b):
+        return pl.ds(self.w3 * b, self.w3), slice(None), slice(None)
+
+
+REDUCE_REFS = 15
+
+
+class Reduce:
+    def __init__(self, n, at, form, src, out, bufs):
+        self.n, self.at, self.form, self.src, self.out = n, at, form, src, out
+        (self.own, self.buf0, self.buf1, self.acc1, self.buf2, self.buf3, self.lsem,
+         self.csend, self.crecv, self.send, self.recv, self.gsend, self.grecv, self.dsend, self.drecv) = bufs
+
+    @staticmethod
+    def scratch(n, form):
+        sem = pltpu.SemaphoreType.DMA
+        return [
+            pltpu.VMEM((PARTS,) + form.l1, F32), pltpu.VMEM((PARTS,) + form.l1, F32),
+            pltpu.VMEM((PARTS, n - 1) + form.l2, F32), pltpu.VMEM((PARTS,) + form.l2, F32),
+            pltpu.VMEM((PARTS, n - 1) + form.l3, F32), pltpu.VMEM((PARTS, n) + form.l3, F32),
+            sem((PARTS,)), sem((PARTS,)), sem((PARTS,)), sem((3, PARTS, n - 1)), sem((3, PARTS, n - 1)),
+            sem((2, PARTS, n - 1)), sem((2, PARTS, n - 1)), sem((PARTS,)), sem((PARTS,)),
+        ]
+
+    def spots(self, p):
+        a1, a2, a3 = ORDERS[p]
+        at = self.at
+        return at.coord[a1], at.coord[a2], at.coord[a3]
+
+    def copies(self, stage, p):
+        at, n, form = self.at, self.n, self.form
+        A1, A2, A3 = self.spots(p)
+        a1, a2, a3 = ORDERS[p]
+        c = at.core
+        if stage == 0:
+            return [rcopy(self.src.at[form.full1(p, 1 - c)], self.buf0.at[p], self.csend.at[p], self.crecv.at[p], at.other_core()),
+                    pltpu.make_async_copy(self.src.at[form.full1(p, c)], self.own.at[p], self.lsem.at[p])]
+        out = []
+        if stage == 6:
+            view = self.out.at[form.full1(p, c)]
+            return [rcopy(view, view, self.dsend.at[p], self.drecv.at[p], at.other_core())]
         for k in range(1, n):
-            there = lax.rem(at.coord[a1] + k, n)
-            c = rcopy(acc0.at[p, :, lanes(there * step, step)], buf1.at[p, k - 1],
-                      send.at[0, p, k - 1], recv.at[0, p, k - 1], at.along(a1, k))
-            c.start()
-            copies[0, p, k] = c
-    for p in range(PARTS):
-        a1, a2, _ = ORDERS[p]
-        for k in range(1, n):
-            copies[0, p, k].wait()
-        mine = at.coord[a1] * n * TILE
-        for j in range(n):
-            col = slice(j * TILE, (j + 1) * TILE)
-            combine(acc1, p, pl.ds(j * TILE, TILE),
-                    [acc0[p, :, lanes(mine + j * TILE, TILE)]] + [buf1[p, k, :, col] for k in range(n - 1)])
-        for k in range(1, n):
-            there = lax.rem(at.coord[a2] + k, n)
-            c = rcopy(acc1.at[p, :, lanes(there * TILE, TILE)], buf2.at[p, k - 1],
-                      send.at[1, p, k - 1], recv.at[1, p, k - 1], at.along(a2, k))
-            c.start()
-            copies[1, p, k] = c
-    for p in range(PARTS):
-        _, a2, a3 = ORDERS[p]
-        for k in range(1, n):
-            copies[1, p, k].wait()
-        blocks = [acc1[p, :, lanes(at.coord[a2] * TILE, TILE)]] + [buf2[p, k] for k in range(n - 1)]
-        if with_stats:
-            outs, stats = merge(blocks, 0)
-            acc2[p, :, 0:TILE] = jnp.concatenate(outs, axis=0).T
-            tail = jnp.concatenate(stats + [jnp.zeros((TILE - 4, TILE), F32)], axis=0)
-            acc2[p, :, TILE:2 * TILE] = tail.T
-        else:
-            acc2[p] = functools.reduce(jnp.add, blocks).T
-        for k in range(1, n):
-            there = lax.rem(at.coord[a3] + k, n)
-            c = rcopy(acc2.at[p, pl.ds(pl.multiple_of(there * r, r), r), :], buf3.at[p, k - 1],
-                      send.at[2, p, k - 1], recv.at[2, p, k - 1], at.along(a3, k))
-            c.start()
-            copies[2, p, k] = c
-    for p in range(PARTS):
-        a3 = ORDERS[p][2]
-        for k in range(1, n):
-            copies[2, p, k].wait()
-        blocks = [acc2[p, pl.ds(pl.multiple_of(at.coord[a3] * r, r), r), :]] + [buf3[p, k] for k in range(n - 1)]
-        if with_stats:
-            outs, (m0, m1, l0, l1) = merge(blocks, 1)
-            o_ref[p] = jnp.concatenate([outs[0] / l0, outs[1] / l1], axis=1)
-            col = lax.broadcasted_iota(jnp.int32, (r, TILE), 1)
-            st_ref[p] = jnp.where(col == 0, m0 + jnp.log(l0), jnp.where(col == 1, m1 + jnp.log(l1), 0.0))
-        else:
-            o_ref[p] = functools.reduce(jnp.add, blocks)
-
-
-def reduce_scatter_t(n, cid, x, with_stats):
-    rows = x.shape[1]
-    r = TILE // n
-    wide = 2 * TILE if with_stats else TILE
-    vm = pl.BlockSpec(memory_space=pltpu.VMEM)
-    sem = pltpu.SemaphoreType.DMA
-    half = n * n * TILE
-    outs = [jax.ShapeDtypeStruct((PARTS, r, TILE), F32)] * (2 if with_stats else 1)
-    scratch = [
-        pltpu.VMEM((PARTS, rows, half), F32), pltpu.VMEM((PARTS, rows, half), F32),
-        pltpu.VMEM((PARTS, n - 1, rows, n * TILE), F32), pltpu.VMEM((PARTS, rows, n * TILE), F32),
-        pltpu.VMEM((PARTS, n - 1, rows, TILE), F32), pltpu.VMEM((PARTS, TILE, wide), F32),
-        pltpu.VMEM((PARTS, n - 1, r, wide), F32),
-        sem((PARTS,)), sem((PARTS,)), sem((3, PARTS, n - 1)), sem((3, PARTS, n - 1)),
-    ]
-    res = pl.pallas_call(
-        functools.partial(scatter_kernel, n, with_stats),
-        out_shape=tuple(outs), in_specs=[vm], out_specs=(vm,) * len(outs), scratch_shapes=scratch,
-        name="scatter_out" if with_stats else "scatter_dq",
-        compiler_params=pltpu.CompilerParams(collective_id=cid, has_side_effects=True, vmem_limit_bytes=VMEM_LIMIT),
-    )(x)
-    return res if with_stats else res[0]
+            if stage == 1:
+                args = (self.own.at[p].at[form.in1(lax.rem(A1 + k, n))], self.buf1.at[p, k - 1], self.send.at[0, p, k - 1], self.recv.at[0, p, k - 1], at.along(a1, k))
+            elif stage == 2:
+                args = (self.acc1.at[p].at[form.in2(lax.rem(A2 + k, n))], self.buf2.at[p, k - 1], self.send.at[1, p, k - 1], self.recv.at[1, p, k - 1], at.along(a2, k))
+            elif stage == 3:
+                args = (self.buf3.at[p, A3], self.buf3.at[p, A3], self.send.at[2, p, k - 1], self.recv.at[2, p, k - 1], at.along(a3, k))
+            elif stage == 4:
+                view = self.out.at[form.full3(p, c, A1, A2)]
+                args = (view, view, self.gsend.at[0, p, k - 1], self.grecv.at[0, p, k - 1], at.along(a2, k))
+            else:
+                view = self.out.at[form.full2(p, c, A1)]
+                args = (view, view, self.gsend.at[1, p, k - 1], self.grecv.at[1, p, k - 1], at.along(a1, k))
+            out.append(rcopy(*args))
+        return out
+
+    def advance(self, stage):
+        form, n = self.form, self.n
+        for p in range(PARTS):
+            A1, A2, A3 = self.spots(p)
+            if stage > 0:
+                for c in self.copies(stage - 1, p):
+                    c.wait()
+            if stage == 1:
+                self.own[p] = self.own[p] + self.buf0[p]
+            elif stage == 2:
+                self.acc1[p] = functools.reduce(jnp.add, [self.own[(p,) + form.in1(A1)]] + [self.buf1[p, k] for k in range(n - 1)])
+            elif stage == 3:
+                self.buf3[p, A3] = functools.reduce(jnp.add, [self.acc1[(p,) + form.in2(A2)]] + [self.buf2[p, k] for k in range(n - 1)])
+            elif stage == 4:
+                self.out[form.full3(p, self.at.core, A1, A2)] = functools.reduce(jnp.add, [self.buf3[p, k] for k in range(n)])
+            if stage < 7:
+                for c in self.copies(stage, p):
+                    c.start()
 
 
 QB = 256
@@ -300,93 +435,221 @@
     return [hi, mid, lo]
 
 
-def fwd_kernel(q_ref, k_ref, vt_ref, o_ref):
-    total = q_ref.shape[2]
+def fold_rows(op, v, last):
+    while v.shape[0] > 64:
+        h = v.shape[0] // 2
+        v = op(v[:h], v[h:])
+    return last(v, axis=0, keepdims=True)
+
+
+def blocks_loop(n, scatter, block, events):
+    per = n * TILE // QB
+    at = scatter.at
+
+    def body(t, _):
+        u = t // per
+        k = n - 1 - u // 2
+        near = lax.rem(u, 2)
+        half = jnp.where(near == 1, at.core, 1 - at.core)
+        for p in range(PARTS):
+            inside = scatter.chunk(p, k) * (n * TILE) + lax.rem(t, per) * QB
+            src = pl.multiple_of(half * (n * n * TILE) + inside, QB)
+            block(p, pl.ds(src, QB), near, pl.ds(pl.multiple_of(inside, QB), QB))
+        last = lax.rem(t, per) == per - 1
+
+        @pl.when(last & (near == 0))
+        def _():
+            scatter.far_done(k)
+
+        @pl.when(last & (near == 1))
+        def _():
+            scatter.near_done(k)
+
+        for when, action in events:
+            @pl.when(t == when)
+            def _(action=action):
+                action()
+        return 0
+
+    lax.fori_loop(0, 2 * n * per, body, 0)
+
+
+def put(scatter, near, p, row, col, val):
+    @pl.when(near == 1)
+    def _():
+        scatter.near[p, row, col] = val
+
+    @pl.when(near == 0)
+    def _():
+        scatter.far[p, row, col] = val
+
+
+def fwd_kernel(n, q_ref, k_ref, vt_ref, o_ref, st_ref, *bufs):
     half = TILE // 2
     one = jnp.ones((1, QB), F32)
     aux = aux_rows([one], QB)
-
-    def body(b, _):
-        col = pl.ds(pl.multiple_of(b * QB, QB), QB)
-        for p in range(PARTS):
-            maxes, sums = [], []
-            for j in range(2):
-                qa = jnp.concatenate([q_ref[p, half * j:half * (j + 1), col], aux], axis=0)
-                s = jnp.dot(k_ref[2 * p + j], qa, preferred_element_type=F32)
-                m = jnp.max(s, axis=0, keepdims=True)
-                e = jnp.exp(s - m)
-                l = jnp.sum(e, axis=0, keepdims=True)
-                o_ref[p, half * j:half * (j + 1), col] = jnp.dot(
-                    vt_ref[p, half * j:half * (j + 1), :], e.astype(BF16), preferred_element_type=F32)
-                maxes.append(m)
-                sums.append(l)
-            o_ref[p, TILE:TILE + 8, col] = jnp.concatenate(maxes + sums + [jnp.zeros((4, QB), F32)], axis=0)
-        return 0
-
-    lax.fori_loop(0, total // QB, body, 0)
-
-
-def attention_fwd(q_t, k_aug, v_t):
+    at = Place(n)
+    at.barrier()
+    scatter = Scatter(n, at, True, bufs)
+
+    def block(p, src, near, dst):
+        maxes, sums, outs = [], [], []
+        for j in range(2):
+            qa = jnp.concatenate([q_ref[p, half * j:half * (j + 1), src], aux], axis=0)
+            s = jnp.dot(k_ref[2 * p + j], qa, preferred_element_type=F32)
+            m = fold_rows(jnp.maximum, s, jnp.max)
+            e = jnp.exp(s - m)
+            sums.append(fold_rows(jnp.add, e, jnp.sum))
+            outs.append(jnp.dot(vt_ref[p, half * j:half * (j + 1), :], e.astype(BF16), preferred_element_type=F32))
+            maxes.append(m)
+        val = jnp.concatenate(outs + maxes + sums + [jnp.zeros((4, QB), F32)], axis=0)
+        put(scatter, near, p, slice(None), dst, val)
+
+    blocks_loop(n, scatter, block, [])
+    scatter.finish(o_ref, st_ref)
+
+
+def attention_fwd(n, cid, q_t, k_aug, v_t):
     total, keys = q_t.shape[2], k_aug.shape[1]
+    r = TILE // n
     vm = pl.BlockSpec(memory_space=pltpu.VMEM)
     return pl.pallas_call(
-        fwd_kernel, out_shape=jax.ShapeDtypeStruct((PARTS, TILE + 8, total), F32),
-        in_specs=[vm] * 3, out_specs=vm, name="attention_fwd",
+        functools.partial(fwd_kernel, n), out_shape=(jax.ShapeDtypeStruct((PARTS, r, TILE), F32),) * 2,
+        in_specs=[vm] * 3, out_specs=(vm,) * 2, name="attention_fwd",
+        scratch_shapes=Scatter.scratch(n, TILE + 8, 2 * TILE),
         cost_estimate=pl.CostEstimate(flops=4 * 384 * total * keys, bytes_accessed=12_000_000, transcendentals=6 * total * keys),
-        compiler_params=pltpu.CompilerParams(vmem_limit_bytes=VMEM_LIMIT),
+        compiler_params=pltpu.CompilerParams(collective_id=cid, has_side_effects=True, vmem_limit_bytes=VMEM_LIMIT),
     )(q_t, k_aug, v_t)
 
 
-def bwd_kernel(q_ref, do_ref, st_ref, k_ref, v_ref, kt_ref, dq_ref, dk_ref, dv_ref):
-    total = q_ref.shape[2]
+SCATTER_REFS = 12
+
+
+def bwd_kernel(n, forms, q_ref, do_ref, st_ref, k_ref, v_ref, kt_ref, *refs):
+    count = len(forms)
+    grads, refs = refs[:count], refs[count:]
+    dq_ref, dk_ref, dv_ref = refs[:3]
+    sums, refs = refs[3:3 + count], refs[3 + count:]
+    dk_acc, dv_acc = refs[:2]
+    bufs, refs = refs[2:2 + SCATTER_REFS], refs[2 + SCATTER_REFS:]
     half = TILE // 2
     one = jnp.ones((1, QB), F32)
     zero = jnp.zeros((1, QB), F32)
     blank = jnp.zeros((half, QB), BF16)
     nt = (((1,), (1,)), ((), ()))
-    dk_ref[...] = jnp.zeros_like(dk_ref)
-    dv_ref[...] = jnp.zeros_like(dv_ref)
-
-    def body(b, _):
-        col = pl.ds(pl.multiple_of(b * QB, QB), QB)
-        for p in range(PARTS):
-            probs, dscores, dos, qs = [], [], [], []
-            for j in range(2):
-                qh = q_ref[p, half * j:half * (j + 1), col]
-                doh = do_ref[p, half * j:half * (j + 1), col]
-                lse = st_ref[p, j:j + 1, col]
-                delta = st_ref[p, 2 + j:3 + j, col]
-                qa = jnp.concatenate([qh, aux_rows([one] + split3(-lse), QB)], axis=0)
-                da = jnp.concatenate([doh, aux_rows([zero] + split3(-delta), QB)], axis=0)
-                e = jnp.exp(jnp.dot(k_ref[2 * p + j], qa, preferred_element_type=F32))
-                dp = jnp.dot(v_ref[2 * p + j], da, preferred_element_type=F32)
-                ds = (e * dp).astype(BF16)
-                probs.append(e.astype(BF16))
-                dscores.append(ds)
-                order = (lambda a: [a, blank]) if j == 0 else (lambda a: [blank, a])
-                dos.append(jnp.concatenate(order(doh), axis=0))
-                qs.append(jnp.concatenate(order(qh), axis=0))
-                dq_ref[p, half * j:half * (j + 1), col] = 0.125 * jnp.dot(
-                    kt_ref[p, half * j:half * (j + 1), :], ds, preferred_element_type=F32)
-            dv_ref[p] += (lax.dot_general(probs[0], dos[0], nt, preferred_element_type=F32)
-                          + lax.dot_general(probs[1], dos[1], nt, preferred_element_type=F32))
-            dk_ref[p] += (lax.dot_general(dscores[0], qs[0], nt, preferred_element_type=F32)
-                          + lax.dot_general(dscores[1], qs[1], nt, preferred_element_type=F32))
-        return 0
-
-    lax.fori_loop(0, total // QB, body, 0)
-
-
-def attention_bwd(q_t, do_t, stats, k_aug, v_aug, k_t):
+    at = Place(n)
+    at.barrier()
+    scatter = Scatter(n, at, False, bufs)
+    reduces = [Reduce(n, at, form, grads[i], sums[i], refs[REDUCE_REFS * i:REDUCE_REFS * (i + 1)])
+               for i, form in enumerate(forms)]
+
+    def advance(stage):
+        for red in reduces:
+            red.advance(stage)
+
+    advance(0)
+    dk_acc[...] = jnp.zeros_like(dk_acc)
+    dv_acc[...] = jnp.zeros_like(dv_acc)
+
+    def block(p, src, near, dst):
+        probs, dscores, dos, qs, dqs = [], [], [], [], []
+        for j in range(2):
+            qh = q_ref[p, half * j:half * (j + 1), src]
+            doh = do_ref[p, half * j:half * (j + 1), src]
+            lse = st_ref[p, j:j + 1, src]
+            delta = st_ref[p, 2 + j:3 + j, src]
+            qa = jnp.concatenate([qh, aux_rows([one] + split3(-lse), QB)], axis=0)
+            da = jnp.concatenate([doh, aux_rows([zero] + split3(-delta), QB)], axis=0)
+            e = jnp.exp(jnp.dot(k_ref[2 * p + j], qa, preferred_element_type=F32))
+            dp = jnp.dot(v_ref[2 * p + j], da, preferred_element_type=F32)
+            ds = (e * dp).astype(BF16)
+            probs.append(e.astype(BF16))
+            dscores.append(ds)
+            order = (lambda a: [a, blank]) if j == 0 else (lambda a: [blank, a])
+            dos.append(jnp.concatenate(order(doh), axis=0))
+            qs.append(jnp.concatenate(order(qh), axis=0))
+            dqs.append(0.125 * jnp.dot(kt_ref[p, half * j:half * (j + 1), :], ds, preferred_element_type=F32))
+        dv_acc[p] += (lax.dot_general(probs[0], dos[0], nt, preferred_element_type=F32)
+                      + lax.dot_general(probs[1], dos[1], nt, preferred_element_type=F32))
+        dk_acc[p] += (lax.dot_general(dscores[0], qs[0], nt, preferred_element_type=F32)
+                      + lax.dot_general(dscores[1], qs[1], nt, preferred_element_type=F32))
+        put(scatter, near, p, slice(None), dst, jnp.concatenate(dqs, axis=0))
+
+    trips = 2 * n * (n * TILE // QB)
+    when = [min(w, trips - 1) for w in (1, trips // 2, trips // 2 + 1, trips // 2 + 2, trips // 2 + 3, max(trips // 2 + 3, trips - 2))]
+    blocks_loop(n, scatter, block, [(w, functools.partial(advance, i + 1)) for i, w in enumerate(when)])
+    for p in range(PARTS):
+        dk_ref[:, p * TILE:(p + 1) * TILE] = dk_acc[p].astype(BF16)
+        dv_ref[:, p * TILE:(p + 1) * TILE] = dv_acc[p].astype(BF16)
+    scatter.finish(dq_ref)
+    advance(7)
+
+
+def attention_bwd(n, cid, q_t, do_t, stats, k_aug, v_aug, k_t, wide, tall):
     total, keys = q_t.shape[2], k_aug.shape[1]
+    r = TILE // n
+    forms = [Wide(a.shape, n) for a in wide] + [Tall(a.shape, n) for a in tall]
+    grads = list(wide) + list(tall)
     vm = pl.BlockSpec(memory_space=pltpu.VMEM)
-    acc = jax.ShapeDtypeStruct((PARTS, keys, TILE), F32)
+    flat = jax.ShapeDtypeStruct((keys, PARTS * TILE), BF16)
+    acc = pltpu.VMEM((PARTS, keys, TILE), F32)
+    outs = [jax.ShapeDtypeStruct((PARTS, r, TILE), F32), flat, flat] + [jax.ShapeDtypeStruct(a.shape, F32) for a in grads]
+    scratch = [acc, acc] + Scatter.scratch(n, TILE, TILE)
+    for form in forms:
+        scratch += Reduce.scratch(n, form)
     return pl.pallas_call(
-        bwd_kernel, out_shape=(jax.ShapeDtypeStruct((PARTS, TILE, total), F32), acc, acc),
-        in_specs=[vm] * 6, out_specs=(vm,) * 3, name="attention_bwd",
+        functools.partial(bwd_kernel, n, forms), out_shape=tuple(outs),
+        in_specs=[vm] * 6 + [pl.BlockSpec(memory_space=pl.ANY)] * len(grads), out_specs=(vm,) * len(outs), name="attention_bwd",
+        scratch_shapes=scratch,
         cost_estimate=pl.CostEstimate(flops=10 * 384 * total * keys, bytes_accessed=20_000_000, transcendentals=6 * total * keys),
-        compiler_params=pltpu.CompilerParams(vmem_limit_bytes=VMEM_LIMIT),
-    )(q_t, do_t, stats, k_aug, v_aug, k_t)
+        compiler_params=pltpu.CompilerParams(collective_id=cid, has_side_effects=True, vmem_limit_bytes=VMEM_LIMIT),
+    )(q_t, do_t, stats, k_aug, v_aug, k_t, *grads)
+
+
+def reduce_kernel(n, form, src, small, out, small_out, slots, pair, ssend, srecv, *bufs):
+    at = Place(n)
+    at.barrier()
+    red = Reduce(n, at, form, src, out, bufs)
+
+    def small_copies(stage):
+        if stage == 3:
+            return [rcopy(pair.at[at.core], pair.at[at.core], ssend.at[3, 0], srecv.at[3, 0], at.other_core())]
+        mine = slots.at[stage, at.coord[stage]]
+        return [rcopy(mine, mine, ssend.at[stage, k - 1], srecv.at[stage, k - 1], at.along(stage, k)) for k in range(1, n)]
+
+    red.advance(0)
+    slots[0, at.coord[0]] = small[...]
+    for c in small_copies(0):
+        c.start()
+    for stage in range(1, 8):
+        red.advance(stage)
+        if stage < 5:
+            for c in small_copies(stage - 1):
+                c.wait()
+            if stage < 4:
+                val = functools.reduce(jnp.add, [slots[stage - 1, k] for k in range(n)])
+                if stage < 3:
+                    slots[stage, at.coord[stage]] = val
+                else:
+                    pair[at.core] = val
+                for c in small_copies(stage):
+                    c.start()
+            else:
+                small_out[...] = pair[0] + pair[1]
+
+
+def all_reduce_late(n, cid, stack, small):
+    form = Stack(stack.shape, n)
+    vm = pl.BlockSpec(memory_space=pltpu.VMEM)
+    sem = pltpu.SemaphoreType.DMA
+    return pl.pallas_call(
+        functools.partial(reduce_kernel, n, form),
+        out_shape=(jax.ShapeDtypeStruct(stack.shape, F32), jax.ShapeDtypeStruct(small.shape, F32)),
+        in_specs=[pl.BlockSpec(memory_space=pl.ANY), vm], out_specs=(vm, vm), name="reduce_late",
+        scratch_shapes=[pltpu.VMEM((3, n) + small.shape, F32), pltpu.VMEM((2,) + small.shape, F32),
+                        sem((4, n - 1)), sem((4, n - 1))] + Reduce.scratch(n, form),
+        compiler_params=pltpu.CompilerParams(collective_id=cid, has_side_effects=True, vmem_limit_bytes=VMEM_LIMIT),
+    )(stack, small)
 
 
 def solution(mesh):
@@ -434,8 +697,7 @@
         k_aug = augment(mem_keys, aux_k)
         v_aug = augment(mem_vals, aux_v)
 
-        partial = attention_fwd(q_t, k_aug, v_t)
-        out_parts, lse = reduce_scatter_t(n, 1, partial, True)
+        out_parts, lse = attention_fwd(n, 1, q_t, k_aug, v_t)
         attended_f = by_row(out_parts)
 
         attended = attended_f.astype(BF16)
@@ -461,32 +723,31 @@
         grad_hidden_norm, g_norm_mlp = mlp_norm_pull(grad_normed_mlp)
         grad_hidden = grad_out + grad_hidden_norm
         grad_hidden_b = grad_hidden.astype(BF16)
-        g_wo = jnp.einsum('qe,qd->ed', attended, grad_hidden_b, preferred_element_type=F32).reshape(heads, head_dim, model_dim)
+        g_wo = jnp.einsum('qe,qd->ed', attended, grad_hidden_b, preferred_element_type=F32)
         grad_attended = jnp.einsum('qd,ed->qe', grad_hidden_b, wo, preferred_element_type=F32)
         delta = jnp.sum((grad_attended * attended_f).reshape(q_rows, PARTS, 2, head_dim), axis=-1)
         delta = jnp.transpose(delta, (1, 0, 2))
         stats_in = jnp.concatenate([lse[:, :, 0:2], delta, jnp.zeros((PARTS, q_rows, TILE - 4), F32)], axis=2)
         do_t, stats = all_gather_t(n, 2, by_part(grad_attended.astype(BF16)), stats_in)
 
-        early = lax.psum((g_wo, g_norm_mlp, g_gate, g_up, g_down), 'seq')
-
-        dq_part, dk, dv = attention_bwd(q_t, do_t, stats, k_aug, v_aug, k_t)
-        grad_query_b = by_row(reduce_scatter_t(n, 3, dq_part, False)).astype(BF16)
+        dq_parts, dk_b, dv_b, g_gate, g_up, g_down = attention_bwd(
+            n, 3, q_t, do_t, stats, k_aug, v_aug, k_t, (g_gate, g_up), (g_down,))
+        grad_query_b = by_row(dq_parts).astype(BF16)
 
         g_wq = jnp.einsum('td,te->de', normed, grad_query_b, preferred_element_type=F32)
         grad_normed = jnp.einsum('te,de->td', grad_query_b, wq, preferred_element_type=F32)
         grad_x_norm, g_norm_attn = norm_pull(grad_normed)
         g_dec = grad_hidden + grad_x_norm
-        dk_b = by_row(dk.astype(BF16))
-        dv_b = by_row(dv.astype(BF16))
         g_wk = jnp.einsum('td,te->de', memory, dk_b, preferred_element_type=F32)
         g_wv = jnp.einsum('td,te->de', memory, dv_b, preferred_element_type=F32)
         g_mem = (jnp.einsum('te,de->td', dk_b, wk, preferred_element_type=F32)
                  + jnp.einsum('te,de->td', dv_b, wv, preferred_element_type=F32))
-        late = lax.psum((g_norm_attn, g_wq, g_wk, g_wv), 'seq')
+        small = jnp.concatenate([g_norm_attn[None], g_norm_mlp[None], jnp.zeros((6, model_dim), F32)], axis=0)
+        late, small = all_reduce_late(n, 4, jnp.stack([g_wq, g_wk, g_wv, g_wo]), small)
         cube = (model_dim, heads, head_dim)
-        g_wo, g_norm_mlp, g_gate, g_up, g_down = early
-        g_norm_attn, g_wq, g_wk, g_wv = late
+        g_wq, g_wk, g_wv = late[0], late[1], late[2]
+        g_wo = late[3].reshape(heads, head_dim, model_dim)
+        g_norm_attn, g_norm_mlp = small[0], small[1]
         return (g_dec, g_mem, g_norm_attn, g_wq.reshape(cube), g_wk.reshape(cube), g_wv.reshape(cube),
                 g_wo, g_norm_mlp, g_gate, g_up, g_down)
 

time: 502 us -> 343 us (0.68)
  waiting for transfers between devices: 96 us -> 0 us
  blocking collectives: 64.7 us -> 0 us
  Pallas kernels: 269 us -> 288 us
  between operations: 15.2 us -> 1.83 us
    psum x1 -> x0, waiting for transfers between devices: 96 us -> none  [device_step(): late = lax.psum((g_norm_attn, g_wq, g_wk, g_wv), 'seq')]
    psum x1 -> x0, blocking collectives: 64.7 us -> none  [device_step(): late = lax.psum((g_norm_attn, g_wq, g_wk, g_wv), 'seq')]
    pallas_call x4 -> x3, Pallas kernels: 214 us -> 235 us  [the longest x1 108 us: attention_bwd(): pl.pallas_call(functools.partial(bwd_kernel, n, forms), out_shape=tuple(o...]
    slice x0 -> x5, local copies, waits for them, and re-layouts: none -> 8.47 us  [the longest x3 4.3 us: device_step(): g_wq, g_wk, g_wv = (late[0], late[1], late[2])]
    unnamed x99 -> x65, local copies, waits for them, and re-layouts: 15.8 us -> 8.76 us
  transfers between devices with their start and end apart: 1 -> 0, of which waited for: 1 -> 0; matrix products, arithmetic and copies ran while one was open for 1% -> 0% of each run, Pallas kernels for 0% -> 0%
where the time goes in v2:
time: 343 us; the launch traced here: 342 us
  Pallas kernels  288 us (84%)
  local copies, waits for them, and re-layouts  24.6 us (7%)
  matrix products  21.4 us (6%)
  other arithmetic  6.7 us (2%)
    pallas_call x1, Pallas kernels, attention_bwd(): pl.pallas_call(functools.partial(bwd_kernel, n, forms), out_shape=tuple(o...  108 us
    pallas_call x1, Pallas kernels, attention_fwd(): pl.pallas_call(functools.partial(fwd_kernel, n), out_shape=(jax.ShapeDtyp...  90 us
    pallas_call x2, Pallas kernels, all_gather_t(): pl.pallas_call(functools.partial(gather_kernel, n, has), out_shape=tuple(...  52.9 us
    pallas_call x1, Pallas kernels, all_reduce_late(): pl.pallas_call(functools.partial(reduce_kernel, n, form), out_shape=(jax....  36.4 us
    unnamed x65, local copies, waits for them, and re-layouts  8.76 us

profile of v2, /device:TPU:1, one launch (start us, length us, event | category | flops | bytes accessed | tf_op | source)
XLA Modules:
  0.0 342.2 jit_solution(1233141257806187538)
XLA Ops:
  0.7 1.9 convolution_convert_fusion.1
  2.6 0.4 fusion.57
  3.0 0.5 copy-done.2
  4.4 0.2 fusion.16
  4.6 0.2 fusion.17
  4.9 0.2 fusion.18
  5.1 0.2 fusion.19
  5.3 0.2 fusion.20
  5.6 0.2 copy-done.1
  5.8 0.6 convolution_convert_fusion
  6.5 0.4 fusion.56
  6.9 0.5 copy-done.3
  7.4 0.3 copy-done.4
  7.6 0.1 fusion.5
  7.8 0.2 fusion.7
  8.0 0.2 fusion.9
  8.2 0.2 fusion.11
  8.4 0.2 fusion.13
  8.6 0.4 fusion.15
  9.2 0.2 fusion.3
  9.4 1.0 copy.95
  10.5 0.2 copy-done.28
  10.7 27.7 %gather_q.1.q_ref = bf16[3,128,4096]{2,1,0:T(8,128)(2,1)} custom-call(bf16[3,32,128]{2,1,0:T(8,128)(2,1)} %bitcast.179), custom_call_target="tpu_custom_call" | custom-call | tf_op jit(solution)/shard_map/gather_q/pallas_call | solution.py:153
  38.4 2.3 copy.50
  40.7 90.0 %attention_fwd.1 = (f32[3,32,128]{2,1,0:T(8,128)}, f32[3,32,128]{2,1,0:T(8,128)}) custom-call(bf16[3,128,4096]{2,1,0:T(8,128)(2,1)} %gather_q.1.q_ref, bf16[6,1024,128]{2,1,0:T(8,128)(2,1)} %copy-done.28, bf16[3,128,1024]{2,1,0:T(8,128)(2,1)} %bitcast.173), custom_call_target="tpu_custom_call" | custom-call | flops 6442450944 | bytes 12000000 | tf_op jit(solution)/shard_map/attention_fwd/pallas_call | solution.py:516
  130.7 1.3 multiply_reduce_fusion.2
  132.2 1.6 fusion.60
  133.8 0.3 fusion.61
  134.1 1.9 fusion.26.refs_2_
  136.0 0.5 multiply_convert_fusion.1
  136.5 1.9 fusion.64.refs_1_
  138.4 1.9 fusion.63.refs_0_
  140.3 0.5 fusion.62
  140.8 0.6 multiply_reduce_fusion
  141.6 0.2 bitcast_multiply_fusion
  141.8 0.4 copy-done.21
  142.2 0.1 reshape.124
  142.3 0.2 reduce_sum.65
  142.6 0.7 maximum_maximum_fusion.refs_1_
  143.3 0.6 copy.94
  143.9 25.2 %gather_stats.1 = (bf16[3,128,4096]{2,1,0:T(8,128)(2,1)}, f32[3,8,4096]{2,1,0:T(8,128)}) custom-call(bf16[3,32,128]{2,1,0:T(8,128)(2,1)} %bitcast.180, f32[3,32,128]{2,1,0:T(8,128)} %maximum_maximum_fusion.refs_1_), custom_call_target="tpu_custom_call" | custom-call | tf_op jit(solution)/shard_map/gather_stats/pallas_call | solution.py:153
  169.1 2.3 copy.55
  171.4 108.4 %attention_bwd.1 = (f32[3,32,128]{2,1,0:T(8,128)}, bf16[1024,384]{1,0:T(8,128)(2,1)}, bf16[1024,384]{1,0:T(8,128)(2,1)}, f32[384,1536]{1,0:T(8,128)}, f32[384,1536]{1,0:T(8,128)}, /*index=5*/f32[1536,384]{1,0:T(8,128)}) custom-call(bf16[3,128,4096]{2,1,0:T(8,128)(2,1)} %gather_q.1.q_ref, bf16[3,128,4096]{2,1,0:T(8,128)(2,1)} %get-tuple-element.25.do_ref, ...), custom_call_target="tpu_custom_call" | custom-call | flops 16106127360 | bytes 20000000 | tf_op jit(solution)/shard_map/attention_bwd/pallas_call | solution.py:600
  279.8 2.0 fusion.30
  281.9 0.7 maximum_maximum_fusion.1.small
  282.6 1.1 convolution_bitcast_fusion
  283.7 1.2 convolution_bitcast_fusion.1
  284.9 0.6 convolution_bitcast_fusion.2
  285.5 0.6 convolution_bitcast_fusion.3
  286.1 1.6 pad_maximum_fusion.src
  287.7 36.4 %reduce_late.1 = (f32[4,384,384]{2,1,0:T(8,128)}, f32[8,384]{1,0:T(8,128)}) custom-call(f32[4,384,384]{2,1,0:T(8,128)} %pad_maximum_fusion.src, f32[8,384]{1,0:T(8,128)} %maximum_maximum_fusion.1.small), custom_call_target="tpu_custom_call" | custom-call | tf_op jit(solution)/shard_map/reduce_late/pallas_call | solution.py:645
  324.1 2.8 fusion.55
  326.8 2.2 copy.59
  329.0 1.0 copy.60
  330.1 1.0 copy.61
  331.1 1.4 slice_reduce_fusion
  332.6 0.6 fusion.65
  333.3 1.8 convolution_add_fusion
  335.0 0.7 fusion.32
  335.8 1.4 copy.110
  337.2 1.1 copy-done.12
  338.3 1.4 copy.111
  339.7 1.1 copy-done.11
  340.8 1.4 copy.112
  (75 shorter events, 1.0 us)
Async XLA Ops:
  0.6 135.4 %copy-start = (bf16[1536,384]{1,0:T(8,128)(2,1)S(1)}, bf16[1536,384]{1,0:T(8,128)(2,1)}, u32[]{:S(2)}) copy-start(bf16[1536,384]{1,0:T(8,128)(2,1)} %param.25) | copy-start | bytes 3538948
  2.6 0.9 copy-start.2
  4.6 1.1 copy-start.1
  4.6 1.2 copy-start.14
  6.5 0.9 copy-start.3
  6.5 1.1 copy-start.4
  8.2 0.9 copy-start.19
  8.2 1.0 copy-start.29
  8.2 1.0 copy-start.17
  9.0 1.5 copy-start.27
  9.0 1.7 copy-start.28
  40.7 90.0 %copy-start.20 = (bf16[32,384]{1,0:T(8,128)(2,1)S(1)}, bf16[32,384]{1,0:T(8,128)(2,1)}, u32[]{:S(2)}) copy-start(bf16[32,384]{1,0:T(8,128)(2,1)} %param.13) | copy-start | bytes 73732
  40.7 91.4 %copy-start.30 = (bf16[384]{0:T(512)(128)(2,1)S(1)}, bf16[384]{0:T(512)(128)(2,1)}, u32[]{:S(2)}) copy-start(bf16[384]{0:T(512)(128)(2,1)} %param.22) | copy-start | bytes 2308
  130.7 3.1 copy-start.6
  130.7 3.4 copy-start.25
  138.4 2.4 copy-start.5
  140.3 1.2 copy-start.16
  140.3 1.2 copy-start.23
  140.8 1.8 copy-start.26
  141.6 0.6 copy-start.21
  279.8 5.1 %copy-start.7 = (bf16[1024,384]{1,0:T(8,128)(2,1)S(1)}, bf16[1024,384]{1,0:T(8,128)(2,1)}, u32[]{:S(2)}) copy-start(bf16[1024,384]{1,0:T(8,128)(2,1)} %get-tuple-element.29) | copy-start | bytes 2359300
  283.7 1.9 copy-start.9
  326.8 5.7 %copy-start.10 = (bf16[1024,384]{1,0:T(8,128)(2,1)S(1)}, bf16[1024,384]{1,0:T(8,128)(2,1)}, u32[]{:S(2)}) copy-start(bf16[1024,384]{1,0:T(8,128)(2,1)} %get-tuple-element.28) | copy-start | bytes 2359300
  326.8 5.7 %copy-start.18 = (bf16[384,6,64]{0,2,1:T(8,128)(2,1)S(1)}, bf16[384,6,64]{0,2,1:T(8,128)(2,1)}, u32[]{:S(2)}) copy-start(bf16[384,6,64]{0,2,1:T(8,128)(2,1)} %param.19) | copy-start | bytes 884740
  331.1 2.1 copy-start.8
  331.1 2.1 copy-start.15
  333.2 1.8 copy-start.22
  333.2 1.8 copy-start.24
  333.2 2.5 copy-start.13
  335.8 2.5 copy-start.12
  338.3 2.5 copy-start.11

commit v3 on v2

--- a/solution.py
+++ b/solution.py
@@ -45,6 +45,13 @@
     def other_core(self):
         return self.me + 1 - 2 * self.core
 
+    def quarter(self):
+        return self.me // (self.n ** 3 // 2)
+
+    def mate(self, q):
+        size = self.n ** 3 // 2
+        return q * size + lax.rem(self.me, size)
+
     def to(self, k):
         return {"seq": k}
 
@@ -54,7 +61,12 @@
             for k in range(1, self.n):
                 pl.semaphore_signal(sem, inc=1, device_id=self.to(self.along(axis, k)), device_id_type=MESH)
         pl.semaphore_signal(sem, inc=1, device_id=self.to(self.other_core()), device_id_type=MESH)
-        pl.semaphore_wait(sem, 3 * (self.n - 1) + 1)
+        extra = 0
+        if self.n < 4:
+            for k in range(1, 4):
+                pl.semaphore_signal(sem, inc=1, device_id=self.to(self.mate(lax.rem(self.quarter() + k, 4))), device_id_type=MESH)
+            extra = 3
+        pl.semaphore_wait(sem, 3 * (self.n - 1) + 1 + extra)
 
 
 def rcopy(src, dst, send, recv, device):
@@ -66,97 +78,206 @@
     return pl.ds(pl.multiple_of(start, TILE), size)
 
 
-def gather_kernel(n, has_stats, *refs):
-    if has_stats:
-        x_ref, s_ref, out_ref, sout_ref, rows, srows, send, recv, ssend, srecv, csend, crecv = refs
-    else:
-        x_ref, out_ref, rows, send, recv, csend, crecv = refs
-    at = Place(n)
-    r = TILE // n
-    at.barrier()
-    pairs = [(0, x_ref, rows, out_ref)]
-    if has_stats:
-        pairs.append((1, s_ref, srows, sout_ref))
-
-    def sems(kind):
-        return (send, recv) if kind == 0 else (ssend, srecv)
-
-    copies = {}
-    for p in range(PARTS):
-        a3 = ORDERS[p][2]
-        mine = pl.ds(pl.multiple_of(at.coord[a3] * r, r), r)
-        for kind, src, dst, _ in pairs:
-            snd, rcv = sems(kind)
+def rows_of(start, size):
+    return pl.ds(pl.multiple_of(start, 8), size)
+
+
+class Gather:
+    def __init__(self, n, at, src, full, bufs):
+        self.n, self.at, self.src, self.full = n, at, src, full
+        self.rows, self.send, self.recv, self.rsend, self.rrecv, self.csend, self.crecv = bufs
+        self.copies = {}
+        self.split = full.shape[1] == TILE and n == 4
+
+    @staticmethod
+    def scratch(n, dtype):
+        sem = pltpu.SemaphoreType.DMA
+        return [pltpu.VMEM((PARTS, TILE, TILE), dtype), sem((3, PARTS, n - 1)), sem((3, PARTS, n - 1)),
+                sem((3, PARTS, 2)), sem((3, PARTS, 2)), sem((PARTS,)), sem((PARTS,))]
+
+    def begin(self):
+        n, at = self.n, self.at
+        r = TILE // n
+        for p in range(PARTS):
+            a3 = ORDERS[p][2]
+            mine = rows_of(at.coord[a3] * r, r)
             for k in range(1, n):
-                c = rcopy(src.at[p], dst.at[p, mine, :], snd.at[0, p, k - 1], rcv.at[0, p, k - 1], at.along(a3, k))
+                c = rcopy(self.src.at[p], self.rows.at[p, mine, :], self.send.at[0, p, k - 1], self.recv.at[0, p, k - 1], at.along(a3, k))
                 c.start()
-                copies[0, p, kind, k] = c
-            dst[p, mine, :] = src[p]
-    for p in range(PARTS):
+                self.copies[0, p, k] = c
+            self.rows[p, mine, :] = self.src[p]
+
+    def turn(self):
+        at, n = self.at, self.n
+        for p in range(PARTS):
+            a1, a2, _ = ORDERS[p]
+            for k in range(1, n):
+                self.copies[0, p, k].wait()
+            block = self.rows[p].astype(F32).T
+            base = ((at.core * n + at.coord[a1]) * n + at.coord[a2]) * TILE
+            self.full[p, :, lanes(base, TILE)] = block[:self.full.shape[1]].astype(self.full.dtype)
+
+    def place(self, stage, p, back):
+        at, n = self.at, self.n
         a1, a2, _ = ORDERS[p]
-        base = ((at.core * n + at.coord[a1]) * n + at.coord[a2]) * TILE
-        for kind, _, dst, full in pairs:
+        if stage == 1:
+            spot = lax.rem(at.coord[a2] + n - back, n)
+            return a2, lanes(((at.core * n + at.coord[a1]) * n + spot) * TILE, TILE)
+        spot = lax.rem(at.coord[a1] + n - back, n)
+        return a1, lanes((at.core * n + spot) * n * TILE, n * TILE)
+
+    def spread(self, stage):
+        n, at = self.n, self.at
+        for p in range(PARTS):
+            axis, cols = self.place(stage, p, 0)
+            view = self.full.at[p, :, cols]
             for k in range(1, n):
-                copies[0, p, kind, k].wait()
-            block = dst[p].astype(F32).T
-            full[p, :, lanes(base, TILE)] = block[:full.shape[1]].astype(full.dtype)
-    for stage in (1, 2):
-        for p in range(PARTS):
-            a1, a2, _ = ORDERS[p]
-            if stage == 1:
-                axis, width = a2, TILE
-                base = ((at.core * n + at.coord[a1]) * n + at.coord[a2]) * TILE
-            else:
-                axis, width = a1, TILE * n
-                base = (at.core * n + at.coord[a1]) * n * TILE
-                for kind, *_ in pairs:
-                    for k in range(1, n):
-                        copies[1, p, kind, k].wait()
-            for kind, _, _, full in pairs:
-                snd, rcv = sems(kind)
-                view = full.at[p, :, lanes(base, width)]
+                if self.split and k == 2:
+                    continue
+                c = rcopy(view, view, self.send.at[stage, p, k - 1], self.recv.at[stage, p, k - 1], at.along(axis, k))
+                c.start()
+                self.copies[stage, p, k] = c
+
+    def settle(self, stage):
+        n, at = self.n, self.at
+        half = TILE // 2
+        if not self.split:
+            for p in range(PARTS):
                 for k in range(1, n):
-                    c = rcopy(view, view, snd.at[stage, p, k - 1], rcv.at[stage, p, k - 1], at.along(axis, k))
-                    c.start()
-                    copies[stage, p, kind, k] = c
+                    self.copies[stage, p, k].wait()
+            return
+        relays = []
+        for p in range(PARTS):
+            for k, i in ((1, 0), (3, 1)):
+                self.copies[stage, p, k].wait_recv()
+                axis, cols = self.place(stage, p, k)
+                view = self.full.at[p, half * i:half * (i + 1), cols]
+                c = rcopy(view, view, self.rsend.at[stage, p, i], self.rrecv.at[stage, p, i], at.along(axis, k))
+                c.start()
+                relays.append(c)
+        for p in range(PARTS):
+            for k in (1, 3):
+                self.copies[stage, p, k].wait_send()
+        for c in relays:
+            c.wait()
+
+    def swap(self):
+        n, at = self.n, self.at
+        width = n * n * TILE
+        out = []
+        for p in range(PARTS):
+            view = self.full.at[p, :, lanes(at.core * width, width)]
+            c = rcopy(view, view, self.csend.at[p], self.crecv.at[p], at.other_core())
+            c.start()
+            out.append(c)
+        return out
+
+
+GATHER_REFS = 7
+
+
+def run_gathers(gathers, between=None):
+    for g in gathers:
+        g.begin()
+    for g in gathers:
+        g.turn()
+        g.spread(1)
+    for g in gathers:
+        g.settle(1)
+        g.spread(2)
+    if between is not None:
+        between()
     final = []
-    for p in range(PARTS):
-        for kind, _, _, full in pairs:
-            for k in range(1, n):
-                copies[2, p, kind, k].wait()
-            width = n * n * TILE
-            view = full.at[p, :, lanes(at.core * width, width)]
-            c = rcopy(view, view, csend.at[kind, p], crecv.at[kind, p], at.other_core())
-            c.start()
-            final.append(c)
+    for g in gathers:
+        g.settle(2)
+        final += g.swap()
     for c in final:
         c.wait()
 
 
-def all_gather_t(n, cid, rows, stats=None):
+def prepare_kernel(n, x_ref, mem_ref, wk_ref, wv_ref, auxk_ref, auxv_ref,
+                   q_ref, keep_ref, k_ref, v_ref, kt_ref, vt_ref, *bufs):
+    gbufs, (msend, mrecv) = bufs[:GATHER_REFS], bufs[GATHER_REFS:]
+    at = Place(n)
+    at.barrier()
+    keep = keep_ref.shape[0]
+    piece = keep // 3
+    quarter = at.quarter()
+    donor = quarter < 3
+
+    def donate(q):
+        return rcopy(mem_ref.at[pl.ds(keep, piece), :], keep_ref.at[pl.ds(q * piece, piece), :], msend, mrecv.at[q], at.mate(3))
+
+    for q in range(3):
+        @pl.when(quarter == q)
+        def _(q=q):
+            donate(q).start()
+
+    def project():
+        @pl.when(donor)
+        def _():
+            keep_ref[...] = mem_ref[0:keep, :]
+
+        @pl.when(quarter == 3)
+        def _():
+            for q in range(3):
+                donate(q).wait_recv()
+
+        low = lax.broadcasted_iota(jnp.int32, (piece, TILE), 1) < TILE // 2
+
+        def some(i, _):
+            rows = pl.ds(pl.multiple_of(i * piece, piece), piece)
+            m = keep_ref[rows, :]
+            for w_ref, aux_ref, a_ref, t_ref in ((wk_ref, auxk_ref, k_ref, kt_ref), (wv_ref, auxv_ref, v_ref, vt_ref)):
+                aux = aux_ref[rows, :].astype(F32)
+                for p in range(PARTS):
+                    b = jnp.dot(m, w_ref[:, p * TILE:(p + 1) * TILE], preferred_element_type=F32).astype(BF16).astype(F32)
+                    a_ref[2 * p, rows, :] = jnp.where(low, b, aux).astype(BF16)
+                    a_ref[2 * p + 1, rows, :] = jnp.where(low, aux, b).astype(BF16)
+                    t_ref[p, :, rows] = b.T.astype(BF16)
+            return 0
+
+        for i in range(3):
+            some(i, 0)
+
+    run_gathers([Gather(n, at, x_ref, q_ref, gbufs)], project)
+    for q in range(3):
+        @pl.when(quarter == q)
+        def _(q=q):
+            donate(q).wait_send()
+
+
+def prepare(n, cid, rows, memory, wk, wv, aux_k, aux_v):
     total = 2 * n * n * TILE
-    r = TILE // n
-    has = stats is not None
+    keep, dim = aux_k.shape[0], memory.shape[1]
     vm = pl.BlockSpec(memory_space=pltpu.VMEM)
-    outs = [jax.ShapeDtypeStruct((PARTS, TILE, total), BF16)]
-    scratch = [pltpu.VMEM((PARTS, TILE, TILE), BF16)]
-    args = [rows]
     sem = pltpu.SemaphoreType.DMA
-    if has:
-        outs.append(jax.ShapeDtypeStruct((PARTS, 8, total), F32))
-        scratch.append(pltpu.VMEM((PARTS, TILE, TILE), F32))
-        args.append(stats)
-    scratch += [sem((3, PARTS, n - 1)), sem((3, PARTS, n - 1))]
-    if has:
-        scratch += [sem((3, PARTS, n - 1)), sem((3, PARTS, n - 1))]
-    scratch += [sem((2, PARTS)), sem((2, PARTS))]
-    res = pl.pallas_call(
-        functools.partial(gather_kernel, n, has),
-        out_shape=tuple(outs), in_specs=[vm] * len(args), out_specs=(vm,) * len(outs),
-        scratch_shapes=scratch, name="gather_stats" if has else "gather_q",
+    shape = jax.ShapeDtypeStruct
+    outs = (shape((PARTS, TILE, total), BF16), shape((keep, dim), BF16), shape((2 * PARTS, keep, TILE), BF16),
+            shape((2 * PARTS, keep, TILE), BF16), shape((PARTS, TILE, keep), BF16), shape((PARTS, TILE, keep), BF16))
+    return pl.pallas_call(
+        functools.partial(prepare_kernel, n), out_shape=outs, in_specs=[vm] * 6, out_specs=(vm,) * 6,
+        scratch_shapes=Gather.scratch(n, BF16) + [sem(()), sem((3,))], name="prepare",
         compiler_params=pltpu.CompilerParams(collective_id=cid, has_side_effects=True, vmem_limit_bytes=VMEM_LIMIT),
-    )(*args)
-    return res if has else res[0]
+    )(rows, memory, wk, wv, aux_k, aux_v)
+
+
+def gather_kernel(n, x_ref, s_ref, out_ref, sout_ref, *bufs):
+    at = Place(n)
+    at.barrier()
+    run_gathers([Gather(n, at, s_ref, sout_ref, bufs[GATHER_REFS:]), Gather(n, at, x_ref, out_ref, bufs[:GATHER_REFS])])
+
+
+def all_gather_t(n, cid, rows, stats):
+    total = 2 * n * n * TILE
+    vm = pl.BlockSpec(memory_space=pltpu.VMEM)
+    return pl.pallas_call(
+        functools.partial(gather_kernel, n),
+        out_shape=(jax.ShapeDtypeStruct((PARTS, TILE, total), BF16), jax.ShapeDtypeStruct((PARTS, 8, total), F32)),
+        in_specs=[vm] * 2, out_specs=(vm,) * 2,
+        scratch_shapes=Gather.scratch(n, BF16) + Gather.scratch(n, F32), name="gather_stats",
+        compiler_params=pltpu.CompilerParams(collective_id=cid, has_side_effects=True, vmem_limit_bytes=VMEM_LIMIT),
+    )(rows, stats)
 
 
 def merge(blocks, rows_axis):
@@ -283,10 +404,6 @@
                 st_ref[p] = jnp.where(col == 0, m0 + jnp.log(l0), jnp.where(col == 1, m1 + jnp.log(l1), 0.0))
             else:
                 o_ref[p] = functools.reduce(jnp.add, blocks)
-
-
-def rows_of(start, size):
-    return pl.ds(pl.multiple_of(start, 8), size)
 
 
 class Wide:
@@ -435,14 +552,7 @@
     return [hi, mid, lo]
 
 
-def fold_rows(op, v, last):
-    while v.shape[0] > 64:
-        h = v.shape[0] // 2
-        v = op(v[:h], v[h:])
-    return last(v, axis=0, keepdims=True)
-
-
-def blocks_loop(n, scatter, block, events):
+def blocks_loop(n, scatter, blocks, events):
     per = n * TILE // QB
     at = scatter.at
 
@@ -451,10 +561,9 @@
         k = n - 1 - u // 2
         near = lax.rem(u, 2)
         half = jnp.where(near == 1, at.core, 1 - at.core)
-        for p in range(PARTS):
-            inside = scatter.chunk(p, k) * (n * TILE) + lax.rem(t, per) * QB
-            src = pl.multiple_of(half * (n * n * TILE) + inside, QB)
-            block(p, pl.ds(src, QB), near, pl.ds(pl.multiple_of(inside, QB), QB))
+        inside = [scatter.chunk(p, k) * (n * TILE) + lax.rem(t, per) * QB for p in range(PARTS)]
+        srcs = [pl.ds(pl.multiple_of(half * (n * n * TILE) + i, QB), QB) for i in inside]
+        blocks(srcs, near, [pl.ds(pl.multiple_of(i, QB), QB) for i in inside])
         last = lax.rem(t, per) == per - 1
 
         @pl.when(last & (near == 0))
@@ -484,28 +593,64 @@
         scatter.far[p, row, col] = val
 
 
-def fwd_kernel(n, q_ref, k_ref, vt_ref, o_ref, st_ref, *bufs):
+def beside(j, block, other):
+    return jnp.concatenate([block, other] if j == 0 else [other, block], axis=0)
+
+
+def shrink(op, v, rows):
+    while v.shape[0] > rows:
+        h = v.shape[0] // 2
+        v = op(v[:h], v[h:])
+    return v
+
+
+KC = 256
+
+
+def fwd_kernel(n, q_ref, k_ref, vt_ref, o_ref, st_ref, s_buf, *bufs):
     half = TILE // 2
+    keys = k_ref.shape[1]
+    kc = min(KC, keys // 3)
+    chunks = keys // kc
     one = jnp.ones((1, QB), F32)
     aux = aux_rows([one], QB)
     at = Place(n)
     at.barrier()
     scatter = Scatter(n, at, True, bufs)
 
-    def block(p, src, near, dst):
-        maxes, sums, outs = [], [], []
-        for j in range(2):
-            qa = jnp.concatenate([q_ref[p, half * j:half * (j + 1), src], aux], axis=0)
-            s = jnp.dot(k_ref[2 * p + j], qa, preferred_element_type=F32)
-            m = fold_rows(jnp.maximum, s, jnp.max)
-            e = jnp.exp(s - m)
-            sums.append(fold_rows(jnp.add, e, jnp.sum))
-            outs.append(jnp.dot(vt_ref[p, half * j:half * (j + 1), :], e.astype(BF16), preferred_element_type=F32))
-            maxes.append(m)
-        val = jnp.concatenate(outs + maxes + sums + [jnp.zeros((4, QB), F32)], axis=0)
-        put(scatter, near, p, slice(None), dst, val)
-
-    blocks_loop(n, scatter, block, [])
+    def blocks(srcs, near, dsts):
+        heads = [(p, j) for p in range(PARTS) for j in range(2)]
+
+        def score(i, c, run):
+            p, j = heads[i]
+            qa = beside(j, q_ref[p, half * j:half * (j + 1), srcs[p]], aux)
+            s = jnp.dot(k_ref[i, c * kc:(c + 1) * kc, :], qa, preferred_element_type=F32)
+            s_buf[i % 2, c * kc:(c + 1) * kc, :] = s
+            top = shrink(jnp.maximum, s, 16)
+            return top if run is None else jnp.maximum(run, top)
+
+        run = None
+        for c in range(chunks):
+            run = score(0, c, run)
+        done = []
+        for i, (p, j) in enumerate(heads):
+            m = jnp.max(run, axis=0, keepdims=True)
+            run, total, out = None, None, None
+            for c in range(chunks):
+                if i + 1 < len(heads):
+                    run = score(i + 1, c, run)
+                e = jnp.exp(s_buf[i % 2, c * kc:(c + 1) * kc, :] - m)
+                part = shrink(jnp.add, e, 16)
+                total = part if total is None else total + part
+                o = jnp.dot(vt_ref[p, half * j:half * (j + 1), c * kc:(c + 1) * kc], e.astype(BF16), preferred_element_type=F32)
+                out = o if out is None else out + o
+            done.append((out, m, jnp.sum(total, axis=0, keepdims=True)))
+            if j == 1:
+                (o0, m0, l0), (o1, m1, l1) = done[-2:]
+                val = jnp.concatenate([o0, o1, m0, m1, l0, l1, jnp.zeros((4, QB), F32)], axis=0)
+                put(scatter, near, p, slice(None), dsts[p], val)
+
+    blocks_loop(n, scatter, blocks, [])
     scatter.finish(o_ref, st_ref)
 
 
@@ -516,7 +661,7 @@
     return pl.pallas_call(
         functools.partial(fwd_kernel, n), out_shape=(jax.ShapeDtypeStruct((PARTS, r, TILE), F32),) * 2,
         in_specs=[vm] * 3, out_specs=(vm,) * 2, name="attention_fwd",
-        scratch_shapes=Scatter.scratch(n, TILE + 8, 2 * TILE),
+        scratch_shapes=[pltpu.VMEM((2, keys, QB), F32)] + Scatter.scratch(n, TILE + 8, 2 * TILE),
         cost_estimate=pl.CostEstimate(flops=4 * 384 * total * keys, bytes_accessed=12_000_000, transcendentals=6 * total * keys),
         compiler_params=pltpu.CompilerParams(collective_id=cid, has_side_effects=True, vmem_limit_bytes=VMEM_LIMIT),
     )(q_t, k_aug, v_t)
@@ -525,13 +670,13 @@
 SCATTER_REFS = 12
 
 
-def bwd_kernel(n, forms, q_ref, do_ref, st_ref, k_ref, v_ref, kt_ref, *refs):
+def bwd_kernel(n, forms, q_ref, do_ref, st_ref, k_ref, v_ref, kt_ref, wk_ref, wv_ref, *refs):
     count = len(forms)
     grads, refs = refs[:count], refs[count:]
-    dq_ref, dk_ref, dv_ref = refs[:3]
-    sums, refs = refs[3:3 + count], refs[3 + count:]
-    dk_acc, dv_acc = refs[:2]
-    bufs, refs = refs[2:2 + SCATTER_REFS], refs[2 + SCATTER_REFS:]
+    dq_ref, dk_ref, dv_ref, dm_ref = refs[:4]
+    sums, refs = refs[4:4 + count], refs[4 + count:]
+    dk_acc, dv_acc, dm_buf, msend, mrecv = refs[:5]
+    bufs, refs = refs[5:5 + SCATTER_REFS], refs[5 + SCATTER_REFS:]
     half = TILE // 2
     one = jnp.ones((1, QB), F32)
     zero = jnp.zeros((1, QB), F32)
@@ -558,16 +703,15 @@
             doh = do_ref[p, half * j:half * (j + 1), src]
             lse = st_ref[p, j:j + 1, src]
             delta = st_ref[p, 2 + j:3 + j, src]
-            qa = jnp.concatenate([qh, aux_rows([one] + split3(-lse), QB)], axis=0)
-            da = jnp.concatenate([doh, aux_rows([zero] + split3(-delta), QB)], axis=0)
+            qa = beside(j, qh, aux_rows([one] + split3(-lse), QB))
+            da = beside(j, doh, aux_rows([zero] + split3(-delta), QB))
             e = jnp.exp(jnp.dot(k_ref[2 * p + j], qa, preferred_element_type=F32))
             dp = jnp.dot(v_ref[2 * p + j], da, preferred_element_type=F32)
             ds = (e * dp).astype(BF16)
             probs.append(e.astype(BF16))
             dscores.append(ds)
-            order = (lambda a: [a, blank]) if j == 0 else (lambda a: [blank, a])
-            dos.append(jnp.concatenate(order(doh), axis=0))
-            qs.append(jnp.concatenate(order(qh), axis=0))
+            dos.append(beside(j, doh, blank))
+            qs.append(beside(j, qh, blank))
             dqs.append(0.125 * jnp.dot(kt_ref[p, half * j:half * (j + 1), :], ds, preferred_element_type=F32))
         dv_acc[p] += (lax.dot_general(probs[0], dos[0], nt, preferred_element_type=F32)
                       + lax.dot_general(probs[1], dos[1], nt, preferred_element_type=F32))
@@ -577,15 +721,52 @@
 
     trips = 2 * n * (n * TILE // QB)
     when = [min(w, trips - 1) for w in (1, trips // 2, trips // 2 + 1, trips // 2 + 2, trips // 2 + 3, max(trips // 2 + 3, trips - 2))]
-    blocks_loop(n, scatter, block, [(w, functools.partial(advance, i + 1)) for i, w in enumerate(when)])
+
+    def blocks(srcs, near, dsts):
+        for p in range(PARTS):
+            block(p, srcs[p], near, dsts[p])
+
+    blocks_loop(n, scatter, blocks, [(w, functools.partial(advance, i + 1)) for i, w in enumerate(when)])
     for p in range(PARTS):
         dk_ref[:, p * TILE:(p + 1) * TILE] = dk_acc[p].astype(BF16)
         dv_ref[:, p * TILE:(p + 1) * TILE] = dv_acc[p].astype(BF16)
+
+    keep = dk_ref.shape[0]
+    piece = keep // 3
+    quarter = at.quarter()
+
+    def give_back(q):
+        return rcopy(dm_buf.at[pl.ds(q * piece, piece), :], dm_ref.at[pl.ds(keep, piece), :], msend.at[q], mrecv, at.mate(q))
+
+    for i in range(3):
+        rows = slice(i * piece, (i + 1) * piece)
+        dm_buf[rows, :] = (lax.dot_general(dk_ref[rows, :], wk_ref[...], nt, preferred_element_type=F32)
+                           + lax.dot_general(dv_ref[rows, :], wv_ref[...], nt, preferred_element_type=F32))
+
+    @pl.when(quarter == 3)
+    def _():
+        for q in range(3):
+            give_back(q).start()
+        dm_ref[...] = jnp.zeros_like(dm_ref)
+
+    @pl.when(quarter < 3)
+    def _():
+        dm_ref[0:keep, :] = dm_buf[...]
+
     scatter.finish(dq_ref)
     advance(7)
 
-
-def attention_bwd(n, cid, q_t, do_t, stats, k_aug, v_aug, k_t, wide, tall):
+    @pl.when(quarter == 3)
+    def _():
+        for q in range(3):
+            give_back(q).wait_send()
+
+    @pl.when(quarter < 3)
+    def _():
+        give_back(0).wait_recv()
+
+
+def attention_bwd(n, cid, m_rows, q_t, do_t, stats, k_aug, v_aug, k_t, wk, wv, wide, tall):
     total, keys = q_t.shape[2], k_aug.shape[1]
     r = TILE // n
     forms = [Wide(a.shape, n) for a in wide] + [Tall(a.shape, n) for a in tall]
@@ -593,17 +774,18 @@
     vm = pl.BlockSpec(memory_space=pltpu.VMEM)
     flat = jax.ShapeDtypeStruct((keys, PARTS * TILE), BF16)
     acc = pltpu.VMEM((PARTS, keys, TILE), F32)
-    outs = [jax.ShapeDtypeStruct((PARTS, r, TILE), F32), flat, flat] + [jax.ShapeDtypeStruct(a.shape, F32) for a in grads]
-    scratch = [acc, acc] + Scatter.scratch(n, TILE, TILE)
+    sem = pltpu.SemaphoreType.DMA
+    outs = [jax.ShapeDtypeStruct((PARTS, r, TILE), F32), flat, flat, jax.ShapeDtypeStruct((m_rows, wk.shape[0]), F32)] + [jax.ShapeDtypeStruct(a.shape, F32) for a in grads]
+    scratch = [acc, acc, pltpu.VMEM((keys, wk.shape[0]), F32), sem((3,)), sem(())] + Scatter.scratch(n, TILE, TILE)
     for form in forms:
         scratch += Reduce.scratch(n, form)
     return pl.pallas_call(
         functools.partial(bwd_kernel, n, forms), out_shape=tuple(outs),
-        in_specs=[vm] * 6 + [pl.BlockSpec(memory_space=pl.ANY)] * len(grads), out_specs=(vm,) * len(outs), name="attention_bwd",
+        in_specs=[vm] * 8 + [pl.BlockSpec(memory_space=pl.ANY)] * len(grads), out_specs=(vm,) * len(outs), name="attention_bwd",
         scratch_shapes=scratch,
         cost_estimate=pl.CostEstimate(flops=10 * 384 * total * keys, bytes_accessed=20_000_000, transcendentals=6 * total * keys),
         compiler_params=pltpu.CompilerParams(collective_id=cid, has_side_effects=True, vmem_limit_bytes=VMEM_LIMIT),
-    )(q_t, do_t, stats, k_aug, v_aug, k_t, *grads)
+    )(q_t, do_t, stats, k_aug, v_aug, k_t, wk, wv, *grads)
 
 
 def reduce_kernel(n, form, src, small, out, small_out, slots, pair, ssend, srecv, *bufs):
@@ -674,29 +856,23 @@
         wide = heads * head_dim
         wq, wk, wv = (w.reshape(model_dim, wide) for w in (wq_cross, wk_cross, wv_cross))
         wo = wo_cross.reshape(wide, model_dim)
-        mem_pos = lax.axis_index('seq') * m_rows + jnp.arange(m_rows)
-        bias = jnp.where(mem_pos < mem_len[0], 0.0, NEG).astype(BF16)
+        keep, piece, size = m_rows * 3 // 4, m_rows // 4, group // 4
+        me = lax.axis_index('seq')
+        slot = jnp.arange(keep)
+        own_pos = me * m_rows + slot
+        given_pos = ((slot // piece) * size + me % size) * m_rows + keep + slot % piece
+        mem_pos = jnp.where(me // size == 3, given_pos, own_pos)
+        bias = jnp.where(mem_pos < mem_len[0], 0.0, NEG)[:, None]
+        lane = jnp.arange(TILE)[None, :] % head_dim
+        flag = jnp.where((lane >= 1) & (lane <= 3), 1.0, 0.0)
+        aux_k = jnp.where(lane == 0, bias, flag).astype(BF16)
+        aux_v = jnp.broadcast_to(flag, aux_k.shape).astype(BF16)
 
         x_in = dec_in.astype(F32)
         normed_f, norm_pull = jax.vjp(rms_norm, x_in, norm_attn.astype(F32))
         normed = normed_f.astype(BF16)
         local_query = jnp.dot(normed, wq, preferred_element_type=F32).astype(BF16) * jnp.asarray(head_dim ** -0.5, BF16)
-        q_t = all_gather_t(n, 0, by_part(local_query))
-
-        mem_keys = jnp.dot(memory, wk, preferred_element_type=F32).astype(BF16)
-        mem_vals = jnp.dot(memory, wv, preferred_element_type=F32).astype(BF16)
-        k_t = mem_keys.T.reshape(PARTS, TILE, m_rows)
-        v_t = mem_vals.T.reshape(PARTS, TILE, m_rows)
-        ones = jnp.ones((m_rows, 3), BF16)
-        aux_k = jnp.concatenate([bias[:, None], ones, jnp.zeros((m_rows, 60), BF16)], axis=1)
-        aux_v = jnp.concatenate([jnp.zeros((m_rows, 1), BF16), ones, jnp.zeros((m_rows, 60), BF16)], axis=1)
-
-        def augment(a, aux):
-            return jnp.stack([jnp.concatenate([a[:, head_dim * h:head_dim * (h + 1)], aux], axis=1) for h in range(heads)])
-
-        k_aug = augment(mem_keys, aux_k)
-        v_aug = augment(mem_vals, aux_v)
-
+        q_t, kept, k_aug, v_aug, k_t, v_t = prepare(n, 0, by_part(local_query), memory, wk, wv, aux_k, aux_v)
         out_parts, lse = attention_fwd(n, 1, q_t, k_aug, v_t)
         attended_f = by_row(out_parts)
 
@@ -730,18 +906,16 @@
         stats_in = jnp.concatenate([lse[:, :, 0:2], delta, jnp.zeros((PARTS, q_rows, TILE - 4), F32)], axis=2)
         do_t, stats = all_gather_t(n, 2, by_part(grad_attended.astype(BF16)), stats_in)
 
-        dq_parts, dk_b, dv_b, g_gate, g_up, g_down = attention_bwd(
-            n, 3, q_t, do_t, stats, k_aug, v_aug, k_t, (g_gate, g_up), (g_down,))
+        dq_parts, dk_b, dv_b, g_mem, g_gate, g_up, g_down = attention_bwd(
+            n, 3, m_rows, q_t, do_t, stats, k_aug, v_aug, k_t, wk, wv, (g_gate, g_up), (g_down,))
         grad_query_b = by_row(dq_parts).astype(BF16)
 
         g_wq = jnp.einsum('td,te->de', normed, grad_query_b, preferred_element_type=F32)
         grad_normed = jnp.einsum('te,de->td', grad_query_b, wq, preferred_element_type=F32)
         grad_x_norm, g_norm_attn = norm_pull(grad_normed)
         g_dec = grad_hidden + grad_x_norm
-        g_wk = jnp.einsum('td,te->de', memory, dk_b, preferred_element_type=F32)
-        g_wv = jnp.einsum('td,te->de', memory, dv_b, preferred_element_type=F32)
-        g_mem = (jnp.einsum('te,de->td', dk_b, wk, preferred_element_type=F32)
-                 + jnp.einsum('te,de->td', dv_b, wv, preferred_element_type=F32))
+        g_wk = jnp.einsum('td,te->de', kept, dk_b, preferred_element_type=F32)
+        g_wv = jnp.einsum('td,te->de', kept, dv_b, preferred_element_type=F32)
         small = jnp.concatenate([g_norm_attn[None], g_norm_mlp[None], jnp.zeros((6, model_dim), F32)], axis=0)
         late, small = all_reduce_late(n, 4, jnp.stack([g_wq, g_wk, g_wv, g_wo]), small)
         cube = (model_dim, heads, head_dim)

time: 343 us -> 326 us (0.950)
  Pallas kernels: 288 us -> 276 us
  matrix products: 21.4 us -> 17.9 us
    pallas_call x1, Pallas kernels: 90 us -> 50.3 us  [attention_fwd(): pl.pallas_call(functools.partial(fwd_kernel, n), out_shape=(jax.ShapeDtyp...]
    pallas_call x2, Pallas kernels: 52.9 us -> 73.8 us  [the longest x1 42.3 us: prepare(): pl.pallas_call(functools.partial(prepare_kernel, n), out_shape=outs, in_s...]
    pallas_call x1, Pallas kernels: 108 us -> 114 us  [attention_bwd(): pl.pallas_call(functools.partial(bwd_kernel, n, forms), out_shape=tuple(o...]
    convert_element_type x2 -> x0, local copies, waits for them, and re-layouts: 4.6 us -> none  [the longest x1 2.31 us: device_step(): mem_keys = jnp.dot(memory, wk, preferred_element_type=F32).astype(BF16)]
    reshape x0 -> x2, local copies, waits for them, and re-layouts: none -> 3.69 us  [device_step(): w.reshape(model_dim, wide)]
    unnamed x65 -> x32, local copies, waits for them, and re-layouts: 8.76 us -> 9.18 us
where the time goes in v3:
time: 326 us; the launch traced here: 325 us
  Pallas kernels  276 us (85%)
  local copies, waits for them, and re-layouts  22.3 us (7%)
  matrix products  17.9 us (5%)
  other arithmetic  6.48 us (2%)
    pallas_call x1, Pallas kernels, attention_bwd(): pl.pallas_call(functools.partial(bwd_kernel, n, forms), out_shape=tuple(o...  114 us
    pallas_call x1, Pallas kernels, attention_fwd(): pl.pallas_call(functools.partial(fwd_kernel, n), out_shape=(jax.ShapeDtyp...  50.3 us
    pallas_call x1, Pallas kernels, prepare(): pl.pallas_call(functools.partial(prepare_kernel, n), out_shape=outs, in_s...  42.3 us
    pallas_call x1, Pallas kernels, all_reduce_late(): pl.pallas_call(functools.partial(reduce_kernel, n, form), out_shape=(jax....  38.4 us
    pallas_call x1, Pallas kernels, all_gather_t(): pl.pallas_call(functools.partial(gather_kernel, n), out_shape=(jax.ShapeD...  31.5 us
    unnamed x32, local copies, waits for them, and re-layouts  9.18 us

profile of v3, /device:TPU:1, one launch (start us, length us, event | category | flops | bytes accessed | tf_op | source)
XLA Modules:
  0.0 324.8 jit_solution(14971571689906971137)
XLA Ops:
  0.6 0.0 copy-start
  1.5 0.8 select_convert_fusion.auxk_ref
  2.3 0.8 fusion.15
  3.2 0.7 convert_element_type.69
  3.9 1.2 fusion.3
  5.1 0.6 copy.83
  5.7 1.8 copy.42.wk_ref
  7.6 1.8 copy.43.wv_ref
  9.4 0.7 broadcast_in_dim.72.auxv_ref
  10.1 42.3 %prepare.1 = (bf16[3,128,4096]{2,1,0:T(8,128)(2,1)}, bf16[768,384]{1,0:T(8,128)(2,1)}, bf16[6,768,128]{2,1,0:T(8,128)(2,1)}, bf16[6,768,128]{2,1,0:T(8,128)(2,1)...) custom-call(bf16[3,32,128]{2,1,0:T(8,128)(2,1)} %bitcast.109, bf16[1024,384]{1,0:T(8,128)(2,1)} %mem_ref.1, ...), custom_call_target="tpu_custom_call" | custom-call | tf_op jit(solution)/shard_map/prepare/pallas_call | solution.py:258
  52.4 0.0 copy-start.7
  52.4 0.0 copy-start.8
  52.4 0.0 copy-start.13
  52.4 50.3 %attention_fwd.1 = (f32[3,32,128]{2,1,0:T(8,128)}, f32[3,32,128]{2,1,0:T(8,128)}) custom-call(bf16[3,128,4096]{2,1,0:T(8,128)(2,1)} %get-tuple-element.30.q_ref, bf16[6,768,128]{2,1,0:T(8,128)(2,1)} %get-tuple-element.31.k_ref, bf16[3,128,768]{2,1,0:T(8,128)(2,1)} %get-tuple-element.32.vt_ref), custom_call_target="tpu_custom_call" | custom-call | flops 4831838208 | bytes 12000000 | tf_op jit(solution)/shard_map/attention_fwd/pallas_call | solution.py:661
  102.8 0.0 copy-start.11
  102.8 0.0 copy-done.7
  102.8 0.0 copy-done.8
  102.8 1.1 multiply_reduce_fusion.2
  103.9 0.0 copy-done.13
  103.9 0.1 multiply_convert_fusion.3
  104.0 1.6 fusion.56
  105.6 1.6 fusion.57
  107.1 1.9 fusion.8.refs_2_
  109.1 0.0 copy-done
  109.1 0.5 multiply_convert_fusion.1
  109.6 0.0 copy-start.2
  109.6 1.9 fusion.60.refs_1_
  111.5 1.9 fusion.59.refs_0_
  113.4 0.0 copy-done.2
  113.4 0.5 fusion.58
  113.8 0.0 copy-done.1
  113.9 0.6 multiply_reduce_fusion
  114.5 0.1 fusion.13
  114.6 0.2 bitcast_multiply_fusion
  114.8 0.1 reshape.157
  114.9 0.2 reduce_sum.65
  115.2 0.1 pad.9.clone
  115.3 0.0 copy-done.12
  115.3 0.7 maximum_maximum_fusion.s_ref
  116.0 0.6 copy.82
  116.6 31.5 %gather_stats.1 = (bf16[3,128,4096]{2,1,0:T(8,128)(2,1)}, f32[3,8,4096]{2,1,0:T(8,128)}) custom-call(bf16[3,32,128]{2,1,0:T(8,128)(2,1)} %bitcast.110, f32[3,32,128]{2,1,0:T(8,128)} %maximum_maximum_fusion.s_ref), custom_call_target="tpu_custom_call" | custom-call | tf_op jit(solution)/shard_map/gather_stats/pallas_call | solution.py:274
  148.1 113.9 %attention_bwd.1 = (f32[3,32,128]{2,1,0:T(8,128)}, bf16[768,384]{1,0:T(8,128)(2,1)}, bf16[768,384]{1,0:T(8,128)(2,1)}, f32[1024,384]{1,0:T(8,128)}, f32[384,1536...) custom-call(bf16[3,128,4096]{2,1,0:T(8,128)(2,1)} %get-tuple-element.30.q_ref, ...), custom_call_target="tpu_custom_call" | custom-call | flops 12079595520 | bytes 20000000 | tf_op jit(solution)/shard_map/attention_bwd/pallas_call | solution.py:782
  262.0 1.3 fusion.12
  263.3 0.1 pad.2.clone
  263.4 0.7 maximum_maximum_fusion.1.small
  264.0 1.5 convolution_bitcast_fusion.3
  265.6 1.6 convolution_bitcast_fusion.2
  267.2 0.0 copy-done.10
  267.2 0.3 convolution_bitcast_fusion.1
  267.5 0.3 convolution_bitcast_fusion
  267.8 1.6 pad_maximum_fusion.src
  269.3 38.4 %reduce_late.1 = (f32[4,384,384]{2,1,0:T(8,128)}, f32[8,384]{1,0:T(8,128)}) custom-call(f32[4,384,384]{2,1,0:T(8,128)} %pad_maximum_fusion.src, f32[8,384]{1,0:T(8,128)} %maximum_maximum_fusion.1.small), custom_call_target="tpu_custom_call" | custom-call | tf_op jit(solution)/shard_map/reduce_late/pallas_call | solution.py:827
  307.8 2.6 fusion.53
  310.4 1.0 copy.51
  311.4 1.0 copy.52
  312.5 1.0 copy.53
  313.5 1.5 slice_reduce_fusion
  315.0 0.7 fusion.14
  315.7 2.7 copy.89
  318.4 1.4 copy.90
  319.8 1.1 copy-done.5
  320.9 1.4 copy.91
  322.3 1.1 copy-done.4
  323.4 1.4 copy.92
  (26 shorter events, 0.1 us)
Async XLA Ops:
  0.6 108.4 %copy-start = (bf16[1536,384]{1,0:T(8,128)(2,1)S(1)}, bf16[1536,384]{1,0:T(8,128)(2,1)}, u32[]{:S(2)}) copy-start(bf16[1536,384]{1,0:T(8,128)(2,1)} %param.25) | copy-start | bytes 3538948
  52.4 50.4 %copy-start.7 = (bf16[6,64,384]{2,1,0:T(8,128)(2,1)S(1)}, bf16[6,64,384]{2,1,0:T(8,128)(2,1)}, u32[]{:S(2)}) copy-start(bf16[6,64,384]{2,1,0:T(8,128)(2,1)} %param.21) | copy-start | bytes 884740
  52.4 50.4 %copy-start.8 = (bf16[32,384]{1,0:T(8,128)(2,1)S(1)}, bf16[32,384]{1,0:T(8,128)(2,1)}, u32[]{:S(2)}) copy-start(bf16[32,384]{1,0:T(8,128)(2,1)} %param.13) | copy-start | bytes 73732
  52.4 51.4 %copy-start.13 = (bf16[384]{0:T(512)(128)(2,1)S(1)}, bf16[384]{0:T(512)(128)(2,1)}, u32[]{:S(2)}) copy-start(bf16[384]{0:T(512)(128)(2,1)} %param.22) | copy-start | bytes 2308
  102.8 4.4 %copy-start.11 = (f32[32,384]{1,0:T(8,128)S(1)}, f32[32,384]{1,0:T(8,128)}, u32[]{:S(2)}) copy-start(f32[32,384]{1,0:T(8,128)} %param.16) | copy-start | bytes 147460
  109.6 3.8 %copy-start.2 = (bf16[384,1536]{1,0:T(8,128)(2,1)S(1)}, bf16[384,1536]{1,0:T(8,128)(2,1)}, u32[]{:S(2)}) copy-start(bf16[384,1536]{1,0:T(8,128)(2,1)} %param.23) | copy-start | bytes 3538948
  111.5 2.4 copy-start.1
  111.5 3.1 copy-start.9
  113.4 1.9 copy-start.12
  148.1 116.0 %copy-start.3 = (bf16[768,384]{1,0:T(8,128)(2,1)S(1)}, bf16[768,384]{1,0:T(8,128)(2,1)}, u32[]{:S(2)}) copy-start(bf16[768,384]{1,0:T(8,128)(2,1)} %get-tuple-element.41) | copy-start | bytes 1769476
  262.0 5.2 %copy-start.10 = (f32[3,32,128]{2,1,0:T(8,128)S(1)}, f32[3,32,128]{2,1,0:T(8,128)}, u32[]{:S(2)}) copy-start(f32[3,32,128]{2,1,0:T(8,128)} %get-tuple-element.39) | copy-start | bytes 147460
  313.5 4.8 %copy-start.6 = (f32[384,1536]{1,0:T(8,128)S(1)}, f32[384,1536]{1,0:T(8,128)}, u32[]{:S(2)}) copy-start(f32[384,1536]{1,0:T(8,128)} %get-tuple-element.97) | copy-start | bytes 7077892
  318.3 2.5 copy-start.5
  320.9 2.5 copy-start.4

commit v4 on v3

v4 whole, which is shorter than its diff:
```python
import functools

import jax
import jax.numpy as jnp
from jax import lax
from jax.experimental import pallas as pl
from jax.experimental.pallas import tpu as pltpu
from jax.sharding import PartitionSpec as P

F32 = jnp.float32
BF16 = jnp.bfloat16
MESH = pl.DeviceIdType.MESH
VMEM_LIMIT = 62 * 1024 * 1024
NEG = -1e30
ORDERS = ((0, 1, 2), (2, 0, 1), (1, 2, 0))
PARTS = 3
TILE = 128
HALF = TILE // 2
ALL = slice(None)


def rms_norm(tensor, gain):
    mean_sq = jnp.mean(tensor * tensor, axis=-1, keepdims=True)
    return tensor * lax.rsqrt(mean_sq + 1e-6) * gain


def gated_unit(gate_pre, up_pre):
    return jax.nn.silu(gate_pre) * up_pre


class Place:
    def __init__(self, n):
        self.n = n
        me = lax.axis_index("seq")
        self.me = me
        self.core = lax.rem(me, 2)
        x = lax.rem(me // 2, n)
        y = lax.rem(me // (2 * n), n)
        z = me // (2 * n * n)
        self.coord = (z, y, x)
        self.stride = (2 * n * n, 2 * n, 2)

    def along(self, axis, k):
        here = self.coord[axis]
        return self.me + (lax.rem(here + k, self.n) - here) * self.stride[axis]

    def other_core(self):
        return self.me + 1 - 2 * self.core

    def quarter(self):
        return self.me // (self.n ** 3 // 2)

    def mate(self, q):
        size = self.n ** 3 // 2
        return q * size + lax.rem(self.me, size)

    def to(self, k):
        return {"seq": k}

    def barrier(self):
        sem = pltpu.get_barrier_semaphore()
        for axis in range(3):
            for k in range(1, self.n):
                pl.semaphore_signal(sem, inc=1, device_id=self.to(self.along(axis, k)), device_id_type=MESH)
        pl.semaphore_signal(sem, inc=1, device_id=self.to(self.other_core()), device_id_type=MESH)
        extra = 0
        if self.n < 4:
            for k in range(1, 4):
                pl.semaphore_signal(sem, inc=1, device_id=self.to(self.mate(lax.rem(self.quarter() + k, 4))), device_id_type=MESH)
            extra = 3
        pl.semaphore_wait(sem, 3 * (self.n - 1) + 1 + extra)


def rcopy(src, dst, send, recv, device):
    return pltpu.make_async_remote_copy(src_ref=src, dst_ref=dst, send_sem=send, recv_sem=recv,
                                        device_id={"seq": device}, device_id_type=MESH)


def lanes(start, size):
    return pl.ds(pl.multiple_of(start, TILE), size)


def rows_of(start, size):
    return pl.ds(pl.multiple_of(start, 8), size)


class Gather:
    def __init__(self, n, at, src, full, bufs):
        self.n, self.at, self.src, self.full = n, at, src, full
        self.rows, self.send, self.recv, self.csend, self.crecv = bufs
        self.copies = {}

    @staticmethod
    def scratch(n, dtype):
        sem = pltpu.SemaphoreType.DMA
        return [pltpu.VMEM((PARTS, TILE, TILE), dtype), sem((3, PARTS, n - 1)), sem((3, PARTS, n - 1)),
                sem((PARTS,)), sem((PARTS,))]

    def begin(self):
        n, at = self.n, self.at
        r = TILE // n
        for p in range(PARTS):
            a3 = ORDERS[p][2]
            mine = rows_of(at.coord[a3] * r, r)
            for k in range(1, n):
                c = rcopy(self.src.at[p], self.rows.at[p, mine, :], self.send.at[0, p, k - 1], self.recv.at[0, p, k - 1], at.along(a3, k))
                c.start()
                self.copies[0, p, k] = c
            self.rows[p, mine, :] = self.src[p]

    def turn(self):
        at, n = self.at, self.n
        for p in range(PARTS):
            a1, a2, _ = ORDERS[p]
            for k in range(1, n):
                self.copies[0, p, k].wait()
            block = self.rows[p].astype(F32).T
            base = ((at.core * n + at.coord[a1]) * n + at.coord[a2]) * TILE
            self.full[p, :, lanes(base, TILE)] = block[:self.full.shape[1]].astype(self.full.dtype)

    def place(self, stage, p, back):
        at, n = self.at, self.n
        a1, a2, _ = ORDERS[p]
        if stage == 1:
            spot = lax.rem(at.coord[a2] + n - back, n)
            return a2, lanes(((at.core * n + at.coord[a1]) * n + spot) * TILE, TILE)
        spot = lax.rem(at.coord[a1] + n - back, n)
        return a1, lanes((at.core * n + spot) * n * TILE, n * TILE)

    def spread(self, stage):
        n, at = self.n, self.at
        for p in range(PARTS):
            axis, cols = self.place(stage, p, 0)
            view = self.full.at[p, :, cols]
            for k in range(1, n):
                c = rcopy(view, view, self.send.at[stage, p, k - 1], self.recv.at[stage, p, k - 1], at.along(axis, k))
                c.start()
                self.copies[stage, p, k] = c

    def settle(self, stage):
        n = self.n
        for p in range(PARTS):
            for k in range(1, n):
                self.copies[stage, p, k].wait()

    def swap(self):
        n, at = self.n, self.at
        width = n * n * TILE
        out = []
        for p in range(PARTS):
            view = self.full.at[p, :, lanes(at.core * width, width)]
            c = rcopy(view, view, self.csend.at[p], self.crecv.at[p], at.other_core())
            c.start()
            out.append(c)
        return out


GATHER_REFS = 5


def run_gathers(gathers, between=None):
    for g in gathers:
        g.begin()
    for g in gathers:
        g.turn()
        g.spread(1)
    for g in gathers:
        g.settle(1)
        g.spread(2)
    if between is not None:
        between()
    final = []
    for g in gathers:
        g.settle(2)
        final += g.swap()
    for c in final:
        c.wait()


def merge(blocks, rows_axis):
    take = (lambda b, i, j: b[i:j]) if rows_axis == 0 else (lambda b, i, j: b[:, i:j])
    outs, maxes, sums = [], [], []
    for h in range(2):
        ms = [take(b, TILE + h, TILE + h + 1) for b in blocks]
        m = functools.reduce(jnp.maximum, ms)
        ws = [jnp.exp(v - m) for v in ms]
        o = sum(take(b, HALF * h, HALF * h + HALF) * w for b, w in zip(blocks, ws))
        l = sum(take(b, TILE + 2 + h, TILE + 3 + h) * w for b, w in zip(blocks, ws))
        outs.append(o)
        maxes.append(m)
        sums.append(l)
    return outs, maxes + sums


class Scatter:
    def __init__(self, n, at, with_stats, bufs):
        self.n, self.at, self.with_stats = n, at, with_stats
        (self.far, self.near, self.buf0, self.buf1, self.acc1, self.buf2, self.acc2, self.buf3, self.pass_buf,
         self.csend, self.crecv, self.send, self.recv, self.psend, self.precv) = bufs
        self.relay = n == 4
        self.step = n * TILE

    @staticmethod
    def scratch(n, rows, wide):
        sem = pltpu.SemaphoreType.DMA
        half = n * n * TILE
        r = TILE // n
        return [
            pltpu.VMEM((PARTS, rows, half), F32), pltpu.VMEM((PARTS, rows, half), F32), pltpu.VMEM((PARTS, rows, half), F32),
            pltpu.VMEM((PARTS, n - 1, rows, n * TILE), F32), pltpu.VMEM((PARTS, rows, n * TILE), F32),
            pltpu.VMEM((PARTS, n - 1, rows, TILE), F32), pltpu.VMEM((PARTS, TILE, wide), F32),
            pltpu.VMEM((PARTS, n - 1, r, wide), F32), pltpu.VMEM((PARTS, 2, rows, n * HALF), F32),
            sem((PARTS, n)), sem((PARTS, n)), sem((3, PARTS, n - 1)), sem((3, PARTS, n - 1)), sem((PARTS, 2)), sem((PARTS, 2)),
        ]

    def visit(self, i):
        if self.relay:
            return jnp.where(i == 0, 2, jnp.where(i == 1, 3, jnp.where(i == 2, 1, 0)))
        return self.n - 1 - i

    def pass_copy(self, p, i):
        width = self.step // 2
        return rcopy(self.near.at[p, :, lanes(self.chunk(p, 2) * self.step + i * width, width)], self.pass_buf.at[p, i],
                     self.psend.at[p, i], self.precv.at[p, i], self.at.along(ORDERS[p][0], 1 + 2 * i))

    def take_over(self, p, i):
        self.pass_copy(p, i).wait_recv()
        width = self.step // 2
        for j in range(width // TILE):
            col = lanes(self.chunk(p, 1 + 2 * i) * self.step + i * width + j * TILE, TILE)
            self.combine(self.near, p, col, [self.near[p, :, col], self.pass_buf[p, i, :, j * TILE:(j + 1) * TILE]])
        self.first_copy(p, 1 + 2 * i).start()

    def chunk(self, p, k):
        return lax.rem(self.at.coord[ORDERS[p][0]] + k, self.n)

    def combine(self, dst, p, col, vals):
        if self.with_stats:
            outs, stats = merge(vals, 0)
            dst[p, 0:HALF, col] = outs[0]
            dst[p, HALF:TILE, col] = outs[1]
            dst[p, TILE:TILE + 8, col] = jnp.concatenate(stats + [jnp.zeros_like(stats[0])] * 4, axis=0)
        else:
            dst[p, :, col] = functools.reduce(jnp.add, vals)

    def core_copy(self, p, k):
        view = (p, ALL, lanes(self.chunk(p, k) * self.step, self.step))
        return rcopy(self.far.at[view], self.buf0.at[view], self.csend.at[p, k], self.crecv.at[p, k], self.at.other_core())

    def first_copy(self, p, k):
        return rcopy(self.near.at[p, :, lanes(self.chunk(p, k) * self.step, self.step)], self.buf1.at[p, k - 1],
                     self.send.at[0, p, k - 1], self.recv.at[0, p, k - 1], self.at.along(ORDERS[p][0], k))

    def far_done(self, k):
        for p in range(PARTS):
            self.core_copy(p, k).start()

    def near_done(self, k):
        for p in range(PARTS):
            self.core_copy(p, k).wait()

            def fold(j, _, p=p):
                col = lanes(self.chunk(p, k) * self.step + j * TILE, TILE)
                self.combine(self.near, p, col, [self.near[p, :, col], self.buf0[p, :, col]])
                return 0

            lax.fori_loop(0, self.n, fold, 0)

            if self.relay:
                @pl.when(k == 2)
                def _(p=p):
                    for i in range(2):
                        self.pass_copy(p, i).start()

                for i in range(2):
                    @pl.when(k == 1 + 2 * i)
                    def _(p=p, i=i):
                        self.take_over(p, i)
            else:
                @pl.when(k > 0)
                def _(p=p):
                    self.first_copy(p, k).start()

    def finish(self, o_ref, st_ref=None):
        n, at = self.n, self.at
        r = TILE // n
        copies = {}
        for p in range(PARTS):
            a1, a2, _ = ORDERS[p]
            direct = (1, 3) if self.relay else range(1, n)
            for k in direct:
                self.first_copy(p, k).wait()
            if self.relay:
                for i in range(2):
                    self.pass_copy(p, i).wait_send()
            mine = at.coord[a1] * n * TILE
            for j in range(n):
                col = slice(j * TILE, (j + 1) * TILE)
                self.combine(self.acc1, p, pl.ds(j * TILE, TILE),
                             [self.near[p, :, lanes(mine + j * TILE, TILE)]] + [self.buf1[p, k - 1, :, col] for k in direct])
            for k in range(1, n):
                there = lax.rem(at.coord[a2] + k, n)
                c = rcopy(self.acc1.at[p, :, lanes(there * TILE, TILE)], self.buf2.at[p, k - 1],
                          self.send.at[1, p, k - 1], self.recv.at[1, p, k - 1], at.along(a2, k))
                c.start()
                copies[1, p, k] = c
        for p in range(PARTS):
            _, a2, a3 = ORDERS[p]
            for k in range(1, n):
                copies[1, p, k].wait()
            blocks = [self.acc1[p, :, lanes(at.coord[a2] * TILE, TILE)]] + [self.buf2[p, k] for k in range(n - 1)]
            if self.with_stats:
                outs, stats = merge(blocks, 0)
                self.acc2[p, :, 0:TILE] = jnp.concatenate(outs, axis=0).T
                tail = jnp.concatenate(stats + [jnp.zeros((TILE - 4, TILE), F32)], axis=0)
                self.acc2[p, :, TILE:2 * TILE] = tail.T
            else:
                self.acc2[p] = functools.reduce(jnp.add, blocks).T
            for k in range(1, n):
                there = lax.rem(at.coord[a3] + k, n)
                c = rcopy(self.acc2.at[p, pl.ds(pl.multiple_of(there * r, r), r), :], self.buf3.at[p, k - 1],
                          self.send.at[2, p, k - 1], self.recv.at[2, p, k - 1], at.along(a3, k))
                c.start()
                copies[2, p, k] = c
        for p in range(PARTS):
            a3 = ORDERS[p][2]
            for k in range(1, n):
                copies[2, p, k].wait()
            blocks = [self.acc2[p, pl.ds(pl.multiple_of(at.coord[a3] * r, r), r), :]] + [self.buf3[p, k] for k in range(n - 1)]
            if self.with_stats:
                outs, (m0, m1, l0, l1) = merge(blocks, 1)
                o_ref[p] = jnp.concatenate([outs[0] / l0, outs[1] / l1], axis=1)
                col = lax.broadcasted_iota(jnp.int32, (r, TILE), 1)
                st_ref[p] = jnp.where(col == 0, m0 + jnp.log(l0), jnp.where(col == 1, m1 + jnp.log(l1), 0.0))
            else:
                o_ref[p] = functools.reduce(jnp.add, blocks)


class Wide:
    def __init__(self, shape, n):
        self.part, self.cols = shape[0] // PARTS, shape[1]
        self.r1, self.r2, self.c3 = self.part // 2, self.part // 2 // n, shape[1] // n
        self.l1, self.l2, self.l3 = (self.r1, self.cols), (self.r2, self.cols), (self.r2, self.c3)

    def row(self, p, c, a):
        return self.part * p + self.r1 * c + self.r2 * a

    def full1(self, p, c):
        return rows_of(self.part * p + self.r1 * c, self.r1), ALL

    def full2(self, p, c, a):
        return rows_of(self.row(p, c, a), self.r2), ALL

    def half2(self, p, c, a, i):
        size = self.r2 // 2
        return rows_of(self.row(p, c, a) + i * size, size), ALL

    def hin1(self, a, i):
        size = self.r2 // 2
        return rows_of(self.r2 * a + i * size, size), ALL

    def full3(self, p, c, a, b):
        return rows_of(self.row(p, c, a), self.r2), lanes(self.c3 * b, self.c3)

    def in1(self, a):
        return rows_of(self.r2 * a, self.r2), ALL

    def in2(self, b):
        return ALL, lanes(self.c3 * b, self.c3)


class Tall(Wide):
    def __init__(self, shape, n):
        super().__init__(shape, n)
        self.r3 = self.r2 // n
        self.l3 = (self.r3, self.cols)

    def full3(self, p, c, a, b):
        return rows_of(self.row(p, c, a) + self.r3 * b, self.r3), ALL

    def in2(self, b):
        return rows_of(self.r3 * b, self.r3), ALL


class Stack:
    def __init__(self, shape, n):
        w, rows, cols = shape
        self.part, self.w3 = rows // PARTS, w // n
        self.r1, self.r2 = self.part // 2, self.part // 2 // n
        self.l1, self.l2, self.l3 = (w, self.r1, cols), (w, self.r2, cols), (self.w3, self.r2, cols)

    def full1(self, p, c):
        return ALL, rows_of(self.part * p + self.r1 * c, self.r1), ALL

    def row(self, p, c, a):
        return self.part * p + self.r1 * c + self.r2 * a

    def full2(self, p, c, a):
        return ALL, rows_of(self.row(p, c, a), self.r2), ALL

    def full3(self, p, c, a, b):
        return pl.ds(self.w3 * b, self.w3), rows_of(self.row(p, c, a), self.r2), ALL

    def in1(self, a):
        return ALL, rows_of(self.r2 * a, self.r2), ALL

    def in2(self, b):
        return pl.ds(self.w3 * b, self.w3), ALL, ALL


class Reduce:
    STAGES = ("core", "pass", "first", "second", "third", "back2", "back1", "relay", "swap")

    def __init__(self, n, at, form, src, out, bufs, relay):
        self.n, self.at, self.form, self.src, self.out = n, at, form, src, out
        self.relay = relay and n == 4
        self.stages = [v for v in self.STAGES if self.relay or v not in ("pass", "relay")]
        (self.own, self.buf0, self.buf1, self.acc1, self.buf2, self.buf3, self.lsem,
         self.csend, self.crecv, self.send, self.recv) = bufs

    @staticmethod
    def scratch(n, form):
        sem = pltpu.SemaphoreType.DMA
        kinds = len(Reduce.STAGES)
        return [
            pltpu.VMEM((PARTS,) + form.l1, F32), pltpu.VMEM((PARTS,) + form.l1, F32),
            pltpu.VMEM((PARTS, n - 1) + form.l2, F32), pltpu.VMEM((PARTS,) + form.l2, F32),
            pltpu.VMEM((PARTS, n - 1) + form.l3, F32), pltpu.VMEM((PARTS, n) + form.l3, F32),
            sem((PARTS,)), sem((PARTS,)), sem((PARTS,)), sem((kinds, PARTS, n - 1)), sem((kinds, PARTS, n - 1)),
        ]

    def spots(self, p):
        return [self.at.coord[a] for a in ORDERS[p]]

    def hold(self, p, i):
        return self.buf1.at[(p, 1)].at[self.form.hin1(0, i)]

    def copies(self, stage, p):
        at, n, form = self.at, self.n, self.form
        A1, A2, A3 = self.spots(p)
        a1, a2, a3 = ORDERS[p]
        c = at.core
        if stage == "core":
            return [rcopy(self.src.at[form.full1(p, 1 - c)], self.buf0.at[p], self.csend.at[p], self.crecv.at[p], at.other_core()),
                    pltpu.make_async_copy(self.src.at[form.full1(p, c)], self.own.at[p], self.lsem.at[p])]
        kind = self.STAGES.index(stage)
        out = []

        def add(src, dst, axis, k):
            out.append(rcopy(src, dst, self.send.at[kind, p, k - 1], self.recv.at[kind, p, k - 1], at.along(axis, k)))

        if stage == "swap":
            view = self.out.at[form.full1(p, c)]
            return [rcopy(view, view, self.send.at[kind, p, 0], self.recv.at[kind, p, 0], at.other_core())]
        steps = range(1, n)
        near = (1, n - 1) if self.relay else steps
        if stage == "pass":
            for i, k in enumerate(near):
                add(self.own.at[p].at[form.hin1(lax.rem(A1 + 2, n), i)], self.hold(p, i), a1, k)
        elif stage == "first":
            for k in near:
                add(self.own.at[p].at[form.in1(lax.rem(A1 + k, n))], self.buf1.at[p, k - 1], a1, k)
        elif stage == "second":
            for k in steps:
                add(self.acc1.at[p].at[form.in2(lax.rem(A2 + k, n))], self.buf2.at[p, k - 1], a2, k)
        elif stage == "third":
            for k in steps:
                add(self.buf3.at[p, A3], self.buf3.at[p, A3], a3, k)
        elif stage == "back2":
            view = self.out.at[form.full3(p, c, A1, A2)]
            for k in steps:
                add(view, view, a2, k)
        elif stage == "back1":
            view = self.out.at[form.full2(p, c, A1)]
            for k in near:
                add(view, view, a1, k)
        else:
            for i, k in enumerate(near):
                view = self.out.at[form.half2(p, c, lax.rem(A1 + n - k, n), i)]
                add(view, view, a1, k)
        return out

    def advance(self, step):
        form, n = self.form, self.n
        stage = self.stages[step] if step < len(self.stages) else None
        before = self.stages[step - 1]
        near = (0, n - 2) if self.relay else range(n - 1)
        for p in range(PARTS):
            A1, A2, A3 = self.spots(p)
            if step:
                for c in self.copies(before, p):
                    c.wait()
            own = self.own.at[p]
            if before == "core":
                own[...] += self.buf0[p]
            elif before == "pass":
                for i, k in enumerate((1, n - 1)):
                    own[form.hin1(lax.rem(A1 + k, n), i)] += self.hold(p, i)[...]
            elif before == "first":
                self.acc1[p] = functools.reduce(jnp.add, [own[form.in1(A1)]] + [self.buf1[p, k] for k in near])
            elif before == "second":
                self.buf3[p, A3] = functools.reduce(jnp.add, [self.acc1[(p,) + form.in2(A2)]] + [self.buf2[p, k] for k in range(n - 1)])
            elif before == "third":
                self.out[form.full3(p, self.at.core, A1, A2)] = functools.reduce(jnp.add, [self.buf3[p, k] for k in range(n)])
            if stage:
                for c in self.copies(stage, p):
                    c.start()

    def finish(self, step):
        for i in range(step, len(self.stages) + 1):
            self.advance(i)


REDUCE_REFS = 11


QB = 256


def aux_rows(rows, width):
    pad = jnp.zeros((64 - len(rows), width), F32)
    return jnp.concatenate(list(rows) + [pad], axis=0).astype(BF16)


def split3(v):
    hi = v.astype(BF16).astype(F32)
    mid = (v - hi).astype(BF16).astype(F32)
    lo = (v - hi - mid).astype(BF16).astype(F32)
    return [hi, mid, lo]


def blocks_loop(n, scatter, blocks, events):
    per = n * TILE // QB
    at = scatter.at

    def body(t, _):
        u = t // per
        k = scatter.visit(u // 2)
        near = lax.rem(u, 2)
        half = jnp.where(near == 1, at.core, 1 - at.core)
        inside = [scatter.chunk(p, k) * (n * TILE) + lax.rem(t, per) * QB for p in range(PARTS)]
        srcs = [pl.ds(pl.multiple_of(half * (n * n * TILE) + i, QB), QB) for i in inside]
        blocks(srcs, near, [pl.ds(pl.multiple_of(i, QB), QB) for i in inside])
        last = lax.rem(t, per) == per - 1

        @pl.when(last & (near == 0))
        def _():
            scatter.far_done(k)

        @pl.when(last & (near == 1))
        def _():
            scatter.near_done(k)

        for when, action in events:
            @pl.when(t == when)
            def _(action=action):
                action()
        return 0

    lax.fori_loop(0, 2 * n * per, body, 0)


def put(scatter, near, p, row, col, val):
    @pl.when(near == 1)
    def _():
        scatter.near[p, row, col] = val

    @pl.when(near == 0)
    def _():
        scatter.far[p, row, col] = val


def head(j):
    return slice(HALF * j, HALF * (j + 1))


def beside(j, block, other):
    return jnp.concatenate([block, other] if j == 0 else [other, block], axis=0)


def shrink(op, v, rows):
    while v.shape[0] > rows:
        h = v.shape[0] // 2
        v = op(v[:h], v[h:])
    return v


KC = 256


def fwd_kernel(n, x_ref, mem_ref, wk_ref, wv_ref, auxk_ref, auxv_ref, o_ref, st_ref, *refs):
    saved, refs = refs[:SAVED], refs[SAVED:]
    kept, refs = refs[:SAVED], refs[SAVED:]
    q_ref, keep_ref, k_ref, v_ref, kt_ref = kept
    vt_ref, s_buf, msend, mrecv, save_sem, *refs = refs
    gbufs, bufs = refs[:GATHER_REFS], refs[GATHER_REFS:]
    keys = k_ref.shape[1]
    piece = keys // 3
    kc = min(KC, piece)
    chunks = keys // kc
    at = Place(n)
    at.barrier()
    quarter = at.quarter()

    def donate(q):
        return rcopy(mem_ref.at[pl.ds(keys, piece), :], keep_ref.at[pl.ds(q * piece, piece), :], msend, mrecv.at[q], at.mate(3))

    def saves():
        return [pltpu.make_async_copy(a, b, save_sem.at[i]) for i, (a, b) in enumerate(zip(kept, saved))]

    for q in range(3):
        @pl.when(quarter == q)
        def _(q=q):
            donate(q).start()

    def project():
        @pl.when(quarter < 3)
        def _():
            keep_ref[...] = mem_ref[0:keys, :]

        @pl.when(quarter == 3)
        def _():
            for q in range(3):
                donate(q).wait_recv()

        low = lax.broadcasted_iota(jnp.int32, (piece, TILE), 1) < HALF
        for i in range(3):
            rows = pl.ds(i * piece, piece)
            m = keep_ref[rows, :]
            for w_ref, aux_ref, a_ref, t_ref in ((wk_ref, auxk_ref, k_ref, kt_ref), (wv_ref, auxv_ref, v_ref, vt_ref)):
                aux = aux_ref[rows, :].astype(F32)
                for p in range(PARTS):
                    b = jnp.dot(m, w_ref[:, p * TILE:(p + 1) * TILE], preferred_element_type=F32).astype(BF16).astype(F32)
                    a_ref[2 * p, rows, :] = jnp.where(low, b, aux).astype(BF16)
                    a_ref[2 * p + 1, rows, :] = jnp.where(low, aux, b).astype(BF16)
                    t_ref[p, :, rows] = b.T.astype(BF16)

    run_gathers([Gather(n, at, x_ref, q_ref, gbufs)], project)
    for q in range(3):
        @pl.when(quarter == q)
        def _(q=q):
            donate(q).wait_send()
    for c in saves():
        c.start()
    aux = aux_rows([jnp.ones((1, QB), F32)], QB)
    scatter = Scatter(n, at, True, bufs)

    def blocks(srcs, near, dsts):
        heads = [(p, j) for p in range(PARTS) for j in range(2)]

        def score(i, c, run):
            p, j = heads[i]
            qa = beside(j, q_ref[p, head(j), srcs[p]], aux)
            s = jnp.dot(k_ref[i, c * kc:(c + 1) * kc, :], qa, preferred_element_type=F32)
            s_buf[i % 2, c * kc:(c + 1) * kc, :] = s
            top = shrink(jnp.maximum, s, 16)
            return top if run is None else jnp.maximum(run, top)

        run = None
        for c in range(chunks):
            run = score(0, c, run)
        done = []
        for i, (p, j) in enumerate(heads):
            m = jnp.max(run, axis=0, keepdims=True)
            run, total, out = None, None, None
            for c in range(chunks):
                if i + 1 < len(heads):
                    run = score(i + 1, c, run)
                e = jnp.exp(s_buf[i % 2, c * kc:(c + 1) * kc, :] - m)
                part = shrink(jnp.add, e, 16)
                total = part if total is None else total + part
                o = jnp.dot(vt_ref[p, head(j), c * kc:(c + 1) * kc], e.astype(BF16), preferred_element_type=F32)
                out = o if out is None else out + o
            done.append((out, m, jnp.sum(total, axis=0, keepdims=True)))
            if j == 1:
                (o0, m0, l0), (o1, m1, l1) = done[-2:]
                val = jnp.concatenate([o0, o1, m0, m1, l0, l1, jnp.zeros((4, QB), F32)], axis=0)
                put(scatter, near, p, ALL, dsts[p], val)

    blocks_loop(n, scatter, blocks, [])
    scatter.finish(o_ref, st_ref)
    for c in saves():
        c.wait()


SAVED = 5


def attention_fwd(n, cid, rows, memory, wk, wv, aux_k, aux_v):
    total = 2 * n * n * TILE
    r = TILE // n
    keys, dim = aux_k.shape[0], memory.shape[1]
    vm, hbm = pl.BlockSpec(memory_space=pltpu.VMEM), pl.BlockSpec(memory_space=pl.ANY)
    sem = pltpu.SemaphoreType.DMA
    shapes = ((PARTS, TILE, total), (keys, dim), (2 * PARTS, keys, TILE), (2 * PARTS, keys, TILE), (PARTS, TILE, keys))
    scratch = [pltpu.VMEM(v, BF16) for v in shapes] + [pltpu.VMEM(shapes[-1], BF16), pltpu.VMEM((2, keys, QB), F32),
                                                       sem(()), sem((3,)), sem((SAVED,))]
    return pl.pallas_call(
        functools.partial(fwd_kernel, n),
        out_shape=(jax.ShapeDtypeStruct((PARTS, r, TILE), F32),) * 2 + tuple(jax.ShapeDtypeStruct(v, BF16) for v in shapes),
        in_specs=[vm] * 6, out_specs=(vm,) * 2 + (hbm,) * SAVED, name="attention_fwd",
        scratch_shapes=scratch + Gather.scratch(n, BF16) + Scatter.scratch(n, TILE + 8, 2 * TILE),
        compiler_params=pltpu.CompilerParams(collective_id=cid, has_side_effects=True, vmem_limit_bytes=VMEM_LIMIT),
    )(rows, memory, wk, wv, aux_k, aux_v)


SCATTER_REFS = 15


def bwd_kernel(n, forms, q_ref, x_ref, s_ref, k_ref, v_ref, kt_ref, *refs):
    count = len(forms)
    grads, refs = refs[:count], refs[count:]
    dq_ref, dk_ref, dv_ref, *refs = refs
    sums, refs = refs[:count], refs[count:]
    do_ref, st_ref, dk_acc, dv_acc, *refs = refs
    xbufs, refs = refs[:GATHER_REFS], refs[GATHER_REFS:]
    sbufs, refs = refs[:GATHER_REFS], refs[GATHER_REFS:]
    bufs, refs = refs[:SCATTER_REFS], refs[SCATTER_REFS:]
    one = jnp.ones((1, QB), F32)
    zero = jnp.zeros((1, QB), F32)
    blank = jnp.zeros((HALF, QB), BF16)
    nt = (((1,), (1,)), ((), ()))
    at = Place(n)
    at.barrier()
    scatter = Scatter(n, at, False, bufs)
    reduces = [Reduce(n, at, form, grads[i], sums[i], refs[REDUCE_REFS * i:REDUCE_REFS * (i + 1)], True)
               for i, form in enumerate(forms)]

    def advance(stage):
        for red in reduces:
            red.advance(stage)

    gathers = [Gather(n, at, s_ref, st_ref, sbufs), Gather(n, at, x_ref, do_ref, xbufs)]
    for g in gathers:
        g.begin()
    advance(0)
    dk_acc[...] = jnp.zeros_like(dk_acc)
    dv_acc[...] = jnp.zeros_like(dv_acc)
    for g in gathers:
        g.turn()
        g.spread(1)
    for g in gathers:
        g.settle(1)
        g.spread(2)
    advance(1)
    final = []
    for g in gathers:
        g.settle(2)
        final += g.swap()
    for c in final:
        c.wait()

    def block(p, src, near, dst):
        probs, dscores, dos, qs, dqs = [], [], [], [], []
        for j in range(2):
            qh = q_ref[p, head(j), src]
            doh = do_ref[p, head(j), src]
            lse = st_ref[p, j:j + 1, src]
            delta = st_ref[p, 2 + j:3 + j, src]
            qa = beside(j, qh, aux_rows([one] + split3(-lse), QB))
            da = beside(j, doh, aux_rows([zero] + split3(-delta), QB))
            e = jnp.exp(jnp.dot(k_ref[2 * p + j], qa, preferred_element_type=F32))
            dp = jnp.dot(v_ref[2 * p + j], da, preferred_element_type=F32)
            ds = (e * dp).astype(BF16)
            probs.append(e.astype(BF16))
            dscores.append(ds)
            dos.append(beside(j, doh, blank))
            qs.append(beside(j, qh, blank))
            dqs.append(0.125 * jnp.dot(kt_ref[p, head(j), :], ds, preferred_element_type=F32))
        dv_acc[p] += (lax.dot_general(probs[0], dos[0], nt, preferred_element_type=F32)
                      + lax.dot_general(probs[1], dos[1], nt, preferred_element_type=F32))
        dk_acc[p] += (lax.dot_general(dscores[0], qs[0], nt, preferred_element_type=F32)
                      + lax.dot_general(dscores[1], qs[1], nt, preferred_element_type=F32))
        put(scatter, near, p, ALL, dst, jnp.concatenate(dqs, axis=0))

    trips = 2 * n * (n * TILE // QB)
    when = [min(w, trips - 1) for w in ((0, 3, 5, 7, 9, 12, 14) if reduces[0].relay else (3, 5, 7, 9, 13))]

    def blocks(srcs, near, dsts):
        for p in range(PARTS):
            block(p, srcs[p], near, dsts[p])

    blocks_loop(n, scatter, blocks, [(w, functools.partial(advance, i + 2)) for i, w in enumerate(when)])
    for p in range(PARTS):
        dk_ref[:, p * TILE:(p + 1) * TILE] = dk_acc[p].astype(BF16)
        dv_ref[:, p * TILE:(p + 1) * TILE] = dv_acc[p].astype(BF16)

    scatter.finish(dq_ref)
    for red in reduces:
        red.finish(2 + len(when))


def attention_bwd(n, cid, q_t, do_rows, stats_rows, k_aug, v_aug, k_t, wide, tall):
    total, keys = q_t.shape[2], k_aug.shape[1]
    r = TILE // n
    forms = [Wide(a.shape, n) for a in wide] + [Tall(a.shape, n) for a in tall]
    grads = list(wide) + list(tall)
    vm = pl.BlockSpec(memory_space=pltpu.VMEM)
    flat = jax.ShapeDtypeStruct((keys, PARTS * TILE), BF16)
    acc = pltpu.VMEM((PARTS, keys, TILE), F32)
    outs = [jax.ShapeDtypeStruct((PARTS, r, TILE), F32), flat, flat] + [jax.ShapeDtypeStruct(a.shape, F32) for a in grads]
    scratch = [pltpu.VMEM((PARTS, TILE, total), BF16), pltpu.VMEM((PARTS, 8, total), F32),
               acc, acc]
    scratch += Gather.scratch(n, BF16) + Gather.scratch(n, F32) + Scatter.scratch(n, TILE, TILE)
    for form in forms:
        scratch += Reduce.scratch(n, form)
    return pl.pallas_call(
        functools.partial(bwd_kernel, n, forms), out_shape=tuple(outs),
        in_specs=[vm] * 6 + [pl.BlockSpec(memory_space=pl.ANY)] * len(grads), out_specs=(vm,) * len(outs), name="attention_bwd",
        scratch_shapes=scratch,
        cost_estimate=pl.CostEstimate(flops=10 * 384 * total * keys, bytes_accessed=20_000_000, transcendentals=6 * total * keys),
        compiler_params=pltpu.CompilerParams(collective_id=cid, has_side_effects=True, vmem_limit_bytes=VMEM_LIMIT),
    )(q_t, do_rows, stats_rows, k_aug, v_aug, k_t, *grads)


def reduce_kernel(n, form, src, small, dk_ref, dv_ref, wk_ref, wv_ref, out, small_out, dm_ref,
                  slots, pair, ssend, srecv, dm_buf, msend, mrecv, *bufs):
    at = Place(n)
    at.barrier()
    red = Reduce(n, at, form, src, out, bufs, False)
    keep = dk_ref.shape[0]
    piece = keep // 3
    quarter = at.quarter()
    nt = (((1,), (1,)), ((), ()))

    def give_back(q):
        return rcopy(dm_buf.at[pl.ds(q * piece, piece), :], dm_ref.at[pl.ds(keep, piece), :], msend.at[q], mrecv, at.mate(q))

    def memory_grad():
        for i in range(3):
            rows = slice(i * piece, (i + 1) * piece)
            dm_buf[rows, :] = (lax.dot_general(dk_ref[rows, :], wk_ref[...], nt, preferred_element_type=F32)
                               + lax.dot_general(dv_ref[rows, :], wv_ref[...], nt, preferred_element_type=F32))

        @pl.when(quarter == 3)
        def _():
            for q in range(3):
                give_back(q).start()
            dm_ref[...] = jnp.zeros_like(dm_ref)

        @pl.when(quarter < 3)
        def _():
            dm_ref[0:keep, :] = dm_buf[...]

    def small_copies(stage):
        if stage == 3:
            return [rcopy(pair.at[at.core], pair.at[at.core], ssend.at[3, 0], srecv.at[3, 0], at.other_core())]
        mine = slots.at[stage, at.coord[stage]]
        return [rcopy(mine, mine, ssend.at[stage, k - 1], srecv.at[stage, k - 1], at.along(stage, k)) for k in range(1, n)]

    red.advance(0)
    slots[0, at.coord[0]] = small[...]
    for c in small_copies(0):
        c.start()
    for stage in range(1, 8):
        red.advance(stage)
        if stage == 1:
            memory_grad()
        if stage < 5:
            for c in small_copies(stage - 1):
                c.wait()
            if stage < 4:
                val = functools.reduce(jnp.add, [slots[stage - 1, k] for k in range(n)])
                if stage < 3:
                    slots[stage, at.coord[stage]] = val
                else:
                    pair[at.core] = val
                for c in small_copies(stage):
                    c.start()
            else:
                small_out[...] = pair[0] + pair[1]

    @pl.when(quarter == 3)
    def _():
        for q in range(3):
            give_back(q).wait_send()

    @pl.when(quarter < 3)
    def _():
        give_back(0).wait_recv()


def all_reduce_late(n, cid, m_rows, stack, small, dk, dv, wk, wv):
    form = Stack(stack.shape, n)
    vm = pl.BlockSpec(memory_space=pltpu.VMEM)
    sem = pltpu.SemaphoreType.DMA
    return pl.pallas_call(
        functools.partial(reduce_kernel, n, form),
        out_shape=(jax.ShapeDtypeStruct(stack.shape, F32), jax.ShapeDtypeStruct(small.shape, F32),
                   jax.ShapeDtypeStruct((m_rows, wk.shape[0]), F32)),
        in_specs=[pl.BlockSpec(memory_space=pl.ANY)] + [vm] * 5, out_specs=(vm,) * 3, name="reduce_late",
        scratch_shapes=[pltpu.VMEM((3, n) + small.shape, F32), pltpu.VMEM((2,) + small.shape, F32),
                        sem((4, n - 1)), sem((4, n - 1)), pltpu.VMEM((dk.shape[0], wk.shape[0]), F32), sem((3,)), sem(())]
        + Reduce.scratch(n, form),
        compiler_params=pltpu.CompilerParams(collective_id=cid, has_side_effects=True, vmem_limit_bytes=VMEM_LIMIT // 2),
    )(stack, small, dk, dv, wk, wv)


def solution(mesh):
    group = mesh.shape['seq']
    n = round((group // 2) ** (1 / 3))
    row_spec = P(('data', 'seq'), None)
    weight_spec = P()
    part_vec = P('data')
    part_mat = P('data', None)
    part_cube = P('data', None, None)

    def by_part(a):
        return jnp.transpose(a.reshape(a.shape[0], PARTS, TILE), (1, 0, 2))

    def by_row(a):
        return jnp.transpose(a, (1, 0, 2)).reshape(a.shape[1], PARTS * TILE)

    def device_step(dec_in, memory, mem_len, grad_out, norm_attn, wq_cross, wk_cross, wv_cross, wo_cross, norm_mlp, w_gate, w_up, w_down):
        q_rows, model_dim = dec_in.shape
        m_rows = memory.shape[0]
        heads, head_dim = wq_cross.shape[1], wq_cross.shape[2]
        wide = heads * head_dim
        wq, wk, wv = (w.reshape(model_dim, wide) for w in (wq_cross, wk_cross, wv_cross))
        wo = wo_cross.reshape(wide, model_dim)
        keep, piece, size = m_rows * 3 // 4, m_rows // 4, group // 4
        me = lax.axis_index('seq')
        slot = jnp.arange(keep)
        own_pos = me * m_rows + slot
        given_pos = ((slot // piece) * size + me % size) * m_rows + keep + slot % piece
        mem_pos = jnp.where(me // size == 3, given_pos, own_pos)
        bias = jnp.where(mem_pos < mem_len[0], 0.0, NEG)[:, None]
        lane = jnp.arange(TILE)[None, :] % head_dim
        flag = jnp.where((lane >= 1) & (lane <= 3), 1.0, 0.0)
        aux_k = jnp.where(lane == 0, bias, flag).astype(BF16)
        aux_v = jnp.broadcast_to(flag, aux_k.shape).astype(BF16)

        x_in = dec_in.astype(F32)
        normed_f, norm_pull = jax.vjp(rms_norm, x_in, norm_attn.astype(F32))
        normed = normed_f.astype(BF16)
        local_query = jnp.dot(normed, wq, preferred_element_type=F32).astype(BF16) * jnp.asarray(head_dim ** -0.5, BF16)
        out_parts, lse, q_t, kept, k_aug, v_aug, k_t = attention_fwd(
            n, 1, by_part(local_query), memory, wk, wv, aux_k, aux_v)
        attended_f = by_row(out_parts)

        attended = attended_f.astype(BF16)
        hidden_f = x_in + jnp.dot(attended, wo, preferred_element_type=F32)
        hidden = hidden_f.astype(BF16)
        normed_mlp_f, mlp_norm_pull = jax.vjp(rms_norm, hidden.astype(F32), norm_mlp.astype(F32))
        normed_mlp = normed_mlp_f.astype(BF16)
        gate_pre = jnp.dot(normed_mlp, w_gate, preferred_element_type=F32)
        up_pre = jnp.dot(normed_mlp, w_up, preferred_element_type=F32)
        mlp_f, gated_pull = jax.vjp(gated_unit, gate_pre, up_pre)
        mlp_act = mlp_f.astype(BF16)

        grad_top = grad_out.astype(BF16)
        g_down = jnp.einsum('qf,qd->fd', mlp_act, grad_top, preferred_element_type=F32)
        grad_act = jnp.einsum('qd,fd->qf', grad_top, w_down, preferred_element_type=F32)
        grad_gate, grad_up = gated_pull(grad_act)
        grad_gate_b = grad_gate.astype(BF16)
        grad_up_b = grad_up.astype(BF16)
        g_gate = jnp.einsum('qd,qf->df', normed_mlp, grad_gate_b, preferred_element_type=F32)
        g_up = jnp.einsum('qd,qf->df', normed_mlp, grad_up_b, preferred_element_type=F32)
        grad_normed_mlp = (jnp.einsum('qf,df->qd', grad_gate_b, w_gate, preferred_element_type=F32)
                           + jnp.einsum('qf,df->qd', grad_up_b, w_up, preferred_element_type=F32))
        grad_hidden_norm, g_norm_mlp = mlp_norm_pull(grad_normed_mlp)
        grad_hidden = grad_out + grad_hidden_norm
        grad_hidden_b = grad_hidden.astype(BF16)
        g_wo = jnp.einsum('qe,qd->ed', attended, grad_hidden_b, preferred_element_type=F32)
        grad_attended = jnp.einsum('qd,ed->qe', grad_hidden_b, wo, preferred_element_type=F32)
        delta = jnp.sum((grad_attended * attended_f).reshape(q_rows, PARTS, 2, head_dim), axis=-1)
        delta = jnp.transpose(delta, (1, 0, 2))
        stats_in = jnp.concatenate([lse[:, :, 0:2], delta, jnp.zeros((PARTS, q_rows, TILE - 4), F32)], axis=2)

        dq_parts, dk_b, dv_b, g_gate, g_up, g_down = attention_bwd(
            n, 2, q_t, by_part(grad_attended.astype(BF16)), stats_in, k_aug, v_aug, k_t, (g_gate, g_up), (g_down,))
        grad_query_b = by_row(dq_parts).astype(BF16)

        g_wq = jnp.einsum('td,te->de', normed, grad_query_b, preferred_element_type=F32)
        grad_normed = jnp.einsum('te,de->td', grad_query_b, wq, preferred_element_type=F32)
        grad_x_norm, g_norm_attn = norm_pull(grad_normed)
        g_dec = grad_hidden + grad_x_norm
        g_wk = jnp.einsum('td,te->de', kept, dk_b, preferred_element_type=F32)
        g_wv = jnp.einsum('td,te->de', kept, dv_b, preferred_element_type=F32)
        small = jnp.concatenate([g_norm_attn[None], g_norm_mlp[None], jnp.zeros((6, model_dim), F32)], axis=0)
        late, small, g_mem = all_reduce_late(n, 3, m_rows, jnp.stack([g_wq, g_wk, g_wv, g_wo]), small, dk_b, dv_b, wk, wv)
        cube = (model_dim, heads, head_dim)
        g_wq, g_wk, g_wv = late[0], late[1], late[2]
        g_wo = late[3].reshape(heads, head_dim, model_dim)
        g_norm_attn, g_norm_mlp = small[0], small[1]
        return (g_dec, g_mem, g_norm_attn, g_wq.reshape(cube), g_wk.reshape(cube), g_wv.reshape(cube),
                g_wo, g_norm_mlp, g_gate, g_up, g_down)

    return jax.shard_map(device_step, mesh=mesh,
                         in_specs=(row_spec, row_spec, part_vec, row_spec) + (weight_spec,) * 9,
                         out_specs=(row_spec, row_spec, part_vec, part_cube, part_cube, part_cube, part_cube, part_vec, part_mat, part_mat, part_mat),
                         check_vma=False)
```

time: 326 us -> 288 us (0.88)
  Pallas kernels: 276 us -> 241 us
    pallas_call x2 -> x0, Pallas kernels: 73.8 us -> none  [the longest x1 42.3 us: prepare(): pl.pallas_call(functools.partial(prepare_kernel, n), out_shape=outs, in_s...]
    pallas_call x1, Pallas kernels: 50.3 us -> 81.8 us  [attention_fwd(): pl.pallas_call(functools.partial(fwd_kernel, n), out_shape=(jax.ShapeDtyp...]
    pallas_call x1, Pallas kernels: 38.4 us -> 48.6 us  [all_reduce_late(): pl.pallas_call(functools.partial(reduce_kernel, n, form), out_shape=(jax....]
    unnamed x32 -> x40, local copies, waits for them, and re-layouts: 9.18 us -> 8.9 us
where the time goes in v4:
time: 288 us; the launch traced here: 287 us
  Pallas kernels  241 us (84%)
  local copies, waits for them, and re-layouts  22 us (8%)
  matrix products  17.9 us (6%)
  other arithmetic  4.48 us (2%)
    pallas_call x1, Pallas kernels, attention_bwd(): pl.pallas_call(functools.partial(bwd_kernel, n, forms), out_shape=tuple(o...  111 us
    pallas_call x1, Pallas kernels, attention_fwd(): pl.pallas_call(functools.partial(fwd_kernel, n), out_shape=(jax.ShapeDtyp...  81.8 us
    pallas_call x1, Pallas kernels, all_reduce_late(): pl.pallas_call(functools.partial(reduce_kernel, n, form), out_shape=(jax....  48.6 us
    unnamed x40, local copies, waits for them, and re-layouts  8.9 us

profile of v4, /device:TPU:1, one launch (start us, length us, event | category | flops | bytes accessed | tf_op | source)
XLA Modules:
  0.0 287.3 jit_solution(9447733015356501893)
XLA Ops:
  0.6 0.0 copy-start
  0.7 0.0 copy-start.12
  0.7 0.0 copy-start.11
  0.7 0.0 copy-start.17
  1.5 0.8 select_convert_fusion.auxk_ref
  2.4 0.8 fusion.15
  3.2 0.7 convert_element_type.69
  3.9 1.2 fusion.3
  5.1 0.6 copy.83
  5.8 1.8 copy.42.wk_ref
  7.6 1.8 copy.43.wv_ref
  9.5 0.7 broadcast_in_dim.72.auxv_ref
  10.2 81.8 %attention_fwd.1 = (f32[3,32,128]{2,1,0:T(8,128)}, f32[3,32,128]{2,1,0:T(8,128)}, bf16[3,128,4096]{2,1,0:T(8,128)(2,1)}, bf16[768,384]{1,0:T(8,128)(2,1)}, bf16[...) custom-call(bf16[3,32,128]{2,1,0:T(8,128)(2,1)} %bitcast.109, ...), custom_call_target="tpu_custom_call" | custom-call | tf_op jit(solution)/shard_map/attention_fwd/pallas_call | solution.py:698
  92.0 0.0 copy-done.12
  92.0 0.0 copy-done.11
  92.0 1.1 multiply_reduce_fusion.2
  93.1 0.0 copy-done.17
  93.2 0.1 multiply_convert_fusion.3
  93.2 1.6 fusion.56
  94.8 1.6 fusion.57
  96.4 0.0 copy-done.15
  96.4 1.9 fusion.8.refs_2_
  98.3 0.5 multiply_convert_fusion.1
  98.8 0.0 copy-start.6
  98.8 1.9 fusion.60.refs_1_
  100.7 1.9 fusion.59.refs_0_
  102.6 0.5 fusion.58
  103.1 0.0 copy-done.5
  103.1 0.6 multiply_reduce_fusion
  103.7 0.1 fusion.13
  103.8 0.2 bitcast_multiply_fusion
  104.1 0.1 reshape.157
  104.2 0.2 reduce_sum.65
  104.4 0.1 pad.9.clone
  104.5 0.7 maximum_maximum_fusion.s_ref
  105.2 0.6 copy.82
  105.8 110.8 %attention_bwd.1 = (f32[3,32,128]{2,1,0:T(8,128)}, bf16[768,384]{1,0:T(8,128)(2,1)}, bf16[768,384]{1,0:T(8,128)(2,1)}, f32[384,1536]{1,0:T(8,128)}, f32[384,1536]{1,0:T(8,128)}, /*index=5*/f32[1536,384]{1,0:T(8,128)}) custom-call(bf16[3,128,4096]{2,1,0:T(8,128)(2,1)} %get-tuple-element.28.q_ref, bf16[3,32,128]{2,1,0:T(8,128)(2,1)} %bitcast.111, ...), custom_call_target="tpu_custom_call" | custom-call | flops 12079595520 | bytes 20000000 | tf_op jit(solution)/shard_map/attention_bwd/pallas_call | solution.py:807
  216.6 1.3 fusion.12
  217.9 0.1 pad.2.clone
  218.0 0.1 maximum_maximum_fusion.1.small
  218.1 1.6 convolution_bitcast_fusion.3
  219.7 1.6 convolution_bitcast_fusion.2
  221.2 0.3 convolution_bitcast_fusion.1
  221.6 0.3 convolution_bitcast_fusion
  221.8 0.0 copy-start.1
  221.8 0.0 copy-start.2
  221.9 0.2 pad_maximum_fusion.src
  222.0 0.8 copy-done.1
  222.8 0.1 copy-done.2
  222.9 0.2 copy-done.3
  223.1 0.2 copy-done.4
  223.3 48.6 %reduce_late.1 = (f32[4,384,384]{2,1,0:T(8,128)S(1)}, f32[8,384]{1,0:T(8,128)S(1)}, f32[1024,384]{1,0:T(8,128)S(1)}) custom-call(f32[4,384,384]{2,1,0:T(8,128)S(1)} %pad_maximum_fusion.src, f32[8,384]{1,0:T(8,128)S(1)} %maximum_maximum_fusion.1.small, bf16[768,384]{1,0:T(8,128)(2,1)S(1)} %copy-done.3, bf16[768,384]{1,0:T(8,128)(2,1)S(1)} %copy-done.4, ...), custom_call_target="tpu_custom_call" | custom-call | tf_op jit(solution)/shard_map/reduce_late/pallas_call | solution.py:887
  271.9 1.2 fusion.53
  273.1 2.1 copy.51
  275.2 2.1 copy.52
  277.4 1.0 copy.53
  278.4 0.6 slice_reduce_fusion
  279.0 0.7 fusion.14
  279.7 1.1 copy.89
  280.9 1.4 copy.90
  282.3 1.1 copy-done.9
  283.4 1.4 copy.91
  284.8 1.1 copy-done.8
  285.9 1.4 copy.92
  (32 shorter events, 0.1 us)
Async XLA Ops:
  0.6 97.7 %copy-start = (bf16[1536,384]{1,0:T(8,128)(2,1)S(1)}, bf16[1536,384]{1,0:T(8,128)(2,1)}, u32[]{:S(2)}) copy-start(bf16[1536,384]{1,0:T(8,128)(2,1)} %param.25) | copy-start | bytes 3538948
  0.7 91.4 %copy-start.12 = (bf16[32,384]{1,0:T(8,128)(2,1)S(1)}, bf16[32,384]{1,0:T(8,128)(2,1)}, u32[]{:S(2)}) copy-start(bf16[32,384]{1,0:T(8,128)(2,1)} %param.13) | copy-start | bytes 73732
  0.7 91.4 %copy-start.11 = (bf16[6,64,384]{2,1,0:T(8,128)(2,1)S(1)}, bf16[6,64,384]{2,1,0:T(8,128)(2,1)}, u32[]{:S(2)}) copy-start(bf16[6,64,384]{2,1,0:T(8,128)(2,1)} %param.21) | copy-start | bytes 884740
  0.7 92.5 %copy-start.17 = (bf16[384]{0:T(512)(128)(2,1)S(1)}, bf16[384]{0:T(512)(128)(2,1)}, u32[]{:S(2)}) copy-start(bf16[384]{0:T(512)(128)(2,1)} %param.22) | copy-start | bytes 2308
  10.2 86.2 %copy-start.15 = (f32[32,384]{1,0:T(8,128)S(1)}, f32[32,384]{1,0:T(8,128)}, u32[]{:S(2)}) copy-start(f32[32,384]{1,0:T(8,128)} %param.16) | copy-start | bytes 147460
  98.8 3.8 %copy-start.6 = (bf16[384,1536]{1,0:T(8,128)(2,1)S(1)}, bf16[384,1536]{1,0:T(8,128)(2,1)}, u32[]{:S(2)}) copy-start(bf16[384,1536]{1,0:T(8,128)(2,1)} %param.23) | copy-start | bytes 3538948
  100.7 2.4 copy-start.5
  100.7 3.1 %copy-start.13 = (f32[3,32,128]{2,1,0:T(8,128)S(1)}, f32[3,32,128]{2,1,0:T(8,128)}, u32[]{:S(2)}) copy-start(f32[3,32,128]{2,1,0:T(8,128)} %get-tuple-element.27) | copy-start | bytes 147460
  102.6 1.9 copy-start.16
  105.8 112.3 %copy-start.7 = (bf16[768,384]{1,0:T(8,128)(2,1)S(1)}, bf16[768,384]{1,0:T(8,128)(2,1)}, u32[]{:S(2)}) copy-start(bf16[768,384]{1,0:T(8,128)(2,1)} %get-tuple-element.34) | copy-start | bytes 1769476
  216.6 4.6 %copy-start.14 = (f32[3,32,128]{2,1,0:T(8,128)S(1)}, f32[3,32,128]{2,1,0:T(8,128)}, u32[]{:S(2)}) copy-start(f32[3,32,128]{2,1,0:T(8,128)} %get-tuple-element.33) | copy-start | bytes 147460
  221.8 1.0 copy-start.1
  221.8 1.0 copy-start.2
  221.9 1.2 copy-start.3
  221.9 1.4 copy-start.4
  278.4 2.5 copy-start.10
  280.9 2.5 copy-start.9
  283.4 2.5 copy-start.8

commit v5 on v4

--- a/solution.py
+++ b/solution.py
@@ -158,17 +158,18 @@
 GATHER_REFS = 5
 
 
-def run_gathers(gathers, between=None):
+def run_gathers(gathers, hooks):
     for g in gathers:
         g.begin()
+    hooks[0]()
     for g in gathers:
         g.turn()
         g.spread(1)
+    hooks[1]()
     for g in gathers:
         g.settle(1)
         g.spread(2)
-    if between is not None:
-        between()
+    hooks[2]()
     final = []
     for g in gathers:
         g.settle(2)
@@ -588,7 +589,7 @@
 KC = 256
 
 
-def fwd_kernel(n, x_ref, mem_ref, wk_ref, wv_ref, auxk_ref, auxv_ref, o_ref, st_ref, *refs):
+def fwd_kernel(n, x_ref, mem_ref, wk_ref, wv_ref, len_ref, o_ref, st_ref, *refs):
     saved, refs = refs[:SAVED], refs[SAVED:]
     kept, refs = refs[:SAVED], refs[SAVED:]
     q_ref, keep_ref, k_ref, v_ref, kt_ref = kept
@@ -602,16 +603,20 @@
     at.barrier()
     quarter = at.quarter()
 
-    def donate(q):
-        return rcopy(mem_ref.at[pl.ds(keys, piece), :], keep_ref.at[pl.ds(q * piece, piece), :], msend, mrecv.at[q], at.mate(3))
+    size = piece // 2
+
+    def donate(q, i):
+        return rcopy(mem_ref.at[pl.ds(keys + i * size, size), :], keep_ref.at[pl.ds(q * piece + i * size, size), :],
+                     msend.at[i], mrecv.at[q, i], at.mate(3))
+
+    def give(i):
+        for q in range(3):
+            @pl.when(quarter == q)
+            def _(q=q):
+                donate(q, i).start()
 
     def saves():
         return [pltpu.make_async_copy(a, b, save_sem.at[i]) for i, (a, b) in enumerate(zip(kept, saved))]
-
-    for q in range(3):
-        @pl.when(quarter == q)
-        def _(q=q):
-            donate(q).start()
 
     def project():
         @pl.when(quarter < 3)
@@ -621,25 +626,33 @@
         @pl.when(quarter == 3)
         def _():
             for q in range(3):
-                donate(q).wait_recv()
-
-        low = lax.broadcasted_iota(jnp.int32, (piece, TILE), 1) < HALF
+                for i in range(2):
+                    donate(q, i).wait_recv()
+
+        lane = lax.broadcasted_iota(jnp.int32, (piece, TILE), 1)
+        spot = lax.broadcasted_iota(jnp.int32, (piece, TILE), 0)
+        low = lane < HALF
+        lane = lane % HALF
+        flag = jnp.where((lane > 0) & (lane < 4), 1.0, 0.0)
         for i in range(3):
             rows = pl.ds(i * piece, piece)
             m = keep_ref[rows, :]
-            for w_ref, aux_ref, a_ref, t_ref in ((wk_ref, auxk_ref, k_ref, kt_ref), (wv_ref, auxv_ref, v_ref, vt_ref)):
-                aux = aux_ref[rows, :].astype(F32)
+            start = jnp.where(quarter == 3, at.mate(i) * (keys + piece) + keys, at.me * (keys + piece) + i * piece)
+            bias = jnp.where(start + spot < len_ref[0], 0.0, NEG)
+            aux_k = jnp.where(lane == 0, bias, flag)
+            for w_ref, aux, a_ref, t_ref in ((wk_ref, aux_k, k_ref, kt_ref), (wv_ref, flag, v_ref, vt_ref)):
                 for p in range(PARTS):
                     b = jnp.dot(m, w_ref[:, p * TILE:(p + 1) * TILE], preferred_element_type=F32).astype(BF16).astype(F32)
                     a_ref[2 * p, rows, :] = jnp.where(low, b, aux).astype(BF16)
                     a_ref[2 * p + 1, rows, :] = jnp.where(low, aux, b).astype(BF16)
                     t_ref[p, :, rows] = b.T.astype(BF16)
 
-    run_gathers([Gather(n, at, x_ref, q_ref, gbufs)], project)
+    run_gathers([Gather(n, at, x_ref, q_ref, gbufs)], [functools.partial(give, 0), functools.partial(give, 1), project])
     for q in range(3):
         @pl.when(quarter == q)
         def _(q=q):
-            donate(q).wait_send()
+            for i in range(2):
+                donate(q, i).wait_send()
     for c in saves():
         c.start()
     aux = aux_rows([jnp.ones((1, QB), F32)], QB)
@@ -686,22 +699,23 @@
 SAVED = 5
 
 
-def attention_fwd(n, cid, rows, memory, wk, wv, aux_k, aux_v):
+def attention_fwd(n, cid, rows, memory, wk, wv, mem_len):
     total = 2 * n * n * TILE
     r = TILE // n
-    keys, dim = aux_k.shape[0], memory.shape[1]
+    m_rows, dim = memory.shape
+    keys = m_rows * 3 // 4
     vm, hbm = pl.BlockSpec(memory_space=pltpu.VMEM), pl.BlockSpec(memory_space=pl.ANY)
     sem = pltpu.SemaphoreType.DMA
     shapes = ((PARTS, TILE, total), (keys, dim), (2 * PARTS, keys, TILE), (2 * PARTS, keys, TILE), (PARTS, TILE, keys))
     scratch = [pltpu.VMEM(v, BF16) for v in shapes] + [pltpu.VMEM(shapes[-1], BF16), pltpu.VMEM((2, keys, QB), F32),
-                                                       sem(()), sem((3,)), sem((SAVED,))]
+                                                       sem((2,)), sem((3, 2)), sem((SAVED,))]
     return pl.pallas_call(
         functools.partial(fwd_kernel, n),
         out_shape=(jax.ShapeDtypeStruct((PARTS, r, TILE), F32),) * 2 + tuple(jax.ShapeDtypeStruct(v, BF16) for v in shapes),
-        in_specs=[vm] * 6, out_specs=(vm,) * 2 + (hbm,) * SAVED, name="attention_fwd",
+        in_specs=[vm] * 4 + [pl.BlockSpec(memory_space=pltpu.SMEM)], out_specs=(vm,) * 2 + (hbm,) * SAVED, name="attention_fwd",
         scratch_shapes=scratch + Gather.scratch(n, BF16) + Scatter.scratch(n, TILE + 8, 2 * TILE),
         compiler_params=pltpu.CompilerParams(collective_id=cid, has_side_effects=True, vmem_limit_bytes=VMEM_LIMIT),
-    )(rows, memory, wk, wv, aux_k, aux_v)
+    )(rows, memory, wk, wv, mem_len)
 
 
 SCATTER_REFS = 15
@@ -731,24 +745,12 @@
             red.advance(stage)
 
     gathers = [Gather(n, at, s_ref, st_ref, sbufs), Gather(n, at, x_ref, do_ref, xbufs)]
-    for g in gathers:
-        g.begin()
-    advance(0)
-    dk_acc[...] = jnp.zeros_like(dk_acc)
-    dv_acc[...] = jnp.zeros_like(dv_acc)
-    for g in gathers:
-        g.turn()
-        g.spread(1)
-    for g in gathers:
-        g.settle(1)
-        g.spread(2)
-    advance(1)
-    final = []
-    for g in gathers:
-        g.settle(2)
-        final += g.swap()
-    for c in final:
-        c.wait()
+
+    def clear():
+        dk_acc[...] = jnp.zeros_like(dk_acc)
+        dv_acc[...] = jnp.zeros_like(dv_acc)
+
+    run_gathers(gathers, [functools.partial(advance, 0), clear, functools.partial(advance, 1)])
 
     def block(p, src, near, dst):
         probs, dscores, dos, qs, dqs = [], [], [], [], []
@@ -813,6 +815,9 @@
     )(q_t, do_rows, stats_rows, k_aug, v_aug, k_t, *grads)
 
 
+BITS = 8
+
+
 def reduce_kernel(n, form, src, small, dk_ref, dv_ref, wk_ref, wv_ref, out, small_out, dm_ref,
                   slots, pair, ssend, srecv, dm_buf, msend, mrecv, *bufs):
     at = Place(n)
@@ -823,8 +828,18 @@
     quarter = at.quarter()
     nt = (((1,), (1,)), ((), ()))
 
-    def give_back(q):
-        return rcopy(dm_buf.at[pl.ds(q * piece, piece), :], dm_ref.at[pl.ds(keep, piece), :], msend.at[q], mrecv, at.mate(q))
+    bit = piece // BITS
+
+    def give_back(q, i):
+        return rcopy(dm_buf.at[pl.ds(q * piece + i * bit, bit), :], dm_ref.at[pl.ds(keep + i * bit, bit), :],
+                     msend.at[q, i], mrecv.at[i], at.mate(q))
+
+    def give_bits(bits):
+        @pl.when(quarter == 3)
+        def _():
+            for i in bits:
+                for q in range(3):
+                    give_back(q, i).start()
 
     def memory_grad():
         for i in range(3):
@@ -834,8 +849,6 @@
 
         @pl.when(quarter == 3)
         def _():
-            for q in range(3):
-                give_back(q).start()
             dm_ref[...] = jnp.zeros_like(dm_ref)
 
         @pl.when(quarter < 3)
@@ -856,6 +869,8 @@
         red.advance(stage)
         if stage == 1:
             memory_grad()
+        if stage < 7:
+            give_bits([stage - 1] if stage < 5 else [2 * stage - 6, 2 * stage - 5])
         if stage < 5:
             for c in small_copies(stage - 1):
                 c.wait()
@@ -872,12 +887,14 @@
 
     @pl.when(quarter == 3)
     def _():
-        for q in range(3):
-            give_back(q).wait_send()
+        for i in range(BITS):
+            for q in range(3):
+                give_back(q, i).wait_send()
 
     @pl.when(quarter < 3)
     def _():
-        give_back(0).wait_recv()
+        for i in range(BITS):
+            give_back(0, i).wait_recv()
 
 
 def all_reduce_late(n, cid, m_rows, stack, small, dk, dv, wk, wv):
@@ -890,7 +907,7 @@
                    jax.ShapeDtypeStruct((m_rows, wk.shape[0]), F32)),
         in_specs=[pl.BlockSpec(memory_space=pl.ANY)] + [vm] * 5, out_specs=(vm,) * 3, name="reduce_late",
         scratch_shapes=[pltpu.VMEM((3, n) + small.shape, F32), pltpu.VMEM((2,) + small.shape, F32),
-                        sem((4, n - 1)), sem((4, n - 1)), pltpu.VMEM((dk.shape[0], wk.shape[0]), F32), sem((3,)), sem(())]
+                        sem((4, n - 1)), sem((4, n - 1)), pltpu.VMEM((dk.shape[0], wk.shape[0]), F32), sem((3, BITS)), sem((BITS,))]
         + Reduce.scratch(n, form),
         compiler_params=pltpu.CompilerParams(collective_id=cid, has_side_effects=True, vmem_limit_bytes=VMEM_LIMIT // 2),
     )(stack, small, dk, dv, wk, wv)
@@ -918,24 +935,12 @@
         wide = heads * head_dim
         wq, wk, wv = (w.reshape(model_dim, wide) for w in (wq_cross, wk_cross, wv_cross))
         wo = wo_cross.reshape(wide, model_dim)
-        keep, piece, size = m_rows * 3 // 4, m_rows // 4, group // 4
-        me = lax.axis_index('seq')
-        slot = jnp.arange(keep)
-        own_pos = me * m_rows + slot
-        given_pos = ((slot // piece) * size + me % size) * m_rows + keep + slot % piece
-        mem_pos = jnp.where(me // size == 3, given_pos, own_pos)
-        bias = jnp.where(mem_pos < mem_len[0], 0.0, NEG)[:, None]
-        lane = jnp.arange(TILE)[None, :] % head_dim
-        flag = jnp.where((lane >= 1) & (lane <= 3), 1.0, 0.0)
-        aux_k = jnp.where(lane == 0, bias, flag).astype(BF16)
-        aux_v = jnp.broadcast_to(flag, aux_k.shape).astype(BF16)
-
         x_in = dec_in.astype(F32)
         normed_f, norm_pull = jax.vjp(rms_norm, x_in, norm_attn.astype(F32))
         normed = normed_f.astype(BF16)
         local_query = jnp.dot(normed, wq, preferred_element_type=F32).astype(BF16) * jnp.asarray(head_dim ** -0.5, BF16)
         out_parts, lse, q_t, kept, k_aug, v_aug, k_t = attention_fwd(
-            n, 1, by_part(local_query), memory, wk, wv, aux_k, aux_v)
+            n, 1, by_part(local_query), memory, wk, wv, mem_len)
         attended_f = by_row(out_parts)
 
         attended = attended_f.astype(BF16)

time: 288 us -> 274 us (0.951)
  Pallas kernels: 241 us -> 226 us
    pallas_call x1, Pallas kernels: 48.6 us -> 36.4 us  [all_reduce_late(): pl.pallas_call(functools.partial(reduce_kernel, n, form), out_shape=(jax....]
    pallas_call x1, Pallas kernels: 81.8 us -> 78.6 us  [attention_fwd(): pl.pallas_call(functools.partial(fwd_kernel, n), out_shape=(jax.ShapeDtyp...]
where the time goes in v5:
time: 274 us; the launch traced here: 271 us
  Pallas kernels  226 us (82%)
  local copies, waits for them, and re-layouts  21.3 us (8%)
  matrix products  17.9 us (7%)
  other arithmetic  3.7 us (1%)
    pallas_call x1, Pallas kernels, attention_bwd(): pl.pallas_call(functools.partial(bwd_kernel, n, forms), out_shape=tuple(o...  111 us
    pallas_call x1, Pallas kernels, attention_fwd(): pl.pallas_call(functools.partial(fwd_kernel, n), out_shape=(jax.ShapeDtyp...  78.6 us
    pallas_call x1, Pallas kernels, all_reduce_late(): pl.pallas_call(functools.partial(reduce_kernel, n, form), out_shape=(jax....  36.4 us
    unnamed x40, local copies, waits for them, and re-layouts  8.91 us

profile of v5, /device:TPU:1, one launch (start us, length us, event | category | flops | bytes accessed | tf_op | source)
XLA Modules:
  0.0 270.6 jit_solution(15179330961276693960)
XLA Ops:
  0.6 0.0 copy-start
  0.7 0.0 copy-start.12
  0.7 0.0 copy-start.11
  0.7 0.0 copy-start.17
  0.7 1.0 fusion.15
  1.7 0.7 convert_element_type.63
  2.3 1.2 fusion.3
  3.6 0.6 copy.83
  4.2 1.8 copy.42.wk_ref
  6.1 1.8 copy.43.wv_ref
  8.6 78.6 %attention_fwd.1 = (f32[3,32,128]{2,1,0:T(8,128)}, f32[3,32,128]{2,1,0:T(8,128)}, bf16[3,128,4096]{2,1,0:T(8,128)(2,1)}, bf16[768,384]{1,0:T(8,128)(2,1)}, bf16[...) custom-call(bf16[3,32,128]{2,1,0:T(8,128)(2,1)} %bitcast.107, ...), custom_call_target="tpu_custom_call" | custom-call | tf_op jit(solution)/shard_map/attention_fwd/pallas_call | solution.py:712
  87.2 0.0 copy-done.12
  87.2 1.1 multiply_reduce_fusion.2
  88.3 0.1 multiply_convert_fusion.3
  88.4 1.6 fusion.40
  90.0 1.6 fusion.41
  91.6 0.0 copy-done.15
  91.6 0.5 multiply_convert_fusion.1
  92.1 0.0 copy-start.6
  92.1 1.9 fusion.44.refs_1_
  94.0 1.9 fusion.43.refs_0_
  95.9 0.5 fusion.42
  96.3 0.0 copy-done.5
  96.4 0.6 multiply_reduce_fusion
  97.0 0.1 fusion.13
  97.1 0.2 bitcast_multiply_fusion
  97.3 0.1 reshape.101
  97.5 0.2 reduce_sum.65
  97.7 0.1 pad.9.clone
  97.8 0.0 copy-done.16
  97.8 0.7 maximum_maximum_fusion.s_ref
  98.5 0.6 copy.82
  99.1 1.9 fusion.8.refs_2_
  101.0 111.1 %attention_bwd.1 = (f32[3,32,128]{2,1,0:T(8,128)}, bf16[768,384]{1,0:T(8,128)(2,1)}, bf16[768,384]{1,0:T(8,128)(2,1)}, f32[384,1536]{1,0:T(8,128)}, f32[384,1536]{1,0:T(8,128)}, /*index=5*/f32[1536,384]{1,0:T(8,128)}) custom-call(bf16[3,128,4096]{2,1,0:T(8,128)(2,1)} %get-tuple-element.28.q_ref, bf16[3,32,128]{2,1,0:T(8,128)(2,1)} %bitcast.109, ...), custom_call_target="tpu_custom_call" | custom-call | flops 12079595520 | bytes 20000000 | tf_op jit(solution)/shard_map/attention_bwd/pallas_call | solution.py:809
  212.1 1.3 fusion.12
  213.4 0.1 pad.2.clone
  213.5 0.1 maximum_maximum_fusion.1.small
  213.6 0.0 copy-done.7
  213.6 1.6 convolution_bitcast_fusion.3
  215.2 1.6 convolution_bitcast_fusion.2
  216.7 0.3 convolution_bitcast_fusion.1
  217.1 0.3 convolution_bitcast_fusion
  217.3 0.0 copy-start.1
  217.3 0.0 copy-start.2
  217.4 0.0 copy-start.3
  217.4 0.0 copy-start.4
  217.4 0.2 pad_maximum_fusion.src
  217.5 0.8 copy-done.1
  218.3 0.1 copy-done.2
  218.4 0.2 copy-done.3
  218.6 0.2 copy-done.4
  218.8 36.4 %reduce_late.1 = (f32[4,384,384]{2,1,0:T(8,128)S(1)}, f32[8,384]{1,0:T(8,128)S(1)}, f32[1024,384]{1,0:T(8,128)S(1)}) custom-call(f32[4,384,384]{2,1,0:T(8,128)S(1)} %pad_maximum_fusion.src, f32[8,384]{1,0:T(8,128)S(1)} %maximum_maximum_fusion.1.small, bf16[768,384]{1,0:T(8,128)(2,1)S(1)} %copy-done.3, bf16[768,384]{1,0:T(8,128)(2,1)S(1)} %copy-done.4, ...), custom_call_target="tpu_custom_call" | custom-call | tf_op jit(solution)/shard_map/reduce_late/pallas_call | solution.py:904
  255.2 1.2 fusion.37
  256.4 2.1 copy.51
  258.5 2.1 copy.52
  260.7 1.0 copy.53
  261.7 0.6 slice_reduce_fusion
  262.3 0.7 fusion.14
  263.0 1.1 copy.89
  264.2 1.4 copy.90
  265.6 1.1 copy-done.9
  266.7 1.4 copy.91
  268.1 1.1 copy-done.8
  269.2 1.4 copy.92
  (26 shorter events, 0.1 us)
Async XLA Ops:
  0.6 90.9 %copy-start = (bf16[1536,384]{1,0:T(8,128)(2,1)S(1)}, bf16[1536,384]{1,0:T(8,128)(2,1)}, u32[]{:S(2)}) copy-start(bf16[1536,384]{1,0:T(8,128)(2,1)} %param.25) | copy-start | bytes 3538948
  0.7 86.5 %copy-start.12 = (bf16[32,384]{1,0:T(8,128)(2,1)S(1)}, bf16[32,384]{1,0:T(8,128)(2,1)}, u32[]{:S(2)}) copy-start(bf16[32,384]{1,0:T(8,128)(2,1)} %param.13) | copy-start | bytes 73732
  0.7 86.5 %copy-start.11 = (bf16[6,64,384]{2,1,0:T(8,128)(2,1)S(1)}, bf16[6,64,384]{2,1,0:T(8,128)(2,1)}, u32[]{:S(2)}) copy-start(bf16[6,64,384]{2,1,0:T(8,128)(2,1)} %param.21) | copy-start | bytes 884740
  0.7 87.6 %copy-start.17 = (bf16[384]{0:T(512)(128)(2,1)S(1)}, bf16[384]{0:T(512)(128)(2,1)}, u32[]{:S(2)}) copy-start(bf16[384]{0:T(512)(128)(2,1)} %param.22) | copy-start | bytes 2308
  7.9 83.7 %copy-start.15 = (f32[32,384]{1,0:T(8,128)S(1)}, f32[32,384]{1,0:T(8,128)}, u32[]{:S(2)}) copy-start(f32[32,384]{1,0:T(8,128)} %param.16) | copy-start | bytes 147460
  92.1 3.8 %copy-start.6 = (bf16[384,1536]{1,0:T(8,128)(2,1)S(1)}, bf16[384,1536]{1,0:T(8,128)(2,1)}, u32[]{:S(2)}) copy-start(bf16[384,1536]{1,0:T(8,128)(2,1)} %param.23) | copy-start | bytes 3538948
  94.0 2.4 copy-start.5
  94.0 3.1 %copy-start.13 = (f32[3,32,128]{2,1,0:T(8,128)S(1)}, f32[3,32,128]{2,1,0:T(8,128)}, u32[]{:S(2)}) copy-start(f32[3,32,128]{2,1,0:T(8,128)} %get-tuple-element.27) | copy-start | bytes 147460
  95.9 1.9 copy-start.16
  101.0 112.6 %copy-start.7 = (bf16[768,384]{1,0:T(8,128)(2,1)S(1)}, bf16[768,384]{1,0:T(8,128)(2,1)}, u32[]{:S(2)}) copy-start(bf16[768,384]{1,0:T(8,128)(2,1)} %get-tuple-element.34) | copy-start | bytes 1769476
  212.1 4.6 %copy-start.14 = (f32[3,32,128]{2,1,0:T(8,128)S(1)}, f32[3,32,128]{2,1,0:T(8,128)}, u32[]{:S(2)}) copy-start(f32[3,32,128]{2,1,0:T(8,128)} %get-tuple-element.33) | copy-start | bytes 147460
  217.3 1.0 copy-start.1
  217.3 1.0 copy-start.2
  217.4 1.2 copy-start.3
  217.4 1.4 copy-start.4
  261.7 2.5 copy-start.10
  264.2 2.5 copy-start.9
  266.7 2.5 copy-start.8
